TPU v7x, 16 devices: a 4x2x1 block of a 4x4x8 slice. The times are simulated.
16 devices in a mesh: dp: 2 (over y, z), tp: 8 (over x, core).
Axes of the slice: x: 4, y: 2, z: 1, core: 2. Of those that a mesh axis runs over, the one named last changes fastest.
The devices are a block of a 4x4x8 slice.
Arguments:
- hidden: bfloat16 [4, 2048, 2048], P('dp'), parts along dimension 0
- lengths: int32 [4], P('dp'), parts along dimension 0
- w_query: bfloat16 [2, 2048, 8, 256], P(None, None, 'tp')
- w_key: bfloat16 [2, 2048, 8, 256], P(None, None, 'tp')
- w_value: bfloat16 [2, 2048, 8, 256], P(None, None, 'tp')
- w_out: bfloat16 [2, 8, 256, 2048], P(None, 'tp')
- w_gate: bfloat16 [2, 2048, 8192], P(None, None, 'tp')
- w_up: bfloat16 [2, 2048, 8192], P(None, None, 'tp')
- w_down: bfloat16 [2, 8192, 2048], P(None, 'tp')
- norm_attn: float32 [2, 2048], replicated
- norm_mlp: float32 [2, 2048], replicated
Outputs:
- output 1: bfloat16 [4, 2048, 2048], P('dp'), parts along dimension 0
- output 2: bfloat16 [2, 4, 8, 2048, 256], P(None, 'dp', 'tp'), parts along dimension 1
- output 3: bfloat16 [2, 4, 8, 2048, 256], P(None, 'dp', 'tp'), parts along dimension 1
There are 2 independent parts. A program takes and returns all parts, laid end to end along the dimension named above; an argument that names none is the same for every part.
All inputs are finite; a program needn't handle non-finite values.
Results may differ from a plain program's by a relative error of at most 0.018677.
Values are sent between devices in bfloat16 or wider.
A program may use at most 768 MiB of HBM per device.

v0:
```python
import jax
import jax.numpy as jnp
from jax import lax
from jax.sharding import PartitionSpec as P

RMS_EPS = 1e-6
ROPE_BASE = 10000.0


def rms_norm(x_in, norm_gain):
    x_f32 = x_in.astype(jnp.float32)
    mean_sq = jnp.mean(x_f32 * x_f32, axis=-1, keepdims=True)
    return (x_f32 * lax.rsqrt(mean_sq + RMS_EPS) * (1.0 + norm_gain)).astype(jnp.bfloat16)


def rope_tables(seq_len, head_dim):
    half_dim = head_dim // 2
    inv_freq = ROPE_BASE ** (-jnp.arange(half_dim, dtype=jnp.float32) * (2.0 / head_dim))
    angles = jnp.arange(seq_len, dtype=jnp.float32)[:, None] * inv_freq[None, :]
    return jnp.cos(angles)[:, None, :], jnp.sin(angles)[:, None, :]


def apply_rope(x_in, cos_t, sin_t):
    half_dim = x_in.shape[-1] // 2
    x_low = x_in[..., :half_dim]
    x_high = x_in[..., half_dim:]
    return jnp.concatenate([x_low * cos_t - x_high * sin_t, x_high * cos_t + x_low * sin_t], axis=-1)


def attention(normed, lengths, w_query, w_key, w_value, cos_t, sin_t):
    head_dim = w_query.shape[-1]
    seq_len = normed.shape[1]
    query = jnp.einsum("duo,ojf->dujf", normed, w_query, preferred_element_type=jnp.float32)
    keys = jnp.einsum("duo,ojf->dujf", normed, w_key, preferred_element_type=jnp.float32)
    values = jnp.einsum("duo,ojf->dujf", normed, w_value, preferred_element_type=jnp.float32).astype(jnp.bfloat16)
    query_rot = (apply_rope(query, cos_t, sin_t) * (head_dim ** -0.5)).astype(jnp.bfloat16)
    key_rot = apply_rope(keys, cos_t, sin_t).astype(jnp.bfloat16)
    scores = jnp.einsum("bqhd,bkhd->bhqk", query_rot, key_rot, preferred_element_type=jnp.float32)
    positions = jnp.arange(seq_len)
    allowed = (positions[None, None, :] <= positions[None, :, None]) & (positions[None, None, :] < lengths[:, None, None])
    scores = jnp.where(allowed[:, None, :, :], scores, -1e30)
    attn_probs = jax.nn.softmax(scores, axis=-1).astype(jnp.bfloat16)
    attn_out = jnp.einsum("bhqk,bkhd->bqhd", attn_probs, values, preferred_element_type=jnp.float32).astype(jnp.bfloat16)
    return attn_out, key_rot, values


def mlp_partial(normed, w_gate, w_up, w_down):
    gate_pre = jnp.einsum("bsm,mf->bsf", normed, w_gate, preferred_element_type=jnp.float32)
    up_proj = jnp.einsum("bsm,mf->bsf", normed, w_up, preferred_element_type=jnp.float32)
    hidden_act = (jax.nn.gelu(gate_pre, approximate=True) * up_proj).astype(jnp.bfloat16)
    return jnp.einsum("bsf,fm->bsm", hidden_act, w_down, preferred_element_type=jnp.float32)


def solution(mesh):
    head_cols = P(None, None, "tp", None)
    head_rows = P(None, "tp", None, None)
    ff_cols = P(None, None, "tp")
    ff_rows = P(None, "tp", None)

    def shard_body(hidden, lengths, w_query, w_key, w_value, w_out, w_gate, w_up, w_down, norm_attn, norm_mlp):
        cos_t, sin_t = rope_tables(hidden.shape[1], w_query.shape[-1])
        hidden_state = hidden
        key_list = []
        value_list = []
        for layer_idx in range(w_query.shape[0]):
            normed = rms_norm(hidden_state, norm_attn[layer_idx])
            attn_out, key_rot, values = attention(normed, lengths, w_query[layer_idx], w_key[layer_idx], w_value[layer_idx], cos_t, sin_t)
            part_sum = jnp.einsum("bqhd,hdm->bqm", attn_out, w_out[layer_idx], preferred_element_type=jnp.float32).astype(jnp.bfloat16)
            summed = lax.psum(part_sum, "tp")
            hidden_state = (hidden_state.astype(jnp.float32) + summed.astype(jnp.float32)).astype(jnp.bfloat16)
            normed = rms_norm(hidden_state, norm_mlp[layer_idx])
            part_sum = mlp_partial(normed, w_gate[layer_idx], w_up[layer_idx], w_down[layer_idx]).astype(jnp.bfloat16)
            summed = lax.psum(part_sum, "tp")
            hidden_state = (hidden_state.astype(jnp.float32) + summed.astype(jnp.float32)).astype(jnp.bfloat16)
            key_list.append(jnp.swapaxes(key_rot, 1, 2))
            value_list.append(jnp.swapaxes(values, 1, 2))
        return hidden_state, jnp.stack(key_list), jnp.stack(value_list)

    return jax.shard_map(
        shard_body,
        mesh=mesh,
        in_specs=(P("dp"), P("dp"), head_cols, head_cols, head_cols, head_rows, ff_cols, ff_cols, ff_rows, P(), P()),
        out_specs=(P("dp"), P(None, "dp", "tp"), P(None, "dp", "tp")),
        check_vma=False,
    )
```

profile of v0, /device:TPU:112, one launch (start us, length us, event | category | flops | bytes accessed | tf_op | source)
XLA Modules:
  0.0 1120.7 jit_solution(18254704173229081960)
XLA Ops:
  7.2 0.1 all-reduce.5.cloned.1.call-start
  7.3 4.1 iota_compare_fusion
  11.4 1.4 slice_add_fusion.1
  12.8 7.2 fusion.2
  20.0 8.8 fusion.100
  28.8 8.8 fusion.103
  37.6 3.7 fusion.143
  41.3 0.1 iota_compare_fusion.1
  41.4 20.8 %fusion.114 = bf16[2,2048,256]{2,1,0:T(8,128)(2,1)} fusion(bf16[2,2048,2048]{2,1,0:T(8,128)(2,1)} %param.11, f32[2048]{0:T(1024)S(1)} %bitcast.155, f32[2,2048]{1,0:T(2,128)S(1)} %add_rsqrt_fusion.3, bf16[2,2048,1,256]{3,1,2,0:T(8,128)(2,1)S(1)} %copy-done.23), kind=kOutput, calls=%fused_computation.113 | convolution fusion | flops 4329570304 | bytes 19947520 | tf_op jit(solution)/shard_map/duo,ojf->dujf/dot_general | solution.py:35
  62.2 3.4 subtract_bitcast_fusion.1
  65.6 21.0 %fusion.191 = (f32[2,2048]{1,0:T(2,128)S(1)}, f32[2,2048,2048]{1,2,0:T(8,128)}) fusion(pred[2,2048]{1,0:T(4,128)(4,1)S(1)} %iota_compare_fusion.1, pred[2048,2048]{0,1:T(8,128)(4,1)} %iota_compare_fusion, bf16[2,2048,128]{1,2,0:T(8,128)(2,1)S(1)} %bitcast.136, bf16[2,2048,128]{1,2,0:T(8,128)(2,1)S(1)} %bitcast.138, f32[2,2048,128]{1,2,0:T(8,128)} %get-tuple-element.17, ...), kind=kOutput, calls=%fused_computation.182 | convolution fusion | flops 4335863808 | bytes 44060672 | tf_op jit(solution)/shard_map/sub | solution.py:42
  86.6 20.4 %convolution_convert_fusion.3 = bf16[2,2048,2048]{2,1,0:T(8,128)(2,1)} fusion(bf16[2,2048,256]{2,1,0:T(8,128)(2,1)} %fusion.114, f32[2,2048,2048]{1,2,0:T(8,128)} %get-tuple-element.31, f32[2,2048]{1,0:T(2,128)S(1)} %get-tuple-element.30, bf16[2,1,256,2048]{3,2,1,0:T(8,128)(2,1)} %param.16), kind=kOutput, calls=%fused_computation.74 | convolution fusion | flops 8616148992 | bytes 53493760 | tf_op jit(solution)/shard_map/bqhd,hdm->bqm/dot_general | solution.py:68
  107.0 0.1 all-reduce.5.cloned.1.call-update
  107.1 0.1 all-reduce.7.cloned.1.call-start
  107.1 0.6 copy-done.13
  107.7 0.6 slice_add_fusion
  108.3 176.2 %all-reduce.5.cloned.1.call-done = bf16[2,2048,2048]{2,1,0:T(8,128)(2,1)} async-done(((bf16[2,2048,2048]{2,1,0:T(8,128)(2,1)}), bf16[2,2048,2048]{2,1,0:T(8,128)(2,1)}) %all-reduce.5.cloned.1.call-update) | async-done | bytes 16777232 | tf_op jit(solution)/shard_map/psum | solution.py:69
  284.5 14.7 %fusion.6 = (f32[2,2048]{1,0:T(2,128)S(1)}, bf16[2,2048,2048]{2,1,0:T(8,128)(2,1)S(1)}) fusion(bf16[2,2048,2048]{2,1,0:T(8,128)(2,1)} %all-reduce.5.cloned.1.call-done, bf16[2,2048,2048]{2,1,0:T(8,128)(2,1)} %param.11), kind=kLoop, calls=%fused_computation.20 | loop fusion | flops 58716160 | bytes 50348032 | tf_op jit(solution)/shard_map/reduce_sum | solution.py:12
  299.2 5.7 copy-done.1
  304.9 21.9 %fusion.50 = f32[2,2048,1024]{2,1,0:T(8,128)} fusion(bf16[2,2048,2048]{2,1,0:T(8,128)(2,1)S(1)} %get-tuple-element.11, f32[2048]{0:T(1024)S(1)} %bitcast.151, f32[2,2048]{1,0:T(2,128)S(1)} %add_rsqrt_fusion.2, bf16[2,2048,1024]{2,1,0:T(8,128)(2,1)} %param.18), kind=kOutput, calls=%fused_computation.69 | convolution fusion | flops 17213423616 | bytes 37773312 | tf_op jit(solution)/shard_map/bsm,mf->bsf/dot_general | solution.py:49
  326.9 30.0 %fusion.28.clone.5 = bf16[2,2048,1024]{2,1,0:T(8,128)(2,1)} fusion(f32[2,2048,1024]{2,1,0:T(8,128)} %fusion.50, bf16[2,2048,2048]{2,1,0:T(8,128)(2,1)} %copy-done.1, f32[2048]{0:T(1024)S(1)} %bitcast.152, f32[2,2048]{1,0:T(2,128)S(1)} %add_rsqrt_fusion.2, bf16[2,2048,1024]{2,1,0:T(8,128)(2,1)} %param.17), kind=kOutput, calls=%fused_computation.48.clone.clone.clone.2 | convolution fusion | flops 17255366656 | bytes 46161920 | tf_op jit(solution)/shard_map/bsm,mf->bsf/dot_general | solution.py:48
  356.9 23.6 %convolution_convert_fusion.2 = bf16[2,2048,2048]{2,1,0:T(8,128)(2,1)} fusion(bf16[2,1024,2048]{2,1,0:T(8,128)(2,1)} %param.19, bf16[2,2048,1024]{2,1,0:T(8,128)(2,1)} %fusion.28.clone.5), kind=kOutput, calls=%fused_computation.73 | convolution fusion | flops 17188257792 | bytes 29360128 | tf_op jit(solution)/shard_map/bsf,fm->bsm/dot_general | solution.py:51
  380.6 0.1 all-reduce.9.cloned.1.call-start
  380.6 174.8 %all-reduce.7.cloned.1.call-done = bf16[2,2048,2048]{2,1,0:T(8,128)(2,1)} async-done(((bf16[2,2048,2048]{2,1,0:T(8,128)(2,1)}), bf16[2,2048,2048]{2,1,0:T(8,128)(2,1)}) %all-reduce.7.cloned.1.call-update) | async-done | bytes 16777232 | tf_op jit(solution)/shard_map/psum | solution.py:73
  555.4 20.2 %fusion.10 = (f32[2,2048]{1,0:T(2,128)S(1)}, bf16[2,2048,2048]{2,1,0:T(8,128)(2,1)}) fusion(bf16[2,2048,2048]{2,1,0:T(8,128)(2,1)} %all-reduce.7.cloned.1.call-done, bf16[2,2048,2048]{2,1,0:T(8,128)(2,1)} %copy-done.1), kind=kLoop, calls=%fused_computation.24 | loop fusion | flops 58716160 | bytes 50348032 | tf_op jit(solution)/shard_map/reduce_sum | solution.py:12
  575.6 8.9 fusion.109
  584.6 8.8 fusion.106
  593.4 10.0 fusion.117
  603.3 3.4 subtract_bitcast_fusion
  606.7 21.0 %fusion.196 = (f32[2,2048]{1,0:T(2,128)S(1)}, f32[2,2048,2048]{1,2,0:T(8,128)}) fusion(pred[2,2048]{1,0:T(4,128)(4,1)S(1)} %copy-done.15, pred[2048,2048]{0,1:T(8,128)(4,1)} %iota_compare_fusion, bf16[2,2048,128]{1,2,0:T(8,128)(2,1)S(1)} %bitcast.140, bf16[2,2048,128]{1,2,0:T(8,128)(2,1)S(1)} %bitcast.142, f32[2,2048,128]{1,2,0:T(8,128)} %get-tuple-element.13, ...), kind=kOutput, calls=%fused_computation.183 | convolution fusion | flops 4335863808 | bytes 44060672 | tf_op jit(solution)/shard_map/sub | solution.py:42
  627.7 20.3 %convolution_convert_fusion.1 = bf16[2,2048,2048]{2,1,0:T(8,128)(2,1)} fusion(bf16[2,2048,256]{2,1,0:T(8,128)(2,1)} %fusion.117, f32[2,2048,2048]{1,2,0:T(8,128)} %get-tuple-element.33, f32[2,2048]{1,0:T(2,128)S(1)} %get-tuple-element.32, bf16[2,1,256,2048]{3,2,1,0:T(8,128)(2,1)} %param.16), kind=kOutput, calls=%fused_computation.72 | convolution fusion | flops 8616148992 | bytes 53493760 | tf_op jit(solution)/shard_map/bqhd,hdm->bqm/dot_general | solution.py:68
  648.0 0.1 all-reduce.9.cloned.1.call-update
  648.1 0.1 all-reduce.11.cloned.1.call-start
  648.2 174.7 %all-reduce.9.cloned.1.call-done = bf16[2,2048,2048]{2,1,0:T(8,128)(2,1)} async-done(((bf16[2,2048,2048]{2,1,0:T(8,128)(2,1)}), bf16[2,2048,2048]{2,1,0:T(8,128)(2,1)}) %all-reduce.9.cloned.1.call-update) | async-done | bytes 16777232 | tf_op jit(solution)/shard_map/psum | solution.py:69
  822.9 14.7 %fusion.14 = (f32[2,2048]{1,0:T(2,128)S(1)}, bf16[2,2048,2048]{2,1,0:T(8,128)(2,1)S(1)}) fusion(bf16[2,2048,2048]{2,1,0:T(8,128)(2,1)} %all-reduce.9.cloned.1.call-done, bf16[2,2048,2048]{2,1,0:T(8,128)(2,1)} %get-tuple-element.9), kind=kLoop, calls=%fused_computation.28 | loop fusion | flops 58716160 | bytes 50348032 | tf_op jit(solution)/shard_map/reduce_sum | solution.py:12
  837.6 6.1 copy-done
  843.8 21.9 %fusion.46 = f32[2,2048,1024]{2,1,0:T(8,128)} fusion(bf16[2,2048,2048]{2,1,0:T(8,128)(2,1)S(1)} %get-tuple-element.7, f32[2048]{0:T(1024)S(1)} %bitcast.146, f32[2,2048]{1,0:T(2,128)S(1)} %add_rsqrt_fusion, bf16[2,2048,1024]{2,1,0:T(8,128)(2,1)} %param.18), kind=kOutput, calls=%fused_computation.67 | convolution fusion | flops 17213423616 | bytes 37773312 | tf_op jit(solution)/shard_map/bsm,mf->bsf/dot_general | solution.py:49
  865.7 29.9 %fusion.37.clone.5 = bf16[2,2048,1024]{2,1,0:T(8,128)(2,1)} fusion(f32[2,2048,1024]{2,1,0:T(8,128)} %fusion.46, bf16[2,2048,2048]{2,1,0:T(8,128)(2,1)} %copy-done, f32[2048]{0:T(1024)S(1)} %bitcast.147, f32[2,2048]{1,0:T(2,128)S(1)} %add_rsqrt_fusion, bf16[2,2048,1024]{2,1,0:T(8,128)(2,1)} %param.17), kind=kOutput, calls=%fused_computation.57.clone.clone.clone.2 | convolution fusion | flops 17255366656 | bytes 46161920 | tf_op jit(solution)/shard_map/bsm,mf->bsf/dot_general | solution.py:48
  895.6 23.4 %convolution_convert_fusion = bf16[2,2048,2048]{2,1,0:T(8,128)(2,1)} fusion(bf16[2,1024,2048]{2,1,0:T(8,128)(2,1)} %param.19, bf16[2,2048,1024]{2,1,0:T(8,128)(2,1)} %fusion.37.clone.5), kind=kOutput, calls=%fused_computation.71 | convolution fusion | flops 17188257792 | bytes 29360128 | tf_op jit(solution)/shard_map/bsf,fm->bsm/dot_general | solution.py:51
  919.0 0.1 all-reduce.11.cloned.1.call-update
  919.1 1.2 copy-done.7
  920.2 0.3 copy-done.9
  920.5 0.3 copy-done.11
  920.9 3.2 maximum_maximum_fusion
  924.1 6.2 copy.28
  930.2 4.6 maximum_bitcast_fusion
  934.9 159.1 %all-reduce.11.cloned.1.call-done = bf16[2,2048,2048]{2,1,0:T(8,128)(2,1)} async-done(((bf16[2,2048,2048]{2,1,0:T(8,128)(2,1)}), bf16[2,2048,2048]{2,1,0:T(8,128)(2,1)}) %all-reduce.11.cloned.1.call-update) | async-done | bytes 16777232 | tf_op jit(solution)/shard_map/psum | solution.py:73
  1093.9 19.8 %fusion.17 = bf16[2,2048,2048]{2,1,0:T(8,128)(2,1)} fusion(bf16[2,2048,2048]{2,1,0:T(8,128)(2,1)} %copy-done, bf16[2,2048,2048]{2,1,0:T(8,128)(2,1)} %all-reduce.11.cloned.1.call-done), kind=kLoop, calls=%fused_computation.31 | loop fusion | flops 33554432 | bytes 50331648 | tf_op jit(solution)/shard_map/convert_element_type | solution.py:74
  (50 shorter events, 0.2 us)
Async XLA Ops:
  7.2 12.9 %copy-start.21 = (bf16[2,2048,1,256]{3,1,2,0:T(8,128)(2,1)S(1)}, bf16[2,2048,1,256]{3,1,2,0:T(8,128)(2,1)}, u32[]{:S(2)}) copy-start(bf16[2,2048,1,256]{3,1,2,0:T(8,128)(2,1)} %param.13) | copy-start | bytes 6291460
  7.2 277.3 %all-reduce.5.cloned.1.call-start = ((), (), s32[]{:S(2)}) async-start(), calls=%async_computation | async-start | bytes 33554432 | tf_op jit(solution)/shard_map/psum | solution.py:69
  20.0 8.8 copy-start.19
  28.8 12.5 %copy-start.18 = (s32[2]{0:T(128)S(1)}, s32[2]{0:T(128)}, u32[]{:S(2)}) copy-start(s32[2]{0:T(128)} %param.12) | copy-start | bytes 28
  28.8 12.6 %copy-start.23 = (bf16[2,2048,1,256]{3,1,2,0:T(8,128)(2,1)S(1)}, bf16[2,2048,1,256]{3,1,2,0:T(8,128)(2,1)}, u32[]{:S(2)}) copy-start(bf16[2,2048,1,256]{3,1,2,0:T(8,128)(2,1)} %param.15) | copy-start | bytes 6291460
  41.3 20.9 %copy-start.2 = (f32[2048,128]{0,1:T(8,128)}, f32[2048,128]{0,1:T(8,128)S(1)}, u32[]{:S(2)}) copy-start(f32[2048,128]{0,1:T(8,128)S(1)} %get-tuple-element.28) | copy-start | bytes 3145732
  41.3 20.9 %copy-start.4 = (f32[2048,128]{0,1:T(8,128)}, f32[2048,128]{0,1:T(8,128)S(1)}, u32[]{:S(2)}) copy-start(f32[2048,128]{0,1:T(8,128)S(1)} %get-tuple-element.29) | copy-start | bytes 3145732
  41.4 24.2 %copy-start.14 = (pred[2,2048]{1,0:T(4,128)(4,1)}, pred[2,2048]{1,0:T(4,128)(4,1)S(1)}, u32[]{:S(2)}) copy-start(pred[2,2048]{1,0:T(4,128)(4,1)S(1)} %iota_compare_fusion.1) | copy-start | bytes 12292
  65.6 21.0 %copy-start.6 = (bf16[2,2048,1,128]{1,3,0,2:T(8,128)(2,1)}, bf16[2,2048,1,128]{1,3,0,2:T(8,128)(2,1)S(1)}, u32[]{:S(2)}) copy-start(bf16[2,2048,1,128]{1,3,0,2:T(8,128)(2,1)S(1)} %get-tuple-element.22) | copy-start | bytes 3145732
  65.6 21.0 %copy-start.8 = (bf16[2,2048,1,128]{1,3,0,2:T(8,128)(2,1)}, bf16[2,2048,1,128]{1,3,0,2:T(8,128)(2,1)S(1)}, u32[]{:S(2)}) copy-start(bf16[2,2048,1,128]{1,3,0,2:T(8,128)(2,1)S(1)} %get-tuple-element.23) | copy-start | bytes 3145732
  107.0 0.7 copy-start.13
  107.1 448.3 %all-reduce.7.cloned.1.call-start = ((), (), s32[]{:S(2)}) async-start(), calls=%async_computation.1 | async-start | bytes 33554432 | tf_op jit(solution)/shard_map/psum | solution.py:73
  299.2 5.7 copy-start.1
  380.6 195.0 %copy-start.17 = (f32[1,2048]{1,0:T(1,128)S(1)}, f32[1,2048]{1,0:T(1,128)}, u32[]{:S(2)}) copy-start(f32[1,2048]{1,0:T(1,128)} %get-tuple-element.26) | copy-start | bytes 24580
  380.6 195.0 %copy-start.20 = (bf16[2,2048,1,256]{3,1,2,0:T(8,128)(2,1)S(1)}, bf16[2,2048,1,256]{3,1,2,0:T(8,128)(2,1)}, u32[]{:S(2)}) copy-start(bf16[2,2048,1,256]{3,1,2,0:T(8,128)(2,1)} %param.14) | copy-start | bytes 6291460
  380.6 442.3 %all-reduce.9.cloned.1.call-start = ((), (), s32[]{:S(2)}) async-start(), calls=%async_computation.2 | async-start | bytes 33554432 | tf_op jit(solution)/shard_map/psum | solution.py:69
  575.6 8.9 copy-start.22
  584.6 8.8 copy-start.24
  593.3 10.0 copy-start.3
  593.4 10.0 copy-start.5
  603.3 3.4 copy-start.15
  606.7 21.0 %copy-start.10 = (bf16[2,2048,1,128]{1,3,0,2:T(8,128)(2,1)}, bf16[2,2048,1,128]{1,3,0,2:T(8,128)(2,1)S(1)}, u32[]{:S(2)}) copy-start(bf16[2,2048,1,128]{1,3,0,2:T(8,128)(2,1)S(1)} %get-tuple-element.20) | copy-start | bytes 3145732
  606.7 21.0 %copy-start.12 = (bf16[2,2048,1,128]{1,3,0,2:T(8,128)(2,1)}, bf16[2,2048,1,128]{1,3,0,2:T(8,128)(2,1)S(1)}, u32[]{:S(2)}) copy-start(bf16[2,2048,1,128]{1,3,0,2:T(8,128)(2,1)S(1)} %get-tuple-element.21) | copy-start | bytes 3145732
  648.1 195.7 %copy-start.16 = (f32[1,2048]{1,0:T(1,128)S(1)}, f32[1,2048]{1,0:T(1,128)}, u32[]{:S(2)}) copy-start(f32[1,2048]{1,0:T(1,128)} %get-tuple-element.24) | copy-start | bytes 24580
  648.1 445.8 %all-reduce.11.cloned.1.call-start = ((), (), s32[]{:S(2)}) async-start(), calls=%async_computation.3 | async-start | bytes 33554432 | tf_op jit(solution)/shard_map/psum | solution.py:73
  837.6 6.2 copy-start
  919.0 1.2 copy-start.7
  919.0 1.5 copy-start.9
  919.0 1.9 copy-start.11
Sparse Core Ops, SparseCore 0:
  107.2 177.2 all-reduce.4
  380.7 174.6 all-reduce.6
  648.2 174.6 all-reduce.8
  919.2 174.6 all-reduce.10
where the time goes:
time: 1130 us; the launch traced here: 1120 us
  waiting for transfers between devices  685 us (61%)
  matrix products  299 us (26%)
  other arithmetic  101 us (9%)
  local copies, waits for them, and re-layouts  20.5 us (2%)
  between operations  14.6 us (1%)
    psum x4, waiting for transfers between devices, shard_body(): summed = lax.psum(part_sum, 'tp')  685 us
    dot_general x2, matrix products, mlp_partial(): jnp.einsum('bsm,mf->bsf', normed, w_gate, preferred_element_type=jnp.floa...  59.9 us
    reduce_sum x4, other arithmetic, rms_norm(): mean_sq = jnp.mean(x_f32 * x_f32, axis=-1, keepdims=True)  56.7 us
    dot_general x2, matrix products, mlp_partial(): jnp.einsum('bsf,fm->bsm', hidden_act, w_down, preferred_element_type=jnp....  47 us
    dot_general x2, matrix products, mlp_partial(): jnp.einsum('bsm,mf->bsf', normed, w_up, preferred_element_type=jnp.float32)  43.9 us
    sub x2, matrix products, attention(): attn_probs = jax.nn.softmax(scores, axis=-1).astype(jnp.bfloat16)  41.9 us
    dot_general x2, matrix products, shard_body(): jnp.einsum('bqhd,hdm->bqm', attn_out, w_out[layer_idx], preferred_element...  40.7 us
    dot_general x2, matrix products, attention(): jnp.einsum('duo,ojf->dujf', normed, w_value, preferred_element_type=jnp.f...  30.8 us
  transfers between devices with their start and end apart: 4, of which 4 were waited for; matrix products, arithmetic and copies ran while one was open for 1% of the time, Pallas kernels for 0%

commit v1 on v0

v1 whole, which is shorter than its diff:
```python
import functools

import jax
import jax.numpy as jnp
from jax import lax
from jax.experimental import pallas as pl
from jax.experimental.pallas import tpu as pltpu
from jax.sharding import Mesh
from jax.sharding import PartitionSpec as P

RMS_EPS = 1e-6
ROPE_BASE = 10000.0
CORES = 2
CHUNKS = 4
ROW_TILE = 256
FF_TILE = 512
VMEM = 56 * 1024 * 1024


def cost(flops, nbytes, exps=0):
    return pl.CostEstimate(flops=int(flops), bytes_accessed=int(nbytes), transcendentals=int(exps))


def params(**kw):
    return pltpu.CompilerParams(vmem_limit_bytes=VMEM, **kw)


def norm_rows(x_f32, gain):
    mean_sq = jnp.mean(x_f32 * x_f32, axis=-1, keepdims=True)
    return (x_f32 * lax.rsqrt(mean_sq + RMS_EPS) * (1.0 + gain)).astype(jnp.bfloat16)


def qkv_kernel(x_ref, gain_ref, cos_ref, sin_ref, *refs):
    w_refs, (q_ref, k_ref, v_ref) = refs[:-3], refs[-3:]
    normed = norm_rows(x_ref[...].astype(jnp.float32), gain_ref[...])
    cos_t, sin_t = cos_ref[...], sin_ref[...]
    half = cos_t.shape[-1]
    heads = len(w_refs) // 3

    def rope(y, scale):
        low, high = y[:, :half], y[:, half:]
        return jnp.concatenate([(low * cos_t - high * sin_t) * scale, (high * cos_t + low * sin_t) * scale], axis=-1)

    for j in range(heads):
        query = jnp.dot(normed, w_refs[j][...], preferred_element_type=jnp.float32)
        q_ref[j] = rope(query, (2 * half) ** -0.5).astype(jnp.bfloat16)
        keys = jnp.dot(normed, w_refs[heads + j][...], preferred_element_type=jnp.float32)
        k_ref[j] = rope(keys, 1.0).astype(jnp.bfloat16)
        v_ref[j] = jnp.dot(normed, w_refs[2 * heads + j][...], preferred_element_type=jnp.float32).astype(jnp.bfloat16)


def qkv_call(x, gain, cos_t, sin_t, weights):
    rows, width = x.shape
    head = weights[0].shape[-1]
    heads = len(weights) // 3
    tile = min(ROW_TILE, rows)
    out = jax.ShapeDtypeStruct((heads, rows, head), jnp.bfloat16)
    out_spec = pl.BlockSpec((heads, tile, head), lambda i: (0, i, 0))
    whole = pl.BlockSpec((width, head), lambda i: (0, 0), pipeline_mode=pl.Buffered(1))
    table = pl.BlockSpec((tile, head // 2), lambda i: (i, 0))
    return pl.pallas_call(
        qkv_kernel,
        grid=(rows // tile,),
        out_shape=(out, out, out),
        in_specs=[pl.BlockSpec((tile, width), lambda i: (i, 0)), pl.BlockSpec((1, width), lambda i: (0, 0)), table, table]
        + [whole] * len(weights),
        out_specs=(out_spec, out_spec, out_spec),
        compiler_params=params(),
        cost_estimate=cost(2 * rows * width * head * len(weights), 2 * len(weights) * width * head + 2 * rows * width),
    )(x, gain, cos_t, sin_t, *weights)


def attention_kernel(first, len_ref, q_ref, *refs):
    count = (len(refs) - 1) // 2
    k_refs, v_refs, o_ref = refs[:count], refs[count : 2 * count], refs[-1]
    rows = q_ref.shape[1]
    length = len_ref[0]
    query = q_ref[0]
    dims = (((1,), (1,)), ((), ()))
    row_id = lax.broadcasted_iota(jnp.int32, (rows, rows), 0)
    col_id = lax.broadcasted_iota(jnp.int32, (rows, rows), 1)
    blocks = []
    for j in range(count):
        scores = lax.dot_general(query, k_refs[j][0], dims, preferred_element_type=jnp.float32)
        allowed = col_id < length - j * rows
        if j == count - 1:
            allowed = allowed & (col_id <= row_id)
        blocks.append(jnp.where(allowed, scores, -1e30))
    top = functools.reduce(jnp.maximum, [jnp.max(b, axis=-1, keepdims=True) for b in blocks])
    blocks = [jnp.exp(b - top) for b in blocks]
    inv = 1.0 / functools.reduce(jnp.add, [jnp.sum(b, axis=-1, keepdims=True) for b in blocks])
    total = None
    for j in range(count):
        part = jnp.dot((blocks[j] * inv).astype(jnp.bfloat16), v_refs[j][0], preferred_element_type=jnp.float32)
        total = part if total is None else total + part
    o_ref[...] = total.astype(jnp.bfloat16)


def attention_call(length, query, k_list, v_list):
    heads, rows, head = query.shape
    count = len(k_list)
    spec = pl.BlockSpec((1, rows, head), lambda h: (h, 0, 0))
    return pl.pallas_call(
        functools.partial(attention_kernel, count),
        grid=(heads,),
        out_shape=jax.ShapeDtypeStruct((rows, heads * head), jnp.bfloat16),
        in_specs=[pl.BlockSpec(memory_space=pltpu.SMEM)] + [spec] * (1 + 2 * count),
        out_specs=pl.BlockSpec((rows, head), lambda h: (0, h)),
        compiler_params=params(),
        cost_estimate=cost(4 * heads * rows * rows * count * head * 2, 4 * heads * rows * count * head, heads * rows * rows * count),
    )(length, query, *k_list, *v_list)


def out_kernel(x_ref, o_ref, w_ref, gain_ref, mid_ref, normed_ref):
    total = x_ref[...].astype(jnp.float32)
    acc = None
    for c in range(o_ref.shape[0]):
        part = jnp.dot(o_ref[c], w_ref[c], preferred_element_type=jnp.float32)
        acc = part if acc is None else acc + part
    mid = (total + acc).astype(jnp.bfloat16)
    mid_ref[...] = mid
    normed_ref[...] = norm_rows(mid.astype(jnp.float32), gain_ref[...])


def out_call(x, o_all, w_out, gain):
    rows, width = x.shape
    chips, _, inner = o_all.shape
    tile = min(ROW_TILE, rows)
    row_spec = pl.BlockSpec((tile, width), lambda i: (i, 0))
    out = jax.ShapeDtypeStruct((rows, width), jnp.bfloat16)
    return pl.pallas_call(
        out_kernel,
        grid=(rows // tile,),
        out_shape=(out, out),
        in_specs=[
            row_spec,
            pl.BlockSpec((chips, tile, inner), lambda i: (0, i, 0)),
            pl.BlockSpec((chips, inner, width), lambda i: (0, 0, 0), pipeline_mode=pl.Buffered(1)),
            pl.BlockSpec((1, width), lambda i: (0, 0)),
        ],
        out_specs=(row_spec, row_spec),
        compiler_params=params(),
        cost_estimate=cost(2 * rows * chips * inner * width, 2 * chips * inner * width + 8 * rows * width),
    )(x, o_all, w_out, gain)


def mlp_kernel(a_ref, wg_m, wg_o, wu_m, wu_o, wd_m, wd_o, p_ref, acc_ref):
    step = pl.program_id(0)
    normed = a_ref[...]
    acc = None
    for wg, wu, wd in ((wg_m, wu_m, wd_m), (wg_o, wu_o, wd_o)):
        gate = jnp.dot(normed, wg[...], preferred_element_type=jnp.float32)
        up = jnp.dot(normed, wu[...], preferred_element_type=jnp.float32)
        act = (jax.nn.gelu(gate, approximate=True) * up).astype(jnp.bfloat16)
        part = jnp.dot(act, wd[...], preferred_element_type=jnp.float32)
        acc = part if acc is None else acc + part

    @pl.when(step == 0)
    def _():
        acc_ref[...] = acc

    @pl.when(step > 0)
    def _():
        acc_ref[...] += acc

    @pl.when(step == pl.num_programs(0) - 1)
    def _():
        p_ref[...] = acc_ref[...].astype(jnp.bfloat16)


def mlp_call(normed, gate, up, down, layer):
    rows, width = normed.shape
    ff = gate[0].shape[-1]
    tile = min(FF_TILE, ff)
    col = pl.BlockSpec((None, width, tile), lambda i: (layer, 0, i))
    col_p = pl.BlockSpec((width, tile), lambda i: (0, i))
    row = pl.BlockSpec((None, tile, width), lambda i: (layer, i, 0))
    row_p = pl.BlockSpec((tile, width), lambda i: (i, 0))
    return pl.pallas_call(
        mlp_kernel,
        grid=(ff // tile,),
        out_shape=jax.ShapeDtypeStruct((rows, width), jnp.bfloat16),
        in_specs=[pl.BlockSpec((rows, width), lambda i: (0, 0), pipeline_mode=pl.Buffered(1)), col, col_p, col, col_p, row, row_p],
        out_specs=pl.BlockSpec((rows, width), lambda i: (0, 0), pipeline_mode=pl.Buffered(1)),
        scratch_shapes=[pltpu.VMEM((rows, width), jnp.float32)],
        compiler_params=params(),
        cost_estimate=cost(12 * rows * width * ff, 12 * width * ff + 4 * rows * width, 2 * rows * ff),
    )(normed, gate[0], gate[1], up[0], up[1], down[0], down[1])


def rope_tables(seq_len, head_dim):
    half_dim = head_dim // 2
    inv_freq = ROPE_BASE ** (-jnp.arange(half_dim, dtype=jnp.float32) * (2.0 / head_dim))
    angles = jnp.arange(seq_len, dtype=jnp.float32)[:, None] * inv_freq[None, :]
    return jnp.cos(angles), jnp.sin(angles)


def solution(mesh):
    groups, members = mesh.devices.shape
    chips = members // CORES
    fine = Mesh(mesh.devices.reshape(groups, chips, CORES), ("dp", "x", "core"))
    tp = ("x", "core")
    swap = [(0, 1), (1, 0)]

    def partner(value):
        return lax.ppermute(value, "core", swap)

    def shard_body(hidden, lengths, w_query, w_key, w_value, w_out, w_gate, w_up, w_down, norm_attn, norm_mlp):
        core = lax.axis_index("core")
        chip = lax.axis_index("x")
        layers = w_query.shape[0]
        seq, width = hidden.shape[1:]
        head = w_query.shape[-1]
        rows = seq // CHUNKS
        part = rows // chips
        length = lax.dynamic_slice_in_dim(lengths, core, 1)
        x_full = lax.dynamic_index_in_dim(hidden, core, keepdims=False)
        x = [x_full[i * rows : (i + 1) * rows] for i in range(CHUNKS)]
        cos_t, sin_t = rope_tables(seq, head)
        wo_all = []
        qkv_w = []
        mlp_w = []
        for l in range(layers):
            own = [w[l].reshape(width, head) for w in (w_query, w_key, w_value)]
            other = [partner(w) for w in own]
            qkv_w.append([w for pair in zip(own, other) for w in pair])
        for l in range(layers):
            mlp_w.append([(w, partner(w[l])) for w in (w_gate, w_up, w_down)])
            own_rows = lax.all_gather(w_out[l].reshape(head, width), "x")
            wo_all.append(jnp.concatenate([own_rows, partner(own_rows)], axis=1))
        k_cache = []
        v_cache = []
        for l in range(layers):
            keys, values = [], []
            for i in range(CHUNKS):
                tables = (cos_t[i * rows : (i + 1) * rows], sin_t[i * rows : (i + 1) * rows])
                q, k, v = qkv_call(x[i], norm_attn[l][None, :], *tables, qkv_w[l])
                keys.append(k)
                values.append(v)
                o = attention_call(length, q, keys, values)
                o_all = lax.all_gather(o, "x")
                mid, normed = out_call(x[i], o_all, wo_all[l], norm_mlp[l][None, :])
                partial = mlp_call(normed, *mlp_w[l], l)
                summed = lax.psum_scatter(partial, "x", scatter_dimension=0, tiled=True)
                mine = lax.dynamic_slice_in_dim(mid, chip * part, part, axis=0)
                mine = (mine.astype(jnp.float32) + summed.astype(jnp.float32)).astype(jnp.bfloat16)
                if l < layers - 1:
                    x[i] = lax.all_gather(mine, "x", axis=0, tiled=True)
                else:
                    both = lax.all_gather(mine, tp).reshape(chips, CORES, part, width)
                    x[i] = jnp.swapaxes(both, 0, 1).reshape(CORES, rows, width)
            for cache, pieces in ((k_cache, keys), (v_cache, values)):
                own = jnp.concatenate([p[0] for p in pieces], axis=0)
                got = partner(jnp.concatenate([p[1] for p in pieces], axis=0))
                pair = jnp.where(core == 0, jnp.stack([own, got]), jnp.stack([got, own]))
                cache.append(pair[:, None])
        return jnp.concatenate(x, axis=1), jnp.stack(k_cache), jnp.stack(v_cache)

    head_cols = P(None, None, tp, None)
    return jax.shard_map(
        shard_body,
        mesh=fine,
        in_specs=(P("dp"), P("dp"), head_cols, head_cols, head_cols, P(None, tp, None, None), P(None, None, tp), P(None, None, tp), P(None, tp, None), P(), P()),
        out_specs=(P("dp"), P(None, "dp", tp), P(None, "dp", tp)),
        check_vma=False,
    )
```

time: 1130 us -> 822 us (0.73)
  waiting for transfers between devices: 685 us -> 295 us
  Pallas kernels: 0 us -> 384 us
  matrix products: 299 us -> 0 us
  other arithmetic: 101 us -> 54.2 us
  local copies, waits for them, and re-layouts: 20.5 us -> 62.3 us
    psum x4 -> x0, waiting for transfers between devices: 685 us -> none  [shard_body(): summed = lax.psum(part_sum, 'tp')]
    pallas_call x0 -> x32, Pallas kernels: none -> 384 us  [the longest x8 179 us: mlp_call(): pl.pallas_call(mlp_kernel, grid=(ff // tile,), out_shape=jax.ShapeDtypeSt...]
    dot_general x14 -> x0, matrix products: 257 us -> none  [the longest x2 59.9 us: mlp_partial(): jnp.einsum('bsm,mf->bsf', normed, w_gate, preferred_element_type=jnp.floa...]
    all_gather x0 -> x18, waiting for transfers between devices: none -> 190 us  [the longest x4 84.3 us: shard_body(): both = lax.all_gather(mine, tp).reshape(chips, CORES, part, width)]
    reduce_scatter x0 -> x8, waiting for transfers between devices: none -> 94.1 us  [shard_body(): summed = lax.psum_scatter(partial, 'x', scatter_dimension=0, tiled=True)]
    reduce_sum x4 -> x0, other arithmetic: 56.7 us -> none  [rms_norm(): mean_sq = jnp.mean(x_f32 * x_f32, axis=-1, keepdims=True)]
    sub x2 -> x0, matrix products: 41.9 us -> none  [attention(): attn_probs = jax.nn.softmax(scores, axis=-1).astype(jnp.bfloat16)]
    concatenate x2 -> x7, other arithmetic: 6.74 us -> 26.7 us  [the longest x2 17.1 us: shard_body(): wo_all.append(jnp.concatenate([own_rows, partner(own_rows)], axis=1))]
  transfers between devices with their start and end apart: 4 -> 44, of which waited for: 4 -> 22; matrix products, arithmetic and copies ran while one was open for 1% -> 11% of each run, Pallas kernels for 0% -> 47%
where the time goes in v1:
time: 822 us; the launch traced here: 816 us
  Pallas kernels  384 us (47%)
  waiting for transfers between devices  295 us (36%)
  local copies, waits for them, and re-layouts  62.3 us (8%)
  other arithmetic  54.2 us (7%)
  between operations  14.9 us (2%)
    pallas_call x8, Pallas kernels, mlp_call(): pl.pallas_call(mlp_kernel, grid=(ff // tile,), out_shape=jax.ShapeDtypeSt...  179 us
    reduce_scatter x8, waiting for transfers between devices, shard_body(): summed = lax.psum_scatter(partial, 'x', scatter_dimension=0, tiled=True)  94.1 us
    pallas_call x8, Pallas kernels, out_call(): pl.pallas_call(out_kernel, grid=(rows // tile,), out_shape=(out, out), in...  85.7 us
    all_gather x4, waiting for transfers between devices, shard_body(): both = lax.all_gather(mine, tp).reshape(chips, CORES, part, width)  84.3 us
    all_gather x4, waiting for transfers between devices, shard_body(): x[i] = lax.all_gather(mine, 'x', axis=0, tiled=True)  77.9 us
    pallas_call x8, Pallas kernels, qkv_call(): pl.pallas_call(qkv_kernel, grid=(rows // tile,), out_shape=(out, out, out...  66.8 us
    pallas_call x8, Pallas kernels, attention_call(): pl.pallas_call(functools.partial(attention_kernel, count), grid=(heads,),...  52.2 us
    squeeze x3, local copies, waits for them, and re-layouts, shard_body(): mlp_w.append([(w, partner(w[l])) for w in (w_gate, w_up, w_down)])  18.7 us
  transfers between devices with their start and end apart: 44, of which 22 were waited for; matrix products, arithmetic and copies ran while one was open for 11% of the time, Pallas kernels for 47%

profile of v1, /device:TPU:112, one launch (start us, length us, event | category | flops | bytes accessed | tf_op | source)
XLA Modules:
  0.0 815.7 jit_solution(8355346977194775732)
XLA Ops:
  21.3 7.5 dynamic-slice_bitcast_fusion.1
  29.4 8.6 %shard_map.154 = (bf16[2,512,256]{2,1,0:T(8,128)(2,1)}, bf16[2,512,256]{2,1,0:T(8,128)(2,1)}, bf16[2,512,256]{2,1,0:T(8,128)(2,1)}) custom-call(bf16[512,2048]{1,0:T(8,128)(2,1)} %get-tuple-element.86.x_ref, f32[1,2048]{1,0:T(1,128)} %get-tuple-element.144.gain_ref, f32[512,128]{1,0:T(8,128)} %get-tuple-element.149.cos_ref, ...), custom_call_target="tpu_custom_call" | custom-call | flops 3221225472 | bytes 8388608 | tf_op jit(solution)/shard_map/pallas_call | solution.py:61
  38.0 8.3 %shard_map.130 = (bf16[2,512,256]{2,1,0:T(8,128)(2,1)}, bf16[2,512,256]{2,1,0:T(8,128)(2,1)}, bf16[2,512,256]{2,1,0:T(8,128)(2,1)}) custom-call(bf16[512,2048]{1,0:T(8,128)(2,1)} %get-tuple-element.85.x_ref, f32[1,2048]{1,0:T(1,128)} %get-tuple-element.144.gain_ref, f32[512,128]{1,0:T(8,128)} %get-tuple-element.147.cos_ref, ...), custom_call_target="tpu_custom_call" | custom-call | flops 3221225472 | bytes 8388608 | tf_op jit(solution)/shard_map/pallas_call | solution.py:61
  46.3 8.3 %shard_map.138 = (bf16[2,512,256]{2,1,0:T(8,128)(2,1)}, bf16[2,512,256]{2,1,0:T(8,128)(2,1)}, bf16[2,512,256]{2,1,0:T(8,128)(2,1)}) custom-call(bf16[512,2048]{1,0:T(8,128)(2,1)} %get-tuple-element.84.x_ref, f32[1,2048]{1,0:T(1,128)} %get-tuple-element.144.gain_ref, f32[512,128]{1,0:T(8,128)} %get-tuple-element.148.cos_ref, ...), custom_call_target="tpu_custom_call" | custom-call | flops 3221225472 | bytes 8388608 | tf_op jit(solution)/shard_map/pallas_call | solution.py:61
  54.5 8.4 %shard_map.146 = (bf16[2,512,256]{2,1,0:T(8,128)(2,1)}, bf16[2,512,256]{2,1,0:T(8,128)(2,1)}, bf16[2,512,256]{2,1,0:T(8,128)(2,1)}) custom-call(bf16[512,2048]{1,0:T(8,128)(2,1)} %get-tuple-element.83.x_ref, f32[1,2048]{1,0:T(1,128)} %get-tuple-element.144.gain_ref, f32[512,128]{1,0:T(8,128)} %get-tuple-element.150.cos_ref, ...), custom_call_target="tpu_custom_call" | custom-call | flops 3221225472 | bytes 8388608 | tf_op jit(solution)/shard_map/pallas_call | solution.py:61
  62.9 8.8 %shard_map.155 = bf16[512,512]{1,0:T(8,128)(2,1)} custom-call(s32[1]{0:T(128)} %dynamic_slice.32.len_ref, bf16[2,512,256]{2,1,0:T(8,128)(2,1)} %get-tuple-element.73.q_ref, bf16[2,512,256]{2,1,0:T(8,128)(2,1)} %get-tuple-element.44.refs_0_, bf16[2,512,256]{2,1,0:T(8,128)(2,1)} %get-tuple-element.54.refs_1_, bf16[2,512,256]{2,1,0:T(8,128)(2,1)} %get-tuple-element.64.refs_2_, ...), custom_call_target="tpu_custom_call" | custom-call | flops 4294967296 | bytes 4194304 | tf_op jit(solution)/shard_map/pallas_call | solution.py:103
  76.3 6.6 slice_bitcast_fusion.2
  95.5 6.1 slice_bitcast_fusion
  101.9 7.2 shard_map.147
  109.9 8.5 %pad_maximum_fusion.1.w_ref = bf16[4,512,2048]{2,1,0:T(8,128)(2,1)} fusion(bf16[4,256,2048]{2,1,0:T(8,128)(2,1)} %collective-permute-done.3, bf16[4,256,2048]{2,1,0:T(8,128)(2,1)} %bitcast.143), kind=kLoop, calls=%fused_computation.1 | loop fusion | flops 16777216 | bytes 16777216 | tf_op jit(solution)/shard_map/concatenate | solution.py:230
  118.4 10.6 %shard_map.156 = (bf16[512,2048]{1,0:T(8,128)(2,1)}, bf16[512,2048]{1,0:T(8,128)(2,1)}) custom-call(bf16[512,2048]{1,0:T(8,128)(2,1)} %get-tuple-element.86.x_ref, bf16[4,512,512]{2,1,0:T(8,128)(2,1)} %bitcast.156, bf16[4,512,2048]{2,1,0:T(8,128)(2,1)} %pad_maximum_fusion.1.w_ref, f32[1,2048]{1,0:T(1,128)} %get-tuple-element.142.gain_ref), custom_call_target="tpu_custom_call" | custom-call | flops 4294967296 | bytes 16777216 | tf_op jit(solution)/shard_map/pallas_call | solution.py:131
  129.0 22.1 %shard_map.157 = bf16[512,2048]{1,0:T(8,128)(2,1)} custom-call(bf16[512,2048]{1,0:T(8,128)(2,1)} %get-tuple-element.77.a_ref, bf16[2,2048,1024]{2,1,0:T(8,128)(2,1)} %wg_m.15, bf16[2048,1024]{1,0:T(8,128)(2,1)} %collective-permute-done.4.wg_o, bf16[2,2048,1024]{2,1,0:T(8,128)(2,1)} %wu_m.15, bf16[2048,1024]{1,0:T(8,128)(2,1)} %collective-permute-done.5.wu_o, ...), custom_call_target="tpu_custom_call" | custom-call | flops 12884901888 | bytes 29360128 | tf_op jit(solution)/shard_map/pallas_call | solution.py:179
  151.3 10.7 %shard_map.132 = (bf16[512,2048]{1,0:T(8,128)(2,1)}, bf16[512,2048]{1,0:T(8,128)(2,1)}) custom-call(bf16[512,2048]{1,0:T(8,128)(2,1)} %get-tuple-element.85.x_ref, bf16[4,512,512]{2,1,0:T(8,128)(2,1)} %bitcast.152, bf16[4,512,2048]{2,1,0:T(8,128)(2,1)} %pad_maximum_fusion.1.w_ref, f32[1,2048]{1,0:T(1,128)} %get-tuple-element.142.gain_ref), custom_call_target="tpu_custom_call" | custom-call | flops 4294967296 | bytes 16777216 | tf_op jit(solution)/shard_map/pallas_call | solution.py:131
  161.9 22.1 %shard_map.133 = bf16[512,2048]{1,0:T(8,128)(2,1)} custom-call(bf16[512,2048]{1,0:T(8,128)(2,1)} %get-tuple-element.47.a_ref, bf16[2,2048,1024]{2,1,0:T(8,128)(2,1)} %wg_m.15, bf16[2048,1024]{1,0:T(8,128)(2,1)} %collective-permute-done.4.wg_o, bf16[2,2048,1024]{2,1,0:T(8,128)(2,1)} %wu_m.15, bf16[2048,1024]{1,0:T(8,128)(2,1)} %collective-permute-done.5.wu_o, ...), custom_call_target="tpu_custom_call" | custom-call | flops 12884901888 | bytes 29360128 | tf_op jit(solution)/shard_map/pallas_call | solution.py:179
  184.1 10.7 %shard_map.140 = (bf16[512,2048]{1,0:T(8,128)(2,1)}, bf16[512,2048]{1,0:T(8,128)(2,1)}) custom-call(bf16[512,2048]{1,0:T(8,128)(2,1)} %get-tuple-element.84.x_ref, bf16[4,512,512]{2,1,0:T(8,128)(2,1)} %bitcast.150, bf16[4,512,2048]{2,1,0:T(8,128)(2,1)} %pad_maximum_fusion.1.w_ref, f32[1,2048]{1,0:T(1,128)} %get-tuple-element.142.gain_ref), custom_call_target="tpu_custom_call" | custom-call | flops 4294967296 | bytes 16777216 | tf_op jit(solution)/shard_map/pallas_call | solution.py:131
  194.9 22.0 %shard_map.141 = bf16[512,2048]{1,0:T(8,128)(2,1)} custom-call(bf16[512,2048]{1,0:T(8,128)(2,1)} %get-tuple-element.57.a_ref, bf16[2,2048,1024]{2,1,0:T(8,128)(2,1)} %wg_m.15, bf16[2048,1024]{1,0:T(8,128)(2,1)} %collective-permute-done.4.wg_o, bf16[2,2048,1024]{2,1,0:T(8,128)(2,1)} %wu_m.15, bf16[2048,1024]{1,0:T(8,128)(2,1)} %collective-permute-done.5.wu_o, ...), custom_call_target="tpu_custom_call" | custom-call | flops 12884901888 | bytes 29360128 | tf_op jit(solution)/shard_map/pallas_call | solution.py:179
  217.1 10.9 %shard_map.148 = (bf16[512,2048]{1,0:T(8,128)(2,1)}, bf16[512,2048]{1,0:T(8,128)(2,1)}) custom-call(bf16[512,2048]{1,0:T(8,128)(2,1)} %get-tuple-element.83.x_ref, bf16[4,512,512]{2,1,0:T(8,128)(2,1)} %bitcast.154, bf16[4,512,2048]{2,1,0:T(8,128)(2,1)} %pad_maximum_fusion.1.w_ref, f32[1,2048]{1,0:T(1,128)} %get-tuple-element.142.gain_ref), custom_call_target="tpu_custom_call" | custom-call | flops 4294967296 | bytes 16777216 | tf_op jit(solution)/shard_map/pallas_call | solution.py:131
  228.0 22.0 %shard_map.149 = bf16[512,2048]{1,0:T(8,128)(2,1)} custom-call(bf16[512,2048]{1,0:T(8,128)(2,1)} %get-tuple-element.67.a_ref, bf16[2,2048,1024]{2,1,0:T(8,128)(2,1)} %wg_m.15, bf16[2048,1024]{1,0:T(8,128)(2,1)} %collective-permute-done.4.wg_o, bf16[2,2048,1024]{2,1,0:T(8,128)(2,1)} %wu_m.15, bf16[2048,1024]{1,0:T(8,128)(2,1)} %collective-permute-done.5.wu_o, ...), custom_call_target="tpu_custom_call" | custom-call | flops 12884901888 | bytes 29360128 | tf_op jit(solution)/shard_map/pallas_call | solution.py:179
  254.8 13.8 %reduce-scatter.13.cloned.1.call-done = bf16[128,2048]{1,0:T(8,128)(2,1)} async-done(((bf16[512,2048]{1,0:T(8,128)(2,1)}), bf16[128,2048]{1,0:T(8,128)(2,1)}) %reduce-scatter.13.cloned.1.call-update) | async-done | bytes 524304 | tf_op jit(solution)/shard_map/reduce_scatter | solution.py:244
  270.9 26.0 %reduce-scatter.17.cloned.1.call-done = bf16[128,2048]{1,0:T(8,128)(2,1)} async-done(((bf16[512,2048]{1,0:T(8,128)(2,1)}), bf16[128,2048]{1,0:T(8,128)(2,1)}) %reduce-scatter.17.cloned.1.call-update) | async-done | bytes 524304 | tf_op jit(solution)/shard_map/reduce_scatter | solution.py:244
  305.5 19.0 %all-gather.39.cloned.1.call-done.x_ref = bf16[512,2048]{1,0:T(8,128)(2,1)} async-done(((bf16[128,2048]{1,0:T(8,128)(2,1)}), bf16[512,2048]{1,0:T(8,128)(2,1)}) %all-gather.39.cloned.1.call-update) | async-done | bytes 2097168 | tf_op jit(solution)/shard_map/all_gather | solution.py:248
  324.4 8.5 %shard_map.158 = (bf16[2,512,256]{2,1,0:T(8,128)(2,1)}, bf16[2,512,256]{2,1,0:T(8,128)(2,1)}, bf16[2,512,256]{2,1,0:T(8,128)(2,1)}) custom-call(bf16[512,2048]{1,0:T(8,128)(2,1)} %all-gather.39.cloned.1.call-done.x_ref, f32[1,2048]{1,0:T(1,128)} %get-tuple-element.143.gain_ref, f32[512,128]{1,0:T(8,128)} %get-tuple-element.149.cos_ref, ...), custom_call_target="tpu_custom_call" | custom-call | flops 3221225472 | bytes 8388608 | tf_op jit(solution)/shard_map/pallas_call | solution.py:61
  332.9 19.6 %all-gather.33.cloned.1.call-done.x_ref = bf16[512,2048]{1,0:T(8,128)(2,1)} async-done(((bf16[128,2048]{1,0:T(8,128)(2,1)}), bf16[512,2048]{1,0:T(8,128)(2,1)}) %all-gather.33.cloned.1.call-update) | async-done | bytes 2097168 | tf_op jit(solution)/shard_map/all_gather | solution.py:248
  352.5 8.3 %shard_map.134 = (bf16[2,512,256]{2,1,0:T(8,128)(2,1)}, bf16[2,512,256]{2,1,0:T(8,128)(2,1)}, bf16[2,512,256]{2,1,0:T(8,128)(2,1)}) custom-call(bf16[512,2048]{1,0:T(8,128)(2,1)} %all-gather.33.cloned.1.call-done.x_ref, f32[1,2048]{1,0:T(1,128)} %get-tuple-element.143.gain_ref, f32[512,128]{1,0:T(8,128)} %get-tuple-element.147.cos_ref, ...), custom_call_target="tpu_custom_call" | custom-call | flops 3221225472 | bytes 8388608 | tf_op jit(solution)/shard_map/pallas_call | solution.py:61
  360.8 19.6 %all-gather.35.cloned.1.call-done.x_ref = bf16[512,2048]{1,0:T(8,128)(2,1)} async-done(((bf16[128,2048]{1,0:T(8,128)(2,1)}), bf16[512,2048]{1,0:T(8,128)(2,1)}) %all-gather.35.cloned.1.call-update) | async-done | bytes 2097168 | tf_op jit(solution)/shard_map/all_gather | solution.py:248
  380.4 8.3 %shard_map.142 = (bf16[2,512,256]{2,1,0:T(8,128)(2,1)}, bf16[2,512,256]{2,1,0:T(8,128)(2,1)}, bf16[2,512,256]{2,1,0:T(8,128)(2,1)}) custom-call(bf16[512,2048]{1,0:T(8,128)(2,1)} %all-gather.35.cloned.1.call-done.x_ref, f32[1,2048]{1,0:T(1,128)} %get-tuple-element.143.gain_ref, f32[512,128]{1,0:T(8,128)} %get-tuple-element.148.cos_ref, ...), custom_call_target="tpu_custom_call" | custom-call | flops 3221225472 | bytes 8388608 | tf_op jit(solution)/shard_map/pallas_call | solution.py:61
  388.6 19.7 %all-gather.37.cloned.1.call-done.x_ref = bf16[512,2048]{1,0:T(8,128)(2,1)} async-done(((bf16[128,2048]{1,0:T(8,128)(2,1)}), bf16[512,2048]{1,0:T(8,128)(2,1)}) %all-gather.37.cloned.1.call-update) | async-done | bytes 2097168 | tf_op jit(solution)/shard_map/all_gather | solution.py:248
  408.4 8.2 %shard_map.150 = (bf16[2,512,256]{2,1,0:T(8,128)(2,1)}, bf16[2,512,256]{2,1,0:T(8,128)(2,1)}, bf16[2,512,256]{2,1,0:T(8,128)(2,1)}) custom-call(bf16[512,2048]{1,0:T(8,128)(2,1)} %all-gather.37.cloned.1.call-done.x_ref, f32[1,2048]{1,0:T(1,128)} %get-tuple-element.143.gain_ref, f32[512,128]{1,0:T(8,128)} %get-tuple-element.150.cos_ref, ...), custom_call_target="tpu_custom_call" | custom-call | flops 3221225472 | bytes 8388608 | tf_op jit(solution)/shard_map/pallas_call | solution.py:61
  416.6 8.7 %shard_map.159 = bf16[512,512]{1,0:T(8,128)(2,1)} custom-call(s32[1]{0:T(128)} %dynamic_slice.32.len_ref, bf16[2,512,256]{2,1,0:T(8,128)(2,1)} %get-tuple-element.78.q_ref, bf16[2,512,256]{2,1,0:T(8,128)(2,1)} %get-tuple-element.49.refs_0_, bf16[2,512,256]{2,1,0:T(8,128)(2,1)} %get-tuple-element.59.refs_1_, bf16[2,512,256]{2,1,0:T(8,128)(2,1)} %get-tuple-element.69.refs_2_, ...), custom_call_target="tpu_custom_call" | custom-call | flops 4294967296 | bytes 4194304 | tf_op jit(solution)/shard_map/pallas_call | solution.py:103
  425.5 7.2 shard_map.151
  438.8 14.9 %all-gather.47.cloned.1.call-done = bf16[4,1,256,2048]{3,2,1,0:T(8,128)(2,1)} async-done(((bf16[1,1,256,2048]{3,2,1,0:T(8,128)(2,1)}), bf16[4,1,256,2048]{3,2,1,0:T(8,128)(2,1)}) %all-gather.47.cloned.1.call-update) | async-done | bytes 4194320 | tf_op jit(solution)/shard_map/all_gather | solution.py:229
  460.9 8.5 %pad_maximum_fusion.2.w_ref = bf16[4,512,2048]{2,1,0:T(8,128)(2,1)} fusion(bf16[4,256,2048]{2,1,0:T(8,128)(2,1)} %collective-permute-done.10, bf16[4,256,2048]{2,1,0:T(8,128)(2,1)} %bitcast.145), kind=kLoop, calls=%fused_computation.2 | loop fusion | flops 16777216 | bytes 16777216 | tf_op jit(solution)/shard_map/concatenate | solution.py:230
  469.4 13.2 %all-gather.65.cloned.1.call-done = bf16[2048,512]{1,0:T(8,128)(2,1)} async-done(((bf16[512,512]{1,0:T(8,128)(2,1)}), bf16[2048,512]{1,0:T(8,128)(2,1)}) %all-gather.65.cloned.1.call-update) | async-done | bytes 2097168 | tf_op jit(solution)/shard_map/all_gather | solution.py:241
  482.6 10.4 %shard_map.160 = (bf16[512,2048]{1,0:T(8,128)(2,1)}, bf16[512,2048]{1,0:T(8,128)(2,1)}) custom-call(bf16[512,2048]{1,0:T(8,128)(2,1)} %all-gather.39.cloned.1.call-done.x_ref, bf16[4,512,512]{2,1,0:T(8,128)(2,1)} %bitcast.157, bf16[4,512,2048]{2,1,0:T(8,128)(2,1)} %pad_maximum_fusion.2.w_ref, f32[1,2048]{1,0:T(1,128)} %get-tuple-element.141.gain_ref), custom_call_target="tpu_custom_call" | custom-call | flops 4294967296 | bytes 16777216 | tf_op jit(solution)/shard_map/pallas_call | solution.py:131
  493.1 22.7 %shard_map.161 = bf16[512,2048]{1,0:T(8,128)(2,1)} custom-call(bf16[512,2048]{1,0:T(8,128)(2,1)} %get-tuple-element.82.a_ref, bf16[2,2048,1024]{2,1,0:T(8,128)(2,1)} %wg_m.15, bf16[2048,1024]{1,0:T(8,128)(2,1)} %collective-permute-done.11.wg_o, bf16[2,2048,1024]{2,1,0:T(8,128)(2,1)} %wu_m.15, bf16[2048,1024]{1,0:T(8,128)(2,1)} %collective-permute-done.12.wu_o, ...), custom_call_target="tpu_custom_call" | custom-call | flops 12884901888 | bytes 29360128 | tf_op jit(solution)/shard_map/pallas_call | solution.py:179
  515.9 11.0 %shard_map.152 = (bf16[512,2048]{1,0:T(8,128)(2,1)}, bf16[512,2048]{1,0:T(8,128)(2,1)}) custom-call(bf16[512,2048]{1,0:T(8,128)(2,1)} %all-gather.37.cloned.1.call-done.x_ref, bf16[4,512,512]{2,1,0:T(8,128)(2,1)} %bitcast.153, bf16[4,512,2048]{2,1,0:T(8,128)(2,1)} %pad_maximum_fusion.2.w_ref, f32[1,2048]{1,0:T(1,128)} %get-tuple-element.141.gain_ref), custom_call_target="tpu_custom_call" | custom-call | flops 4294967296 | bytes 16777216 | tf_op jit(solution)/shard_map/pallas_call | solution.py:131
  526.9 22.7 %shard_map.153 = bf16[512,2048]{1,0:T(8,128)(2,1)} custom-call(bf16[512,2048]{1,0:T(8,128)(2,1)} %get-tuple-element.72.a_ref, bf16[2,2048,1024]{2,1,0:T(8,128)(2,1)} %wg_m.15, bf16[2048,1024]{1,0:T(8,128)(2,1)} %collective-permute-done.11.wg_o, bf16[2,2048,1024]{2,1,0:T(8,128)(2,1)} %wu_m.15, bf16[2048,1024]{1,0:T(8,128)(2,1)} %collective-permute-done.12.wu_o, ...), custom_call_target="tpu_custom_call" | custom-call | flops 12884901888 | bytes 29360128 | tf_op jit(solution)/shard_map/pallas_call | solution.py:179
  549.7 10.7 %shard_map.144 = (bf16[512,2048]{1,0:T(8,128)(2,1)}, bf16[512,2048]{1,0:T(8,128)(2,1)}) custom-call(bf16[512,2048]{1,0:T(8,128)(2,1)} %all-gather.35.cloned.1.call-done.x_ref, bf16[4,512,512]{2,1,0:T(8,128)(2,1)} %bitcast.151, bf16[4,512,2048]{2,1,0:T(8,128)(2,1)} %pad_maximum_fusion.2.w_ref, f32[1,2048]{1,0:T(1,128)} %get-tuple-element.141.gain_ref), custom_call_target="tpu_custom_call" | custom-call | flops 4294967296 | bytes 16777216 | tf_op jit(solution)/shard_map/pallas_call | solution.py:131
  560.4 22.6 %shard_map.145 = bf16[512,2048]{1,0:T(8,128)(2,1)} custom-call(bf16[512,2048]{1,0:T(8,128)(2,1)} %get-tuple-element.62.a_ref, bf16[2,2048,1024]{2,1,0:T(8,128)(2,1)} %wg_m.15, bf16[2048,1024]{1,0:T(8,128)(2,1)} %collective-permute-done.11.wg_o, bf16[2,2048,1024]{2,1,0:T(8,128)(2,1)} %wu_m.15, bf16[2048,1024]{1,0:T(8,128)(2,1)} %collective-permute-done.12.wu_o, ...), custom_call_target="tpu_custom_call" | custom-call | flops 12884901888 | bytes 29360128 | tf_op jit(solution)/shard_map/pallas_call | solution.py:179
  583.2 10.7 %shard_map.136 = (bf16[512,2048]{1,0:T(8,128)(2,1)}, bf16[512,2048]{1,0:T(8,128)(2,1)}) custom-call(bf16[512,2048]{1,0:T(8,128)(2,1)} %all-gather.33.cloned.1.call-done.x_ref, bf16[4,512,512]{2,1,0:T(8,128)(2,1)} %bitcast.155, bf16[4,512,2048]{2,1,0:T(8,128)(2,1)} %pad_maximum_fusion.2.w_ref, f32[1,2048]{1,0:T(1,128)} %get-tuple-element.141.gain_ref), custom_call_target="tpu_custom_call" | custom-call | flops 4294967296 | bytes 16777216 | tf_op jit(solution)/shard_map/pallas_call | solution.py:131
  593.9 22.6 %shard_map.137 = bf16[512,2048]{1,0:T(8,128)(2,1)} custom-call(bf16[512,2048]{1,0:T(8,128)(2,1)} %get-tuple-element.52.a_ref, bf16[2,2048,1024]{2,1,0:T(8,128)(2,1)} %wg_m.15, bf16[2048,1024]{1,0:T(8,128)(2,1)} %collective-permute-done.11.wg_o, bf16[2,2048,1024]{2,1,0:T(8,128)(2,1)} %wu_m.15, bf16[2048,1024]{1,0:T(8,128)(2,1)} %collective-permute-done.12.wu_o, ...), custom_call_target="tpu_custom_call" | custom-call | flops 12884901888 | bytes 29360128 | tf_op jit(solution)/shard_map/pallas_call | solution.py:179
  624.6 25.3 %reduce-scatter.15.cloned.1.call-done = bf16[128,2048]{1,0:T(8,128)(2,1)} async-done(((bf16[512,2048]{1,0:T(8,128)(2,1)}), bf16[128,2048]{1,0:T(8,128)(2,1)}) %reduce-scatter.15.cloned.1.call-update) | async-done | bytes 524304 | tf_op jit(solution)/shard_map/reduce_scatter | solution.py:244
  652.5 25.6 %reduce-scatter.11.cloned.1.call-done = bf16[128,2048]{1,0:T(8,128)(2,1)} async-done(((bf16[512,2048]{1,0:T(8,128)(2,1)}), bf16[128,2048]{1,0:T(8,128)(2,1)}) %reduce-scatter.11.cloned.1.call-update) | async-done | bytes 524304 | tf_op jit(solution)/shard_map/reduce_scatter | solution.py:244
  696.1 11.1 %all-gather.67.cloned.1.call-done = bf16[1024,2048]{1,0:T(8,128)(2,1)} async-done(((bf16[128,2048]{1,0:T(8,128)(2,1)}), bf16[1024,2048]{1,0:T(8,128)(2,1)}) %all-gather.67.cloned.1.call-update) | async-done | bytes 4194320 | tf_op jit(solution)/shard_map/all_gather | solution.py:250
  712.0 24.4 %all-gather.61.cloned.1.call-done = bf16[1024,2048]{1,0:T(8,128)(2,1)} async-done(((bf16[128,2048]{1,0:T(8,128)(2,1)}), bf16[1024,2048]{1,0:T(8,128)(2,1)}) %all-gather.61.cloned.1.call-update) | async-done | bytes 4194320 | tf_op jit(solution)/shard_map/all_gather | solution.py:250
  741.2 24.5 %all-gather.55.cloned.1.call-done = bf16[1024,2048]{1,0:T(8,128)(2,1)} async-done(((bf16[128,2048]{1,0:T(8,128)(2,1)}), bf16[1024,2048]{1,0:T(8,128)(2,1)}) %all-gather.55.cloned.1.call-update) | async-done | bytes 4194320 | tf_op jit(solution)/shard_map/all_gather | solution.py:250
  770.4 24.4 %all-gather.49.cloned.1.call-done = bf16[1024,2048]{1,0:T(8,128)(2,1)} async-done(((bf16[128,2048]{1,0:T(8,128)(2,1)}), bf16[1024,2048]{1,0:T(8,128)(2,1)}) %all-gather.49.cloned.1.call-update) | async-done | bytes 4194320 | tf_op jit(solution)/shard_map/all_gather | solution.py:250
  799.5 9.4 %pad_maximum_fusion = bf16[2,2048,2048]{2,1,0:T(8,128)(2,1)} fusion(bf16[2,512,2048]{2,1,0:T(8,128)(2,1)S(1)} %bitcast.134, bf16[2,512,2048]{2,1,0:T(8,128)(2,1)S(1)} %bitcast.135, bf16[2,512,2048]{2,1,0:T(8,128)(2,1)} %bitcast.136, bf16[2,512,2048]{2,1,0:T(8,128)(2,1)S(1)} %bitcast.137), kind=kLoop, calls=%fused_computation | loop fusion | flops 67108864 | bytes 33554432 | tf_op jit(solution)/shard_map/concatenate | solution.py:257
  (215 shorter events, 109.9 us)
Async XLA Ops:
  7.2 81.7 %all-gather.43.cloned.1.call-start = ((), (), s32[]{:S(2)}) async-start(), calls=%async_computation.21 | async-start | bytes 5242880 | tf_op jit(solution)/shard_map/all_gather | solution.py:229
  10.6 107.8 %all-gather.63.cloned.1.call-start = ((), (), s32[]{:S(2)}) async-start(), calls=%async_computation.31 | async-start | bytes 2621440 | tf_op jit(solution)/shard_map/all_gather | solution.py:241
  11.8 288.0 %copy-start.5 = (bf16[2048,256]{1,0:T(8,128)(2,1)}, bf16[2048,256]{1,0:T(8,128)(2,1)S(1)}, u32[]{:S(2)}) copy-start(bf16[2048,256]{1,0:T(8,128)(2,1)S(1)} %get-tuple-element.99.refs_0_) | copy-start | bytes 3145732
  11.8 17.5 %collective-permute-start = (bf16[2048,256]{1,0:T(8,128)(2,1)}, bf16[2048,256]{1,0:T(8,128)(2,1)}, u32[]{:S(2)}, u32[]{:S(2)}) collective-permute-start(bf16[2048,256]{1,0:T(8,128)(2,1)} %get-tuple-element.100.refs_0_), channel_id=1, source_target_pairs={{0,1},{1,0},{2,3},{3,2},{4,5},{5,4},{6,7},{7,6},{8,9},{9,8},{10,11... | collective-permute-start | bytes 3145736 | tf_op jit(solution)/shard_map/ppermute | solution.py:206
  13.8 286.1 %copy-start.6 = (bf16[2048,256]{1,0:T(8,128)(2,1)}, bf16[2048,256]{1,0:T(8,128)(2,1)S(1)}, u32[]{:S(2)}) copy-start(bf16[2048,256]{1,0:T(8,128)(2,1)S(1)} %get-tuple-element.97.refs_2_) | copy-start | bytes 3145732
  13.8 15.6 %collective-permute-start.1 = (bf16[2048,256]{1,0:T(8,128)(2,1)}, bf16[2048,256]{1,0:T(8,128)(2,1)}, u32[]{:S(2)}, u32[]{:S(2)}) collective-permute-start(bf16[2048,256]{1,0:T(8,128)(2,1)} %get-tuple-element.98.refs_2_), channel_id=1, source_target_pairs={{0,1},{1,0},{2,3},{3,2},{4,5},{5,4},{6,7},{7,6},{8,9},{9,8},{10,11... | collective-permute-start | bytes 3145736 | tf_op jit(solution)/shard_map/ppermute | solution.py:206
  15.1 285.3 %copy-start.7 = (bf16[2048,256]{1,0:T(8,128)(2,1)}, bf16[2048,256]{1,0:T(8,128)(2,1)S(1)}, u32[]{:S(2)}) copy-start(bf16[2048,256]{1,0:T(8,128)(2,1)S(1)} %get-tuple-element.95.refs_4_) | copy-start | bytes 3145732
  15.1 14.3 %collective-permute-start.2 = (bf16[2048,256]{1,0:T(8,128)(2,1)}, bf16[2048,256]{1,0:T(8,128)(2,1)}, u32[]{:S(2)}, u32[]{:S(2)}) collective-permute-start(bf16[2048,256]{1,0:T(8,128)(2,1)} %get-tuple-element.96.refs_4_), channel_id=1, source_target_pairs={{0,1},{1,0},{2,3},{3,2},{4,5},{5,4},{6,7},{7,6},{8,9},{9,8},{10,11... | collective-permute-start | bytes 3145736 | tf_op jit(solution)/shard_map/ppermute | solution.py:206
  71.7 79.5 %all-gather.41.cloned.1.call-start = ((), (), s32[]{:S(2)}) async-start(), calls=%async_computation.20 | async-start | bytes 2621440 | tf_op jit(solution)/shard_map/all_gather | solution.py:241
  76.2 107.9 %all-gather.51.cloned.1.call-start = ((), (), s32[]{:S(2)}) async-start(), calls=%async_computation.25 | async-start | bytes 2621440 | tf_op jit(solution)/shard_map/all_gather | solution.py:241
  82.8 46.2 %collective-permute-start.4 = (bf16[2048,1024]{1,0:T(8,128)(2,1)}, bf16[2048,1024]{1,0:T(8,128)(2,1)}, u32[]{:S(2)}, u32[]{:S(2)}) collective-permute-start(bf16[2048,1024]{1,0:T(8,128)(2,1)} %get-tuple-element.92), channel_id=1, source_target_pairs={{0,1},{1,0},{2,3},{3,2},{4,5},{5,4},{6,7},{7,6},{8,9},{9,8},{10,11... | collective-permute-start | bytes 12582920 | tf_op jit(solution)/shard_map/ppermute | solution.py:206
  88.8 128.2 %all-gather.57.cloned.1.call-start = ((), (), s32[]{:S(2)}) async-start(), calls=%async_computation.28 | async-start | bytes 2621440 | tf_op jit(solution)/shard_map/all_gather | solution.py:241
  88.9 21.0 %collective-permute-start.3 = (bf16[4,256,2048]{2,1,0:T(8,128)(2,1)}, bf16[4,256,2048]{2,1,0:T(8,128)(2,1)}, u32[]{:S(2)}, u32[]{:S(2)}) collective-permute-start(bf16[4,256,2048]{2,1,0:T(8,128)(2,1)} %bitcast.142), channel_id=1, source_target_pairs={{0,1},{1,0},{2,3},{3,2},{4,5},{5,4},{6,7},{7,6},{8,9},{9,8},{10,11... | collective-permute-start | bytes 12582920 | tf_op jit(solution)/shard_map/ppermute | solution.py:206
  95.2 33.8 %collective-permute-start.5 = (bf16[2048,1024]{1,0:T(8,128)(2,1)}, bf16[2048,1024]{1,0:T(8,128)(2,1)}, u32[]{:S(2)}, u32[]{:S(2)}) collective-permute-start(bf16[2048,1024]{1,0:T(8,128)(2,1)} %get-tuple-element.90), channel_id=1, source_target_pairs={{0,1},{1,0},{2,3},{3,2},{4,5},{5,4},{6,7},{7,6},{8,9},{9,8},{10,11... | collective-permute-start | bytes 12582920 | tf_op jit(solution)/shard_map/ppermute | solution.py:206
  101.6 27.4 %collective-permute-start.6 = (bf16[1024,2048]{1,0:T(8,128)(2,1)}, bf16[1024,2048]{1,0:T(8,128)(2,1)}, u32[]{:S(2)}, u32[]{:S(2)}) collective-permute-start(bf16[1024,2048]{1,0:T(8,128)(2,1)} %get-tuple-element.88), channel_id=1, source_target_pairs={{0,1},{1,0},{2,3},{3,2},{4,5},{5,4},{6,7},{7,6},{8,9},{9,8},{10,11... | collective-permute-start | bytes 12582920 | tf_op jit(solution)/shard_map/ppermute | solution.py:206
  109.2 141.0 %reduce-scatter.21.cloned.1.call-start = ((), (), s32[]{:S(2)}) async-start(), calls=%async_computation.17 | async-start | bytes 2621440 | tf_op jit(solution)/shard_map/reduce_scatter | solution.py:244
  151.2 101.4 %reduce-scatter.9.cloned.1.call-start = ((), (), s32[]{:S(2)}) async-start(), calls=%async_computation.8 | async-start | bytes 2621440 | tf_op jit(solution)/shard_map/reduce_scatter | solution.py:244
  184.0 84.6 %reduce-scatter.13.cloned.1.call-start = ((), (), s32[]{:S(2)}) async-start(), calls=%async_computation.11 | async-start | bytes 2621440 | tf_op jit(solution)/shard_map/reduce_scatter | solution.py:244
  217.0 79.9 %reduce-scatter.17.cloned.1.call-start = ((), (), s32[]{:S(2)}) async-start(), calls=%async_computation.14 | async-start | bytes 2621440 | tf_op jit(solution)/shard_map/reduce_scatter | solution.py:244
  250.1 74.3 %all-gather.39.cloned.1.call-start = ((), (), s32[]{:S(2)}) async-start(), calls=%async_computation.18 | async-start | bytes 2621440 | tf_op jit(solution)/shard_map/all_gather | solution.py:248
  252.4 100.1 %all-gather.33.cloned.1.call-start = ((), (), s32[]{:S(2)}) async-start(), calls=%async_computation.9 | async-start | bytes 2621440 | tf_op jit(solution)/shard_map/all_gather | solution.py:248
  254.7 125.6 %all-gather.35.cloned.1.call-start = ((), (), s32[]{:S(2)}) async-start(), calls=%async_computation.12 | async-start | bytes 2621440 | tf_op jit(solution)/shard_map/all_gather | solution.py:248
  270.8 137.6 %all-gather.37.cloned.1.call-start = ((), (), s32[]{:S(2)}) async-start(), calls=%async_computation.15 | async-start | bytes 2621440 | tf_op jit(solution)/shard_map/all_gather | solution.py:248
  299.1 154.7 %all-gather.47.cloned.1.call-start = ((), (), s32[]{:S(2)}) async-start(), calls=%async_computation.23 | async-start | bytes 5242880 | tf_op jit(solution)/shard_map/all_gather | solution.py:229
  299.7 182.9 %all-gather.65.cloned.1.call-start = ((), (), s32[]{:S(2)}) async-start(), calls=%async_computation.32 | async-start | bytes 2621440 | tf_op jit(solution)/shard_map/all_gather | solution.py:241
  299.8 2.7 collective-permute-start.7
  299.9 4.1 collective-permute-start.8
  300.4 5.1 collective-permute-start.9
  425.4 90.4 %all-gather.59.cloned.1.call-start = ((), (), s32[]{:S(2)}) async-start(), calls=%async_computation.29 | async-start | bytes 2621440 | tf_op jit(solution)/shard_map/all_gather | solution.py:241
  432.7 117.0 %all-gather.53.cloned.1.call-start = ((), (), s32[]{:S(2)}) async-start(), calls=%async_computation.26 | async-start | bytes 2621440 | tf_op jit(solution)/shard_map/all_gather | solution.py:241
  438.8 144.4 %all-gather.45.cloned.1.call-start = ((), (), s32[]{:S(2)}) async-start(), calls=%async_computation.22 | async-start | bytes 2621440 | tf_op jit(solution)/shard_map/all_gather | solution.py:241
  453.8 7.1 collective-permute-start.10
  453.8 39.3 %collective-permute-start.11 = (bf16[2048,1024]{1,0:T(8,128)(2,1)}, bf16[2048,1024]{1,0:T(8,128)(2,1)}, u32[]{:S(2)}, u32[]{:S(2)}) collective-permute-start(bf16[2048,1024]{1,0:T(8,128)(2,1)} %get-tuple-element.91), channel_id=1, source_target_pairs={{0,1},{1,0},{2,3},{3,2},{4,5},{5,4},{6,7},{7,6},{8,9},{9,8},{10,11... | collective-permute-start | bytes 12582920 | tf_op jit(solution)/shard_map/ppermute | solution.py:206
  454.3 38.8 %collective-permute-start.12 = (bf16[2048,1024]{1,0:T(8,128)(2,1)}, bf16[2048,1024]{1,0:T(8,128)(2,1)}, u32[]{:S(2)}, u32[]{:S(2)}) collective-permute-start(bf16[2048,1024]{1,0:T(8,128)(2,1)} %get-tuple-element.89), channel_id=1, source_target_pairs={{0,1},{1,0},{2,3},{3,2},{4,5},{5,4},{6,7},{7,6},{8,9},{9,8},{10,11... | collective-permute-start | bytes 12582920 | tf_op jit(solution)/shard_map/ppermute | solution.py:206
  454.3 38.8 %collective-permute-start.13 = (bf16[1024,2048]{1,0:T(8,128)(2,1)}, bf16[1024,2048]{1,0:T(8,128)(2,1)}, u32[]{:S(2)}, u32[]{:S(2)}) collective-permute-start(bf16[1024,2048]{1,0:T(8,128)(2,1)} %get-tuple-element.87), channel_id=1, source_target_pairs={{0,1},{1,0},{2,3},{3,2},{4,5},{5,4},{6,7},{7,6},{8,9},{9,8},{10,11... | collective-permute-start | bytes 12582920 | tf_op jit(solution)/shard_map/ppermute | solution.py:206
  459.2 157.5 %reduce-scatter.23.cloned.1.call-start = ((), (), s32[]{:S(2)}) async-start(), calls=%async_computation.19 | async-start | bytes 2621440 | tf_op jit(solution)/shard_map/reduce_scatter | solution.py:244
  515.8 106.5 %reduce-scatter.19.cloned.1.call-start = ((), (), s32[]{:S(2)}) async-start(), calls=%async_computation.16 | async-start | bytes 2621440 | tf_op jit(solution)/shard_map/reduce_scatter | solution.py:244
  549.6 100.3 %reduce-scatter.15.cloned.1.call-start = ((), (), s32[]{:S(2)}) async-start(), calls=%async_computation.13 | async-start | bytes 2621440 | tf_op jit(solution)/shard_map/reduce_scatter | solution.py:244
  583.1 95.0 %reduce-scatter.11.cloned.1.call-start = ((), (), s32[]{:S(2)}) async-start(), calls=%async_computation.10 | async-start | bytes 2621440 | tf_op jit(solution)/shard_map/reduce_scatter | solution.py:244
  616.6 90.6 %all-gather.67.cloned.1.call-start = ((), (), s32[]{:S(2)}) async-start(), calls=%async_computation.33 | async-start | bytes 4718592 | tf_op jit(solution)/shard_map/all_gather | solution.py:250
  618.9 117.5 %all-gather.61.cloned.1.call-start = ((), (), s32[]{:S(2)}) async-start(), calls=%async_computation.30 | async-start | bytes 4718592 | tf_op jit(solution)/shard_map/all_gather | solution.py:250
  622.2 30.2 %copy-start.15 = (bf16[2,512,256]{2,1,0:T(8,128)(2,1)S(1)}, bf16[2,512,256]{2,1,0:T(8,128)(2,1)}, u32[]{:S(2)}) copy-start(bf16[2,512,256]{2,1,0:T(8,128)(2,1)} %get-tuple-element.74.refs_3_) | copy-start | bytes 1572868
  624.5 141.1 %all-gather.55.cloned.1.call-start = ((), (), s32[]{:S(2)}) async-start(), calls=%async_computation.27 | async-start | bytes 4718592 | tf_op jit(solution)/shard_map/all_gather | solution.py:250
  652.1 142.7 %all-gather.49.cloned.1.call-start = ((), (), s32[]{:S(2)}) async-start(), calls=%async_computation.24 | async-start | bytes 4718592 | tf_op jit(solution)/shard_map/all_gather | solution.py:250
  680.6 2.7 collective-permute-start.14
  682.1 5.9 collective-permute-start.16
  686.6 2.7 collective-permute-start.15
  687.8 3.2 collective-permute-start.17
  (25 other events, 107.4 us)
Sparse Core Ops, SparseCore 0:
  10.7 46.8 all-gather.42
  71.9 29.2 all-gather.62
  102.7 26.4 all-gather.40
  130.6 26.4 all-gather.50
  158.5 26.4 all-gather.56
  187.7 25.6 reduce-scatter.20
  215.6 25.3 reduce-scatter.8
  243.3 25.3 reduce-scatter.12
  271.5 25.3 reduce-scatter.16
  298.3 26.1 all-gather.38
  326.0 26.4 all-gather.32
  353.9 26.4 all-gather.34
  381.9 26.4 all-gather.36
  409.8 43.9 all-gather.46
  455.7 26.8 all-gather.64
  484.0 26.4 all-gather.58
  511.9 26.4 all-gather.52
  539.8 26.4 all-gather.44
  569.1 25.6 reduce-scatter.22
  596.9 25.3 reduce-scatter.18
  624.5 25.3 reduce-scatter.14
  652.8 25.3 reduce-scatter.10
  679.7 27.3 all-gather.66
  708.6 27.6 all-gather.60
  737.9 27.6 all-gather.54
  767.1 27.6 all-gather.48

commit v2 on v0

v2 whole, which is shorter than its diff:
```python
import functools

import jax
import jax.numpy as jnp
from jax import lax
from jax.experimental import pallas as pl
from jax.experimental.pallas import tpu as pltpu
from jax.sharding import Mesh
from jax.sharding import PartitionSpec as P


RMS_EPS = 1e-6
ROPE_BASE = 10000.0
CORES = 2
CHIPS = 4
CHUNKS = 4
ROW_TILE = 256
FF_TILE = 256
VMEM = 60 * 1024 * 1024
BF16 = jnp.bfloat16
F32 = jnp.float32
ANY = pl.BlockSpec(memory_space=pl.ANY)
SMEM = pl.BlockSpec(memory_space=pltpu.SMEM)
OFFSETS = (0, 3, 1, 2)


def cost(flops, nbytes, exps=0):
    return pl.CostEstimate(flops=int(flops), bytes_accessed=int(nbytes), transcendentals=int(exps))


def norm_rows(x_f32, gain):
    mean_sq = jnp.mean(x_f32 * x_f32, axis=-1, keepdims=True)
    return (x_f32 * lax.rsqrt(mean_sq + RMS_EPS) * (1.0 + gain)).astype(BF16)


def struct(shape, dtype=BF16):
    return jax.ShapeDtypeStruct(shape, dtype)


def whole(shape):
    return pl.BlockSpec(shape, lambda *_: (0,) * len(shape))


def piece_rows(ids_ref, place, half, part):
    return pl.multiple_of(lax.rem(ids_ref[0] + OFFSETS[place], CHIPS) * part + half * (part // 2), part // 2)


def front_kernel(layer, chunk, pieces, ids_ref, len_ref, gain_ref, cos_ref, sin_ref, *refs):
    refs = list(refs)
    x_refs = [refs.pop(0) for _ in range(8 if pieces else 1)]
    w_refs = [refs.pop(0) for _ in range(6)]
    old = [[refs.pop(0) for _ in range(chunk)] for _ in range(4)]
    x_out = refs.pop(0) if pieces else None
    new = [refs.pop(0) for _ in range(4)]
    o_refs = [refs.pop(0) for _ in range(2)]
    x_buf, normed, w_buf, q_buf, x_sem, w_sem, out_sem = refs
    rows, _ = x_buf.shape
    head = q_buf.shape[-1]
    half = head // 2
    if pieces:
        part = rows // CHIPS
        copies = [
            pltpu.make_async_copy(x_refs[n], x_buf.at[pl.ds(piece_rows(ids_ref, n // 2, n % 2, part), part // 2)], x_sem.at[n])
            for n in range(8)
        ]
    else:
        copies = [pltpu.make_async_copy(x_refs[0].at[ids_ref[1], pl.ds(chunk * rows, rows)], x_buf, x_sem.at[0])]
    for c in copies:
        c.start()
    loads = [pltpu.make_async_copy(w_refs[n].at[layer], w_buf.at[n], w_sem.at[n]) for n in range(6)]
    for c in loads:
        c.start()
    for c in copies:
        c.wait()
    save = None
    if pieces:
        save = pltpu.make_async_copy(x_buf, x_out, out_sem)
        save.start()
    tile = min(ROW_TILE, rows)
    for r in range(0, rows, tile):
        normed[pl.ds(r, tile)] = norm_rows(x_buf[pl.ds(r, tile)].astype(F32), gain_ref[...])

    def rope(y, at):
        low, high = y[:, :half], y[:, half:]
        c, s = cos_ref[pl.ds(at, tile)], sin_ref[pl.ds(at, tile)]
        return jnp.concatenate([low * c - high * s, high * c + low * s], axis=-1)

    for n in range(6):
        loads[n].wait()
        for r in range(0, rows, tile):
            y = jnp.dot(normed[pl.ds(r, tile)], w_buf[n], preferred_element_type=F32)
            if n < 2:
                q_buf[n, pl.ds(r, tile)] = (rope(y, r) * head**-0.5).astype(BF16)
            elif n < 4:
                new[n - 2][pl.ds(r, tile)] = rope(y, r).astype(BF16)
            else:
                new[n - 2][pl.ds(r, tile)] = y.astype(BF16)

    dims = (((1,), (1,)), ((), ()))
    length = len_ref[0]
    col = lax.broadcasted_iota(jnp.int32, (1, rows), 1)
    lower = lax.broadcasted_iota(jnp.int32, (tile, rows), 1) - lax.broadcasted_iota(jnp.int32, (tile, rows), 0)
    bias = [jnp.where(col < length - j * rows, 0.0, -1e30).astype(F32) for j in range(chunk + 1)]
    for h in range(2):
        keys = old[h] + [new[h]]
        values = old[2 + h] + [new[2 + h]]
        for r in range(0, rows, tile):
            query = q_buf[h, pl.ds(r, tile)]
            blocks = []
            for j in range(chunk + 1):
                scores = lax.dot_general(query, keys[j][...], dims, preferred_element_type=F32) + bias[j]
                if j == chunk:
                    scores = jnp.where(lower <= r, scores, -1e30)
                blocks.append(scores)
            top = functools.reduce(jnp.maximum, [jnp.max(b, axis=-1, keepdims=True) for b in blocks])
            blocks = [jnp.exp(b - top) for b in blocks]
            inv = 1.0 / functools.reduce(jnp.add, [jnp.sum(b, axis=-1, keepdims=True) for b in blocks])
            total = None
            for j in range(chunk + 1):
                prod = jnp.dot((blocks[j] * inv).astype(BF16), values[j][...], preferred_element_type=F32)
                total = prod if total is None else total + prod
            o_refs[h][pl.ds(r, tile)] = total.astype(BF16)
    if save is not None:
        save.wait()


def front_call(layer, chunk, ids, length, gain, cos_t, sin_t, x_list, weights, old, rows):
    width, head = weights[0].shape[1:]
    pieces = len(x_list) > 1
    small = whole((rows, head))
    table = pl.BlockSpec((rows, head // 2), lambda *_: (chunk, 0))
    flops = 12 * rows * width * head + 8 * rows * rows * (chunk + 1) * head
    out_shape = [struct((rows, head))] * 6
    out_specs = [small] * 6
    if pieces:
        out_shape = [struct((rows, width))] + out_shape
        out_specs = [ANY] + out_specs
    out = pl.pallas_call(
        functools.partial(front_kernel, layer, chunk, pieces),
        grid=(1,),
        out_shape=out_shape,
        in_specs=[SMEM, SMEM, whole((1, width)), table, table] + [ANY] * (len(x_list) + 6) + [small] * (4 * chunk),
        out_specs=out_specs,
        scratch_shapes=[
            pltpu.VMEM((rows, width), BF16),
            pltpu.VMEM((rows, width), BF16),
            pltpu.VMEM((6, width, head), BF16),
            pltpu.VMEM((2, rows, head), BF16),
            pltpu.SemaphoreType.DMA((8,)),
            pltpu.SemaphoreType.DMA((6,)),
            pltpu.SemaphoreType.DMA,
        ],
        compiler_params=pltpu.CompilerParams(vmem_limit_bytes=VMEM),
        cost_estimate=cost(flops, 12 * width * head + 4 * rows * width, 2 * rows * rows * (chunk + 1)),
    )(ids, length, gain, cos_t, sin_t, *x_list, *weights, *[k for group in old for k in group])
    return out if pieces else [None] + list(out)


def back_kernel(chunk, from_hidden, ids_ref, gain_ref, x_ref, *refs):
    refs = list(refs)
    o_refs = [refs.pop(0) for _ in range(8)]
    w_refs = [refs.pop(0) for _ in range(8)]
    ff = [refs.pop(0) for _ in range(6)]
    base = [refs.pop(0) for _ in range(2)]
    sends = [[refs.pop(0) for _ in range(2)] for _ in range(3)]
    x_buf, o_buf, w_buf, normed, acc, x_sem, o_sem, w_sem = refs
    rows, _ = x_buf.shape
    head = o_refs[0].shape[-1]
    part = rows // CHIPS
    step = pl.program_id(0)
    tile = min(ROW_TILE, rows)

    @pl.when(step == 0)
    def _():
        src = x_ref.at[ids_ref[1], pl.ds(chunk * rows, rows)] if from_hidden else x_ref
        x_copy = pltpu.make_async_copy(src, x_buf, x_sem)
        o_copies = [pltpu.make_async_copy(o_refs[n], o_buf.at[:, pl.ds(n * head, head)], o_sem.at[n]) for n in range(8)]
        w_copies = [pltpu.make_async_copy(w_refs[n], w_buf.at[pl.ds(n * head, head)], w_sem.at[n]) for n in range(8)]
        for n in range(8):
            o_copies[n].start()
            w_copies[n].start()
        x_copy.start()
        for group in range(2):
            for n in range(4 * group, 4 * group + 4):
                o_copies[n].wait()
                w_copies[n].wait()
            if group == 1:
                x_copy.wait()
            cut = pl.ds(4 * group * head, 4 * head)
            for r in range(0, rows, tile):
                prod = jnp.dot(o_buf[pl.ds(r, tile), cut], w_buf[cut], preferred_element_type=F32)
                if group == 0:
                    acc[pl.ds(r, tile)] = prod
                else:
                    mid = (x_buf[pl.ds(r, tile)].astype(F32) + (acc[pl.ds(r, tile)] + prod)).astype(BF16)
                    x_buf[pl.ds(r, tile)] = mid
                    normed[pl.ds(r, tile)] = norm_rows(mid.astype(F32), gain_ref[...])

    a = normed[...]
    total = None
    for n in range(2):
        gate = jnp.dot(a, ff[n][...], preferred_element_type=F32)
        up = jnp.dot(a, ff[2 + n][...], preferred_element_type=F32)
        act = (jax.nn.gelu(gate, approximate=True) * up).astype(BF16)
        prod = jnp.dot(act, ff[4 + n][...], preferred_element_type=F32)
        total = prod if total is None else total + prod

    @pl.when(step == 0)
    def _():
        acc[...] = total

    @pl.when(step > 0)
    def _():
        acc[...] += total

    @pl.when(step == pl.num_programs(0) - 1)
    def _():
        for half in range(2):
            own = pl.ds(piece_rows(ids_ref, 0, half, part), part // 2)
            base[half][...] = x_buf[own].astype(F32) + acc[own]
            for place in range(1, 4):
                cut = pl.ds(piece_rows(ids_ref, place, half, part), part // 2)
                sends[place - 1][half][...] = acc[cut].astype(BF16)


def back_call(layer, chunk, ids, gain, x, o_list, w_list, ff_w, rows):
    width = w_list[0].shape[-1]
    head = w_list[0].shape[0]
    ff = ff_w[0].shape[-1]
    tile = min(FF_TILE, ff)
    col = pl.BlockSpec((None, width, tile), lambda i: (layer, 0, i))
    row = pl.BlockSpec((None, tile, width), lambda i: (layer, i, 0))
    half = rows // CHIPS // 2
    return pl.pallas_call(
        functools.partial(back_kernel, chunk, x.ndim == 3),
        grid=(ff // tile,),
        out_shape=[struct((half, width), F32)] * 2 + [struct((half, width))] * 6,
        in_specs=[SMEM, whole((1, width))] + [ANY] * 17 + [col] * 4 + [row] * 2,
        out_specs=[whole((half, width))] * 8,
        scratch_shapes=[
            pltpu.VMEM((rows, width), BF16),
            pltpu.VMEM((rows, 8 * head), BF16),
            pltpu.VMEM((8 * head, width), BF16),
            pltpu.VMEM((rows, width), BF16),
            pltpu.VMEM((rows, width), F32),
            pltpu.SemaphoreType.DMA,
            pltpu.SemaphoreType.DMA((8,)),
            pltpu.SemaphoreType.DMA((8,)),
        ],
        compiler_params=pltpu.CompilerParams(vmem_limit_bytes=VMEM),
        cost_estimate=cost(12 * rows * width * ff + 16 * rows * head * width, 12 * width * ff + 16 * head * width + 8 * rows * width, 2 * rows * ff),
    )(ids, gain, x, *o_list, *w_list, *ff_w)


def place_kernel(chunk, ids_ref, *refs):
    pieces, (h_ref, buf, in_sem, out_sem) = refs[:16], refs[-4:]
    part = 2 * pieces[0].shape[0]
    copies = []
    for n in range(16):
        copies.append(pltpu.make_async_copy(pieces[n], buf.at[n], in_sem.at[n]))
        copies[-1].start()
    outs = []
    for n in range(16):
        prompt = ids_ref[1] if n < 8 else 1 - ids_ref[1]
        at = chunk * part * CHIPS + piece_rows(ids_ref, n % 8 // 2, n % 2, part)
        copies[n].wait()
        outs.append(pltpu.make_async_copy(buf.at[n], h_ref.at[prompt, pl.ds(pl.multiple_of(at, part // 2), part // 2)], out_sem.at[n]))
        outs[-1].start()
    for c in outs:
        c.wait()


def place_call(chunk, ids, pieces, before, shape):
    extra = [] if before is None else [before]
    return pl.pallas_call(
        functools.partial(place_kernel, chunk),
        out_shape=struct(shape),
        in_specs=[SMEM] + [ANY] * (16 + len(extra)),
        out_specs=ANY,
        scratch_shapes=[pltpu.VMEM((16, *pieces[0].shape), BF16), pltpu.SemaphoreType.DMA((16,)), pltpu.SemaphoreType.DMA((16,))],
        input_output_aliases={17: 0} if extra else {},
        compiler_params=pltpu.CompilerParams(vmem_limit_bytes=VMEM),
        cost_estimate=cost(2e9, 1 << 23),
    )(ids, *pieces, *extra)


def rope_tables(seq_len, head_dim):
    half_dim = head_dim // 2
    inv_freq = ROPE_BASE ** (-jnp.arange(half_dim, dtype=F32) * (2.0 / head_dim))
    angles = jnp.arange(seq_len, dtype=F32)[:, None] * inv_freq[None, :]
    return jnp.cos(angles), jnp.sin(angles)


def solution(mesh):
    groups, members = mesh.devices.shape
    chips = members // CORES
    assert chips == CHIPS
    fine = Mesh(mesh.devices.reshape(groups, chips, CORES), ("dp", "x", "core"))
    tp = ("x", "core")

    def swap(value):
        return lax.ppermute(value, "core", [(0, 1), (1, 0)])

    def right(value):
        return lax.ppermute(value, "x", [(i, (i + 1) % chips) for i in range(chips)])

    def left(value):
        return lax.ppermute(value, "x", [((i + 1) % chips, i) for i in range(chips)])

    def gather(a, b):
        ra, rb, la, lb = right(a), right(b), left(a), left(b)
        return [a, b, ra, rb, la, lb, right(ra), left(lb)]

    def add(a, b):
        return (a.astype(F32) + b.astype(F32)).astype(BF16)

    def layers_body(hidden, lengths, w_query, w_key, w_value, w_out, w_gate, w_up, w_down, norm_attn, norm_mlp):
        core = lax.axis_index("core")
        ids = jnp.stack([lax.axis_index("x"), core]).astype(jnp.int32)
        layers = w_query.shape[0]
        _, seq, width = hidden.shape
        head = w_query.shape[-1]
        rows = seq // CHUNKS
        length = lax.dynamic_slice_in_dim(lengths, core, 1)
        cos_t, sin_t = rope_tables(seq, head)
        qkv_w = []
        for w in (w_query, w_key, w_value):
            own = w.reshape(layers, width, head)
            qkv_w += [own, swap(own)]
        ff_w = []
        for w in (w_gate, w_up, w_down):
            ff_w += [w, swap(w)]
        out_w = []
        for l in range(layers):
            own = w_out[l].reshape(head, width)
            from_left, from_right = right(own), left(own)
            far = right(from_left) if l % 2 == 0 else left(from_right)
            mine = [own, from_left, from_right, far]
            out_w.append([w for m in mine for w in (m, swap(m))])
        x = [[hidden]] * CHUNKS
        k_cache, v_cache = [], []
        h_out = None
        for l in range(layers):
            old = [[], [], [], []]
            o_all = []
            for i in range(CHUNKS):
                got = front_call(l, i, ids, length, norm_attn[l][None, :], cos_t, sin_t, x[i], qkv_w, old, rows)
                if l > 0:
                    x[i] = [got[0]]
                old = [group + [k] for group, k in zip(old, got[1:5])]
                o_all.append(gather(*got[5:7]))
            for i in range(CHUNKS):
                out = back_call(l, i, ids, norm_mlp[l][None, :], x[i][0], o_all[i], out_w[l], ff_w, rows)
                base_a, base_b, left_a, left_b, right_a, right_b, far_a, far_b = out
                got_b, got_a = right(right_b), left(left_a)
                to_right = add(right_a, right(far_a))
                to_left = add(left_b, left(far_b))
                new_a = (base_a + right(to_right).astype(F32) + got_a.astype(F32)).astype(BF16)
                new_b = (base_b + got_b.astype(F32) + left(to_left).astype(F32)).astype(BF16)
                x[i] = gather(new_a, new_b)
                if l == layers - 1:
                    h_out = place_call(i, ids, x[i] + [swap(p) for p in x[i]], h_out, hidden.shape)
            for cache, own, other in ((k_cache, old[0], old[1]), (v_cache, old[2], old[3])):
                own = jnp.concatenate(own, axis=0)
                got = swap(jnp.concatenate(other, axis=0))
                cache.append(jnp.where(core == 0, jnp.stack([own, got]), jnp.stack([got, own]))[:, None])
        return h_out, jnp.stack(k_cache), jnp.stack(v_cache)

    head_cols = P(None, None, tp, None)
    step = jax.shard_map(
        layers_body,
        mesh=fine,
        in_specs=(P("dp"), P("dp"), head_cols, head_cols, head_cols, P(None, tp, None, None), P(None, None, tp), P(None, None, tp), P(None, tp, None), P(), P()),
        out_specs=(P("dp"), P(None, "dp", tp), P(None, "dp", tp)),
        check_vma=False,
    )
    return lambda *args: step(*args)
```

time: 1130 us -> 941 us (0.83)
  Pallas kernels: 0 us -> 368 us
  waiting for transfers between devices: 685 us -> 321 us
  matrix products: 299 us -> 0 us
  starting transfers between devices: 0.25 us -> 200 us
  other arithmetic: 101 us -> 24.5 us
    psum x4 -> x0, waiting for transfers between devices: 685 us -> none  [shard_body(): summed = lax.psum(part_sum, 'tp')]
    pallas_call x0 -> x20, Pallas kernels: none -> 368 us  [the longest x8 237 us: back_call(): pl.pallas_call(functools.partial(back_kernel, chunk, x.ndim == 3), grid=(...]
    ppermute x0 -> x200, waiting for transfers between devices: none -> 321 us  [the longest x75 219 us: right(): lax.ppermute(value, 'x', [(i, (i + 1) % chips) for i in range(chips)])]
    dot_general x14 -> x0, matrix products: 257 us -> none  [the longest x2 59.9 us: mlp_partial(): jnp.einsum('bsm,mf->bsf', normed, w_gate, preferred_element_type=jnp.floa...]
    ppermute x0 -> x200, starting transfers between devices: none -> 200 us  [the longest x75 156 us: left(): lax.ppermute(value, 'x', [((i + 1) % chips, i) for i in range(chips)])]
    reduce_sum x4 -> x0, other arithmetic: 56.7 us -> none  [rms_norm(): mean_sq = jnp.mean(x_f32 * x_f32, axis=-1, keepdims=True)]
    sub x2 -> x0, matrix products: 41.9 us -> none  [attention(): attn_probs = jax.nn.softmax(scores, axis=-1).astype(jnp.bfloat16)]
    convert_element_type x1 -> x32, other arithmetic: 19.8 us -> 5.41 us  [the longest x16 2.95 us: add(): return (a.astype(F32) + b.astype(F32)).astype(BF16)]
  transfers between devices with their start and end apart: 4 -> 200, of which waited for: 4 -> 74; matrix products, arithmetic and copies ran while one was open for 1% -> 3% of each run, Pallas kernels for 0% -> 39%
where the time goes in v2:
time: 941 us; the launch traced here: 930 us
  Pallas kernels  368 us (39%)
  waiting for transfers between devices  321 us (34%)
  starting transfers between devices  200 us (21%)
  other arithmetic  24.5 us (3%)
  local copies, waits for them, and re-layouts  13.3 us (1%)
    pallas_call x8, Pallas kernels, back_call(): pl.pallas_call(functools.partial(back_kernel, chunk, x.ndim == 3), grid=(...  237 us
    ppermute x75, waiting for transfers between devices, right(): lax.ppermute(value, 'x', [(i, (i + 1) % chips) for i in range(chips)])  219 us
    ppermute x75, starting transfers between devices, left(): lax.ppermute(value, 'x', [((i + 1) % chips, i) for i in range(chips)])  156 us
    pallas_call x8, Pallas kernels, front_call(): pl.pallas_call(functools.partial(front_kernel, layer, chunk, pieces), gri...  112 us
    ppermute x75, waiting for transfers between devices, left(): lax.ppermute(value, 'x', [((i + 1) % chips, i) for i in range(chips)])  87.2 us
    ppermute x75, starting transfers between devices, right(): lax.ppermute(value, 'x', [(i, (i + 1) % chips) for i in range(chips)])  33.6 us
  transfers between devices with their start and end apart: 200, of which 74 were waited for; matrix products, arithmetic and copies ran while one was open for 3% of the time, Pallas kernels for 39%

profile of v2, /device:TPU:112, one launch (start us, length us, event | category | flops | bytes accessed | tf_op | source)
XLA Modules:
  0.0 930.2 jit_solution(10605743667525326261)
XLA Ops:
  8.5 25.0 %collective-permute-done.10.refs_10_ = bf16[256,2048]{1,0:T(8,128)(2,1)S(1)} collective-permute-done((bf16[256,2048]{1,0:T(8,128)(2,1)S(1)}, bf16[256,2048]{1,0:T(8,128)(2,1)S(1)}, u32[]{:S(2)}, u32[]{:S(2)}) %collective-permute-start.10) | collective-permute-done | bytes 1048608 | tf_op jit(solution)/shard_map/ppermute | solution.py:305
  33.6 11.6 %collective-permute-done.refs_2_.refs_9_ = bf16[2,2048,256]{2,1,0:T(8,128)(2,1)S(1)} collective-permute-done((bf16[2,2048,256]{2,1,0:T(8,128)(2,1)S(1)}, bf16[2,2048,256]{2,1,0:T(8,128)(2,1)S(1)}, u32[]{:S(2)}, u32[]{:S(2)}) %collective-permute-start) | collective-permute-done | bytes 2097184 | tf_op jit(solution)/shard_map/ppermute | solution.py:302
  53.4 4.8 fusion
  60.8 12.3 %shard_map.130 = (bf16[512,256]{1,0:T(8,128)(2,1)}, bf16[512,256]{1,0:T(8,128)(2,1)}, bf16[512,256]{1,0:T(8,128)(2,1)}, bf16[512,256]{1,0:T(8,128)(2,1)}, bf16[5...) custom-call(s32[2]{0:T(128)} %pad_add_fusion.ids_ref, s32[1]{0:T(128)} %dynamic_slice.3.len_ref, ...), custom_call_target="tpu_custom_call" | custom-call | flops 3758096384 | bytes 10485760 | tf_op jit(solution)/shard_map/pallas_call | solution.py:138
  76.1 13.4 %shard_map.131 = (bf16[512,256]{1,0:T(8,128)(2,1)}, bf16[512,256]{1,0:T(8,128)(2,1)}, bf16[512,256]{1,0:T(8,128)(2,1)}, bf16[512,256]{1,0:T(8,128)(2,1)}, bf16[5...) custom-call(s32[2]{0:T(128)} %pad_add_fusion.ids_ref, s32[1]{0:T(128)} %dynamic_slice.3.len_ref, ...), custom_call_target="tpu_custom_call" | custom-call | flops 4294967296 | bytes 10485760 | tf_op jit(solution)/shard_map/pallas_call | solution.py:138
  90.6 14.7 %shard_map.132 = (bf16[512,256]{1,0:T(8,128)(2,1)}, bf16[512,256]{1,0:T(8,128)(2,1)}, bf16[512,256]{1,0:T(8,128)(2,1)}, bf16[512,256]{1,0:T(8,128)(2,1)}, bf16[5...) custom-call(s32[2]{0:T(128)} %pad_add_fusion.ids_ref, s32[1]{0:T(128)} %dynamic_slice.3.len_ref, ...), custom_call_target="tpu_custom_call" | custom-call | flops 4831838208 | bytes 10485760 | tf_op jit(solution)/shard_map/pallas_call | solution.py:138
  105.4 15.6 %shard_map.133 = (bf16[512,256]{1,0:T(8,128)(2,1)}, bf16[512,256]{1,0:T(8,128)(2,1)}, bf16[512,256]{1,0:T(8,128)(2,1)}, bf16[512,256]{1,0:T(8,128)(2,1)}, bf16[5...) custom-call(s32[2]{0:T(128)} %pad_add_fusion.ids_ref, s32[1]{0:T(128)} %dynamic_slice.3.len_ref, ...), custom_call_target="tpu_custom_call" | custom-call | flops 5368709120 | bytes 10485760 | tf_op jit(solution)/shard_map/pallas_call | solution.py:138
  125.2 6.5 collective-permute-done.3.refs_2_
  156.2 5.6 collective-permute-done.34.refs_5_
  162.5 8.9 collective-permute-done.7.refs_6_
  172.9 5.3 collective-permute-done.8.refs_7_
  185.1 29.4 %shard_map.134 = (f32[64,2048]{1,0:T(8,128)}, f32[64,2048]{1,0:T(8,128)}, bf16[64,2048]{1,0:T(8,128)(2,1)}, bf16[64,2048]{1,0:T(8,128)(2,1)}, bf16[64,2048]{1,0:...) custom-call(s32[2]{0:T(128)} %pad_add_fusion.ids_ref, ...), custom_call_target="tpu_custom_call" | custom-call | flops 17179869184 | bytes 41943040 | tf_op jit(solution)/shard_map/pallas_call | solution.py:234
  223.1 29.7 %shard_map.135 = (f32[64,2048]{1,0:T(8,128)}, f32[64,2048]{1,0:T(8,128)}, bf16[64,2048]{1,0:T(8,128)(2,1)}, bf16[64,2048]{1,0:T(8,128)(2,1)}, bf16[64,2048]{1,0:...) custom-call(s32[2]{0:T(128)} %pad_add_fusion.ids_ref, ...), custom_call_target="tpu_custom_call" | custom-call | flops 17179869184 | bytes 41943040 | tf_op jit(solution)/shard_map/pallas_call | solution.py:234
  259.6 29.6 %shard_map.137 = (f32[64,2048]{1,0:T(8,128)}, f32[64,2048]{1,0:T(8,128)}, bf16[64,2048]{1,0:T(8,128)(2,1)}, bf16[64,2048]{1,0:T(8,128)(2,1)}, bf16[64,2048]{1,0:...) custom-call(s32[2]{0:T(128)} %pad_add_fusion.ids_ref, ...), custom_call_target="tpu_custom_call" | custom-call | flops 17179869184 | bytes 41943040 | tf_op jit(solution)/shard_map/pallas_call | solution.py:234
  296.0 30.0 %shard_map.139 = (f32[64,2048]{1,0:T(8,128)}, f32[64,2048]{1,0:T(8,128)}, bf16[64,2048]{1,0:T(8,128)(2,1)}, bf16[64,2048]{1,0:T(8,128)(2,1)}, bf16[64,2048]{1,0:...) custom-call(s32[2]{0:T(128)} %pad_add_fusion.ids_ref, ...), custom_call_target="tpu_custom_call" | custom-call | flops 17179869184 | bytes 41943040 | tf_op jit(solution)/shard_map/pallas_call | solution.py:234
  328.2 8.5 collective-permute-done.37
  337.2 6.7 collective-permute-done.41
  343.9 9.2 collective-permute-done.55
  353.6 8.6 collective-permute-done.59
  362.4 9.4 %collective-permute-done.73 = bf16[64,2048]{1,0:T(8,128)(2,1)S(1)} collective-permute-done((bf16[64,2048]{1,0:T(8,128)(2,1)S(1)}, bf16[64,2048]{1,0:T(8,128)(2,1)S(1)}, u32[]{:S(2)}, u32[]{:S(2)}) %collective-permute-start.73) | collective-permute-done | bytes 262176 | tf_op jit(solution)/shard_map/ppermute | solution.py:305
  372.2 7.0 collective-permute-done.77
  403.3 5.9 collective-permute-done.42
  413.0 6.9 collective-permute-done.56
  432.6 5.6 collective-permute-done.74
  443.9 5.5 collective-permute-done.26.refs_3_
  456.2 4.6 collective-permute-done.44.refs_3_
  484.4 12.3 %shard_map.136 = (bf16[512,2048]{1,0:T(8,128)(2,1)}, bf16[512,256]{1,0:T(8,128)(2,1)}, bf16[512,256]{1,0:T(8,128)(2,1)}, bf16[512,256]{1,0:T(8,128)(2,1)}, bf16[...) custom-call(s32[2]{0:T(128)} %pad_add_fusion.ids_ref, s32[1]{0:T(128)} %dynamic_slice.3.len_ref, ...), custom_call_target="tpu_custom_call" | custom-call | flops 3758096384 | bytes 10485760 | tf_op jit(solution)/shard_map/pallas_call | solution.py:138
  499.8 13.5 %shard_map.138 = (bf16[512,2048]{1,0:T(8,128)(2,1)}, bf16[512,256]{1,0:T(8,128)(2,1)}, bf16[512,256]{1,0:T(8,128)(2,1)}, bf16[512,256]{1,0:T(8,128)(2,1)}, bf16[...) custom-call(s32[2]{0:T(128)} %pad_add_fusion.ids_ref, s32[1]{0:T(128)} %dynamic_slice.3.len_ref, ...), custom_call_target="tpu_custom_call" | custom-call | flops 4294967296 | bytes 10485760 | tf_op jit(solution)/shard_map/pallas_call | solution.py:138
  514.1 14.6 %shard_map.140 = (bf16[512,2048]{1,0:T(8,128)(2,1)}, bf16[512,256]{1,0:T(8,128)(2,1)}, bf16[512,256]{1,0:T(8,128)(2,1)}, bf16[512,256]{1,0:T(8,128)(2,1)}, bf16[...) custom-call(s32[2]{0:T(128)} %pad_add_fusion.ids_ref, s32[1]{0:T(128)} %dynamic_slice.3.len_ref, ...), custom_call_target="tpu_custom_call" | custom-call | flops 4831838208 | bytes 10485760 | tf_op jit(solution)/shard_map/pallas_call | solution.py:138
  529.4 16.1 %shard_map.141 = (bf16[512,2048]{1,0:T(8,128)(2,1)}, bf16[512,256]{1,0:T(8,128)(2,1)}, bf16[512,256]{1,0:T(8,128)(2,1)}, bf16[512,256]{1,0:T(8,128)(2,1)}, bf16[...) custom-call(s32[2]{0:T(128)} %pad_add_fusion.ids_ref, s32[1]{0:T(128)} %dynamic_slice.3.len_ref, ...), custom_call_target="tpu_custom_call" | custom-call | flops 5368709120 | bytes 10485760 | tf_op jit(solution)/shard_map/pallas_call | solution.py:138
  556.7 5.2 collective-permute-done.86.refs_3_
  582.0 29.8 %shard_map.142 = (f32[64,2048]{1,0:T(8,128)}, f32[64,2048]{1,0:T(8,128)}, bf16[64,2048]{1,0:T(8,128)(2,1)}, bf16[64,2048]{1,0:T(8,128)(2,1)}, bf16[64,2048]{1,0:...) custom-call(s32[2]{0:T(128)} %pad_add_fusion.ids_ref, ...), custom_call_target="tpu_custom_call" | custom-call | flops 17179869184 | bytes 41943040 | tf_op jit(solution)/shard_map/pallas_call | solution.py:234
  619.0 29.5 %shard_map.143 = (f32[64,2048]{1,0:T(8,128)}, f32[64,2048]{1,0:T(8,128)}, bf16[64,2048]{1,0:T(8,128)(2,1)}, bf16[64,2048]{1,0:T(8,128)(2,1)}, bf16[64,2048]{1,0:...) custom-call(s32[2]{0:T(128)} %pad_add_fusion.ids_ref, ...), custom_call_target="tpu_custom_call" | custom-call | flops 17179869184 | bytes 41943040 | tf_op jit(solution)/shard_map/pallas_call | solution.py:234
  655.1 29.5 %shard_map.144 = (f32[64,2048]{1,0:T(8,128)}, f32[64,2048]{1,0:T(8,128)}, bf16[64,2048]{1,0:T(8,128)(2,1)}, bf16[64,2048]{1,0:T(8,128)(2,1)}, bf16[64,2048]{1,0:...) custom-call(s32[2]{0:T(128)} %pad_add_fusion.ids_ref, ...), custom_call_target="tpu_custom_call" | custom-call | flops 17179869184 | bytes 41943040 | tf_op jit(solution)/shard_map/pallas_call | solution.py:234
  687.3 29.9 %shard_map.145 = (f32[64,2048]{1,0:T(8,128)}, f32[64,2048]{1,0:T(8,128)}, bf16[64,2048]{1,0:T(8,128)(2,1)}, bf16[64,2048]{1,0:T(8,128)(2,1)}, bf16[64,2048]{1,0:...) custom-call(s32[2]{0:T(128)} %pad_add_fusion.ids_ref, ...), custom_call_target="tpu_custom_call" | custom-call | flops 17179869184 | bytes 41943040 | tf_op jit(solution)/shard_map/pallas_call | solution.py:234
  719.7 5.6 collective-permute-done.102
  725.7 8.1 collective-permute-done.124
  735.6 4.7 collective-permute-done.128
  740.5 7.5 collective-permute-done.150
  749.8 4.5 collective-permute-done.154
  754.4 7.5 collective-permute-done.176
  763.8 4.5 collective-permute-done.180
  769.6 7.9 collective-permute-done.99
  877.5 5.5 collective-permute-done.134.refs_6_
  908.3 4.7 shard_map.146.refs_16_
  914.7 4.5 shard_map.147.refs_16_
  919.2 4.5 shard_map.148.refs_16_
  925.5 4.5 shard_map.149
  (899 shorter events, 351.3 us)
Async XLA Ops:
  3.6 178.2 %collective-permute-start.16 = (bf16[2,2048,1024]{2,1,0:T(8,128)(2,1)}, bf16[2,2048,1024]{2,1,0:T(8,128)(2,1)}, u32[]{:S(2)}, u32[]{:S(2)}) collective-permute-start(bf16[2,2048,1024]{2,1,0:T(8,128)(2,1)} %refs_16_.15), channel_id=1, source_target_pairs={{0,1},{1,0},{2,3},{3,2},{4,5},{5,4},{6,7},{7,6},{8,9},{9,8},{10,11... | collective-permute-start | bytes 25165832 | tf_op jit(solution)/shard_map/ppermute | solution.py:302
  4.0 177.7 %collective-permute-start.17 = (bf16[2,2048,1024]{2,1,0:T(8,128)(2,1)}, bf16[2,2048,1024]{2,1,0:T(8,128)(2,1)}, u32[]{:S(2)}, u32[]{:S(2)}) collective-permute-start(bf16[2,2048,1024]{2,1,0:T(8,128)(2,1)} %refs_18_.15), channel_id=1, source_target_pairs={{0,1},{1,0},{2,3},{3,2},{4,5},{5,4},{6,7},{7,6},{8,9},{9,8},{10,11... | collective-permute-start | bytes 25165832 | tf_op jit(solution)/shard_map/ppermute | solution.py:302
  4.1 177.8 %collective-permute-start.18 = (bf16[2,1024,2048]{2,1,0:T(8,128)(2,1)}, bf16[2,1024,2048]{2,1,0:T(8,128)(2,1)}, u32[]{:S(2)}, u32[]{:S(2)}) collective-permute-start(bf16[2,1024,2048]{2,1,0:T(8,128)(2,1)} %refs_20_.15), channel_id=1, source_target_pairs={{0,1},{1,0},{2,3},{3,2},{4,5},{5,4},{6,7},{7,6},{8,9},{9,8},{10,11... | collective-permute-start | bytes 25165832 | tf_op jit(solution)/shard_map/ppermute | solution.py:302
  4.6 40.6 %collective-permute-start = (bf16[2,2048,256]{2,1,0:T(8,128)(2,1)S(1)}, bf16[2,2048,256]{2,1,0:T(8,128)(2,1)S(1)}, u32[]{:S(2)}, u32[]{:S(2)}) collective-permute-start(bf16[2,2048,256]{2,1,0:T(8,128)(2,1)S(1)} %bitcast.29), channel_id=1, source_target_pairs={{0,1},{1,0},{2,3},{3,2},{4,5},{5,4},{6,7},{7,6},{8,9},{9,8},{10,11... | collective-permute-start | bytes 6291464 | tf_op jit(solution)/shard_map/ppermute | solution.py:302
  76.1 44.8 %collective-permute-start.13 = (bf16[256,2048]{1,0:T(8,128)(2,1)}, bf16[256,2048]{1,0:T(8,128)(2,1)S(1)}, u32[]{:S(2)}, u32[]{:S(2)}) collective-permute-start(bf16[256,2048]{1,0:T(8,128)(2,1)} %collective-permute-done.12.refs_12_), channel_id=1, source_target_pairs={{0,1},{1,0},{2,3},{3,2},{4,5},{5,4},{6,7},{7,6},{8,9},{9,8},{10,11... | collective-permute-start | bytes 3145736 | tf_op jit(solution)/shard_map/ppermute | solution.py:302
  89.5 33.2 %collective-permute-start.14 = (bf16[256,2048]{1,0:T(8,128)(2,1)S(1)}, bf16[256,2048]{1,0:T(8,128)(2,1)S(1)}, u32[]{:S(2)}, u32[]{:S(2)}) collective-permute-start(bf16[256,2048]{1,0:T(8,128)(2,1)S(1)} %copy-done.8), channel_id=1, source_target_pairs={{0,2},{2,4},{4,6},{6,0},{1,3},{3,5},{5,7},{7,1},{8,10},{10,12},{12... | collective-permute-start | bytes 3145736 | tf_op jit(solution)/shard_map/ppermute | solution.py:305
  178.4 38.1 %collective-permute-start.50 = (bf16[512,256]{1,0:T(8,128)(2,1)S(1)}, bf16[512,256]{1,0:T(8,128)(2,1)}, u32[]{:S(2)}, u32[]{:S(2)}) collective-permute-start(bf16[512,256]{1,0:T(8,128)(2,1)S(1)} %copy-done.101), channel_id=1, source_target_pairs={{0,2},{2,4},{4,6},{6,0},{1,3},{3,5},{5,7},{7,1},{8,10},{10,12},{12... | collective-permute-start | bytes 786440 | tf_op jit(solution)/shard_map/ppermute | solution.py:305
  178.6 38.1 %collective-permute-start.52 = (bf16[512,256]{1,0:T(8,128)(2,1)S(1)}, bf16[512,256]{1,0:T(8,128)(2,1)}, u32[]{:S(2)}, u32[]{:S(2)}) collective-permute-start(bf16[512,256]{1,0:T(8,128)(2,1)S(1)} %copy-done.101), channel_id=1, source_target_pairs={{2,0},{4,2},{6,4},{0,6},{3,1},{5,3},{7,5},{1,7},{10,8},{12,10},{14... | collective-permute-start | bytes 786440 | tf_op jit(solution)/shard_map/ppermute | solution.py:308
  181.8 38.1 %collective-permute-start.35 = (bf16[512,256]{1,0:T(8,128)(2,1)}, bf16[512,256]{1,0:T(8,128)(2,1)}, u32[]{:S(2)}, u32[]{:S(2)}) collective-permute-start(bf16[512,256]{1,0:T(8,128)(2,1)} %copy-done.126), channel_id=1, source_target_pairs={{0,2},{2,4},{4,6},{6,0},{1,3},{3,5},{5,7},{7,1},{8,10},{10,12},{12... | collective-permute-start | bytes 786440 | tf_op jit(solution)/shard_map/ppermute | solution.py:305
  181.9 38.0 %collective-permute-start.36 = (bf16[512,256]{1,0:T(8,128)(2,1)}, bf16[512,256]{1,0:T(8,128)(2,1)}, u32[]{:S(2)}, u32[]{:S(2)}) collective-permute-start(bf16[512,256]{1,0:T(8,128)(2,1)} %copy-done.135), channel_id=1, source_target_pairs={{2,0},{4,2},{6,4},{0,6},{3,1},{5,3},{7,5},{1,7},{10,8},{12,10},{14... | collective-permute-start | bytes 786440 | tf_op jit(solution)/shard_map/ppermute | solution.py:308
  214.5 38.4 %collective-permute-start.51 = (bf16[512,256]{1,0:T(8,128)(2,1)}, bf16[512,256]{1,0:T(8,128)(2,1)S(1)}, u32[]{:S(2)}, u32[]{:S(2)}) collective-permute-start(bf16[512,256]{1,0:T(8,128)(2,1)} %get-tuple-element.152.refs_0_), channel_id=1, source_target_pairs={{2,0},{4,2},{6,4},{0,6},{3,1},{5,3},{7,5},{1,7},{10,8},{12,10},{14... | collective-permute-start | bytes 786440 | tf_op jit(solution)/shard_map/ppermute | solution.py:308
  216.6 36.5 %collective-permute-start.67 = (bf16[512,256]{1,0:T(8,128)(2,1)S(1)}, bf16[512,256]{1,0:T(8,128)(2,1)S(1)}, u32[]{:S(2)}, u32[]{:S(2)}) collective-permute-start(bf16[512,256]{1,0:T(8,128)(2,1)S(1)} %copy-done.95), channel_id=1, source_target_pairs={{0,2},{2,4},{4,6},{6,0},{1,3},{3,5},{5,7},{7,1},{8,10},{10,12},{12... | collective-permute-start | bytes 786440 | tf_op jit(solution)/shard_map/ppermute | solution.py:305
  216.6 38.4 %collective-permute-start.70 = (bf16[512,256]{1,0:T(8,128)(2,1)S(1)}, bf16[512,256]{1,0:T(8,128)(2,1)S(1)}, u32[]{:S(2)}, u32[]{:S(2)}) collective-permute-start(bf16[512,256]{1,0:T(8,128)(2,1)S(1)} %copy-done.96), channel_id=1, source_target_pairs={{2,0},{4,2},{6,4},{0,6},{3,1},{5,3},{7,5},{1,7},{10,8},{12,10},{14... | collective-permute-start | bytes 786440 | tf_op jit(solution)/shard_map/ppermute | solution.py:308
  219.9 36.5 %collective-permute-start.53 = (bf16[512,256]{1,0:T(8,128)(2,1)}, bf16[512,256]{1,0:T(8,128)(2,1)S(1)}, u32[]{:S(2)}, u32[]{:S(2)}) collective-permute-start(bf16[512,256]{1,0:T(8,128)(2,1)} %collective-permute-done.49.refs_2_), channel_id=1, source_target_pairs={{0,2},{2,4},{4,6},{6,0},{1,3},{3,5},{5,7},{7,1},{8,10},{10,12},{12... | collective-permute-start | bytes 786440 | tf_op jit(solution)/shard_map/ppermute | solution.py:305
  219.9 37.2 %collective-permute-start.54 = (bf16[512,256]{1,0:T(8,128)(2,1)}, bf16[512,256]{1,0:T(8,128)(2,1)S(1)}, u32[]{:S(2)}, u32[]{:S(2)}) collective-permute-start(bf16[512,256]{1,0:T(8,128)(2,1)} %collective-permute-done.52.refs_5_), channel_id=1, source_target_pairs={{2,0},{4,2},{6,4},{0,6},{3,1},{5,3},{7,5},{1,7},{10,8},{12,10},{14... | collective-permute-start | bytes 786440 | tf_op jit(solution)/shard_map/ppermute | solution.py:308
  252.9 36.3 %collective-permute-start.94 = (bf16[256,2048]{1,0:T(8,128)(2,1)S(1)}, bf16[256,2048]{1,0:T(8,128)(2,1)}, u32[]{:S(2)}, u32[]{:S(2)}) collective-permute-start(bf16[256,2048]{1,0:T(8,128)(2,1)S(1)} %copy-done.55), channel_id=1, source_target_pairs={{2,0},{4,2},{6,4},{0,6},{3,1},{5,3},{7,5},{1,7},{10,8},{12,10},{14... | collective-permute-start | bytes 3145736 | tf_op jit(solution)/shard_map/ppermute | solution.py:308
  253.0 36.3 %collective-permute-start.68 = (bf16[512,256]{1,0:T(8,128)(2,1)S(1)}, bf16[512,256]{1,0:T(8,128)(2,1)S(1)}, u32[]{:S(2)}, u32[]{:S(2)}) collective-permute-start(bf16[512,256]{1,0:T(8,128)(2,1)S(1)} %copy-done.96), channel_id=1, source_target_pairs={{0,2},{2,4},{4,6},{6,0},{1,3},{3,5},{5,7},{7,1},{8,10},{10,12},{12... | collective-permute-start | bytes 786440 | tf_op jit(solution)/shard_map/ppermute | solution.py:305
  255.0 37.5 %collective-permute-start.69 = (bf16[512,256]{1,0:T(8,128)(2,1)S(1)}, bf16[512,256]{1,0:T(8,128)(2,1)S(1)}, u32[]{:S(2)}, u32[]{:S(2)}) collective-permute-start(bf16[512,256]{1,0:T(8,128)(2,1)S(1)} %copy-done.95), channel_id=1, source_target_pairs={{2,0},{4,2},{6,4},{0,6},{3,1},{5,3},{7,5},{1,7},{10,8},{12,10},{14... | collective-permute-start | bytes 786440 | tf_op jit(solution)/shard_map/ppermute | solution.py:308
  256.4 36.3 %collective-permute-start.71 = (bf16[512,256]{1,0:T(8,128)(2,1)S(1)}, bf16[512,256]{1,0:T(8,128)(2,1)S(1)}, u32[]{:S(2)}, u32[]{:S(2)}) collective-permute-start(bf16[512,256]{1,0:T(8,128)(2,1)S(1)} %collective-permute-done.67.refs_2_), channel_id=1, source_target_pairs={{0,2},{2,4},{4,6},{6,0},{1,3},{3,5},{5,7},{7,1},{8,10},{10,12},{12... | collective-permute-start | bytes 786440 | tf_op jit(solution)/shard_map/ppermute | solution.py:305
  257.1 37.5 %collective-permute-start.72 = (bf16[512,256]{1,0:T(8,128)(2,1)S(1)}, bf16[512,256]{1,0:T(8,128)(2,1)S(1)}, u32[]{:S(2)}, u32[]{:S(2)}) collective-permute-start(bf16[512,256]{1,0:T(8,128)(2,1)S(1)} %collective-permute-done.70.refs_5_), channel_id=1, source_target_pairs={{2,0},{4,2},{6,4},{0,6},{3,1},{5,3},{7,5},{1,7},{10,8},{12,10},{14... | collective-permute-start | bytes 786440 | tf_op jit(solution)/shard_map/ppermute | solution.py:308
  289.2 132.9 %collective-permute-start.92 = (bf16[256,2048]{1,0:T(8,128)(2,1)S(1)}, bf16[256,2048]{1,0:T(8,128)(2,1)}, u32[]{:S(2)}, u32[]{:S(2)}) collective-permute-start(bf16[256,2048]{1,0:T(8,128)(2,1)S(1)} %copy-done.55), channel_id=1, source_target_pairs={{0,2},{2,4},{4,6},{6,0},{1,3},{3,5},{5,7},{7,1},{8,10},{10,12},{12... | collective-permute-start | bytes 3145736 | tf_op jit(solution)/shard_map/ppermute | solution.py:305
  289.4 132.9 %collective-permute-start.96 = (bf16[256,2048]{1,0:T(8,128)(2,1)}, bf16[256,2048]{1,0:T(8,128)(2,1)}, u32[]{:S(2)}, u32[]{:S(2)}) collective-permute-start(bf16[256,2048]{1,0:T(8,128)(2,1)} %collective-permute-done.94.refs_12_), channel_id=1, source_target_pairs={{2,0},{4,2},{6,4},{0,6},{3,1},{5,3},{7,5},{1,7},{10,8},{12,10},{14... | collective-permute-start | bytes 3145736 | tf_op jit(solution)/shard_map/ppermute | solution.py:308
  292.6 86.8 %collective-permute-start.21 = (bf16[64,2048]{1,0:T(8,128)(2,1)}, bf16[64,2048]{1,0:T(8,128)(2,1)S(1)}, u32[]{:S(2)}, u32[]{:S(2)}) collective-permute-start(bf16[64,2048]{1,0:T(8,128)(2,1)} %get-tuple-element.136), channel_id=1, source_target_pairs={{2,0},{4,2},{6,4},{0,6},{3,1},{5,3},{7,5},{1,7},{10,8},{12,10},{14... | collective-permute-start | bytes 786440 | tf_op jit(solution)/shard_map/ppermute | solution.py:308
  292.7 33.4 %collective-permute-start.19 = (bf16[64,2048]{1,0:T(8,128)(2,1)}, bf16[64,2048]{1,0:T(8,128)(2,1)}, u32[]{:S(2)}, u32[]{:S(2)}) collective-permute-start(bf16[64,2048]{1,0:T(8,128)(2,1)} %get-tuple-element.135), channel_id=1, source_target_pairs={{0,2},{2,4},{4,6},{6,0},{1,3},{3,5},{5,7},{7,1},{8,10},{10,12},{12... | collective-permute-start | bytes 786440 | tf_op jit(solution)/shard_map/ppermute | solution.py:305
  294.6 33.3 %collective-permute-start.23 = (bf16[64,2048]{1,0:T(8,128)(2,1)}, bf16[64,2048]{1,0:T(8,128)(2,1)S(1)}, u32[]{:S(2)}, u32[]{:S(2)}) collective-permute-start(bf16[64,2048]{1,0:T(8,128)(2,1)} %get-tuple-element.140), channel_id=1, source_target_pairs={{2,0},{4,2},{6,4},{0,6},{3,1},{5,3},{7,5},{1,7},{10,8},{12,10},{14... | collective-permute-start | bytes 786440 | tf_op jit(solution)/shard_map/ppermute | solution.py:308
  326.1 61.4 %collective-permute-start.22 = (bf16[64,2048]{1,0:T(8,128)(2,1)}, bf16[64,2048]{1,0:T(8,128)(2,1)S(1)}, u32[]{:S(2)}, u32[]{:S(2)}) collective-permute-start(bf16[64,2048]{1,0:T(8,128)(2,1)} %get-tuple-element.138), channel_id=1, source_target_pairs={{0,2},{2,4},{4,6},{6,0},{1,3},{3,5},{5,7},{7,1},{8,10},{10,12},{12... | collective-permute-start | bytes 786440 | tf_op jit(solution)/shard_map/ppermute | solution.py:305
  496.8 50.2 %collective-permute-start.91 = (bf16[256,2048]{1,0:T(8,128)(2,1)S(1)}, bf16[256,2048]{1,0:T(8,128)(2,1)}, u32[]{:S(2)}, u32[]{:S(2)}) collective-permute-start(bf16[256,2048]{1,0:T(8,128)(2,1)S(1)} %copy-done.55), channel_id=1, source_target_pairs={{0,1},{1,0},{2,3},{3,2},{4,5},{5,4},{6,7},{7,6},{8,9},{9,8},{10,11... | collective-permute-start | bytes 3145736 | tf_op jit(solution)/shard_map/ppermute | solution.py:302
  496.9 52.1 %collective-permute-start.95 = (bf16[256,2048]{1,0:T(8,128)(2,1)}, bf16[256,2048]{1,0:T(8,128)(2,1)}, u32[]{:S(2)}, u32[]{:S(2)}) collective-permute-start(bf16[256,2048]{1,0:T(8,128)(2,1)} %collective-permute-done.94.refs_12_), channel_id=1, source_target_pairs={{0,1},{1,0},{2,3},{3,2},{4,5},{5,4},{6,7},{7,6},{8,9},{9,8},{10,11... | collective-permute-start | bytes 3145736 | tf_op jit(solution)/shard_map/ppermute | solution.py:302
  497.4 51.5 %collective-permute-start.93 = (bf16[256,2048]{1,0:T(8,128)(2,1)}, bf16[256,2048]{1,0:T(8,128)(2,1)}, u32[]{:S(2)}, u32[]{:S(2)}) collective-permute-start(bf16[256,2048]{1,0:T(8,128)(2,1)} %collective-permute-done.92.refs_10_), channel_id=1, source_target_pairs={{0,1},{1,0},{2,3},{3,2},{4,5},{5,4},{6,7},{7,6},{8,9},{9,8},{10,11... | collective-permute-start | bytes 3145736 | tf_op jit(solution)/shard_map/ppermute | solution.py:302
  497.5 54.6 %collective-permute-start.97 = (bf16[256,2048]{1,0:T(8,128)(2,1)}, bf16[256,2048]{1,0:T(8,128)(2,1)}, u32[]{:S(2)}, u32[]{:S(2)}) collective-permute-start(bf16[256,2048]{1,0:T(8,128)(2,1)} %collective-permute-done.96.refs_14_), channel_id=1, source_target_pairs={{0,1},{1,0},{2,3},{3,2},{4,5},{5,4},{6,7},{7,6},{8,9},{9,8},{10,11... | collective-permute-start | bytes 3145736 | tf_op jit(solution)/shard_map/ppermute | solution.py:302
  573.1 39.4 %collective-permute-start.145 = (bf16[512,256]{1,0:T(8,128)(2,1)S(1)}, bf16[512,256]{1,0:T(8,128)(2,1)}, u32[]{:S(2)}, u32[]{:S(2)}) collective-permute-start(bf16[512,256]{1,0:T(8,128)(2,1)S(1)} %copy-done.200), channel_id=1, source_target_pairs={{0,2},{2,4},{4,6},{6,0},{1,3},{3,5},{5,7},{7,1},{8,10},{10,12},{12... | collective-permute-start | bytes 786440 | tf_op jit(solution)/shard_map/ppermute | solution.py:305
  573.2 40.7 %collective-permute-start.147 = (bf16[512,256]{1,0:T(8,128)(2,1)S(1)}, bf16[512,256]{1,0:T(8,128)(2,1)}, u32[]{:S(2)}, u32[]{:S(2)}) collective-permute-start(bf16[512,256]{1,0:T(8,128)(2,1)S(1)} %copy-done.200), channel_id=1, source_target_pairs={{2,0},{4,2},{6,4},{0,6},{3,1},{5,3},{7,5},{1,7},{10,8},{12,10},{14... | collective-permute-start | bytes 786440 | tf_op jit(solution)/shard_map/ppermute | solution.py:308
  576.4 35.4 %collective-permute-start.144 = (bf16[512,256]{1,0:T(8,128)(2,1)S(1)}, bf16[512,256]{1,0:T(8,128)(2,1)}, u32[]{:S(2)}, u32[]{:S(2)}) collective-permute-start(bf16[512,256]{1,0:T(8,128)(2,1)S(1)} %copy-done.199), channel_id=1, source_target_pairs={{0,2},{2,4},{4,6},{6,0},{1,3},{3,5},{5,7},{7,1},{8,10},{10,12},{12... | collective-permute-start | bytes 786440 | tf_op jit(solution)/shard_map/ppermute | solution.py:305
  578.7 37.0 %collective-permute-start.122 = (bf16[512,256]{1,0:T(8,128)(2,1)S(1)}, bf16[512,256]{1,0:T(8,128)(2,1)S(1)}, u32[]{:S(2)}, u32[]{:S(2)}) collective-permute-start(bf16[512,256]{1,0:T(8,128)(2,1)S(1)} %collective-permute-done.118.refs_2_), channel_id=1, source_target_pairs={{0,2},{2,4},{4,6},{6,0},{1,3},{3,5},{5,7},{7,1},{8,10},{10,12},{12... | collective-permute-start | bytes 786440 | tf_op jit(solution)/shard_map/ppermute | solution.py:305
  578.9 37.1 %collective-permute-start.123 = (bf16[512,256]{1,0:T(8,128)(2,1)}, bf16[512,256]{1,0:T(8,128)(2,1)S(1)}, u32[]{:S(2)}, u32[]{:S(2)}) collective-permute-start(bf16[512,256]{1,0:T(8,128)(2,1)} %collective-permute-done.121.refs_5_), channel_id=1, source_target_pairs={{2,0},{4,2},{6,4},{0,6},{3,1},{5,3},{7,5},{1,7},{10,8},{12,10},{14... | collective-permute-start | bytes 786440 | tf_op jit(solution)/shard_map/ppermute | solution.py:308
  611.8 36.7 %collective-permute-start.146 = (bf16[512,256]{1,0:T(8,128)(2,1)S(1)}, bf16[512,256]{1,0:T(8,128)(2,1)}, u32[]{:S(2)}, u32[]{:S(2)}) collective-permute-start(bf16[512,256]{1,0:T(8,128)(2,1)S(1)} %copy-done.199), channel_id=1, source_target_pairs={{2,0},{4,2},{6,4},{0,6},{3,1},{5,3},{7,5},{1,7},{10,8},{12,10},{14... | collective-permute-start | bytes 786440 | tf_op jit(solution)/shard_map/ppermute | solution.py:308
  612.5 36.1 %collective-permute-start.170 = (bf16[512,256]{1,0:T(8,128)(2,1)S(1)}, bf16[512,256]{1,0:T(8,128)(2,1)}, u32[]{:S(2)}, u32[]{:S(2)}) collective-permute-start(bf16[512,256]{1,0:T(8,128)(2,1)S(1)} %copy-done.197), channel_id=1, source_target_pairs={{0,2},{2,4},{4,6},{6,0},{1,3},{3,5},{5,7},{7,1},{8,10},{10,12},{12... | collective-permute-start | bytes 786440 | tf_op jit(solution)/shard_map/ppermute | solution.py:305
  613.9 34.8 %collective-permute-start.173 = (bf16[512,256]{1,0:T(8,128)(2,1)S(1)}, bf16[512,256]{1,0:T(8,128)(2,1)}, u32[]{:S(2)}, u32[]{:S(2)}) collective-permute-start(bf16[512,256]{1,0:T(8,128)(2,1)S(1)} %copy-done.198), channel_id=1, source_target_pairs={{2,0},{4,2},{6,4},{0,6},{3,1},{5,3},{7,5},{1,7},{10,8},{12,10},{14... | collective-permute-start | bytes 786440 | tf_op jit(solution)/shard_map/ppermute | solution.py:308
  615.7 36.2 %collective-permute-start.148 = (bf16[512,256]{1,0:T(8,128)(2,1)}, bf16[512,256]{1,0:T(8,128)(2,1)}, u32[]{:S(2)}, u32[]{:S(2)}) collective-permute-start(bf16[512,256]{1,0:T(8,128)(2,1)} %collective-permute-done.144.refs_2_), channel_id=1, source_target_pairs={{0,2},{2,4},{4,6},{6,0},{1,3},{3,5},{5,7},{7,1},{8,10},{10,12},{12... | collective-permute-start | bytes 786440 | tf_op jit(solution)/shard_map/ppermute | solution.py:305
  615.9 36.0 %collective-permute-start.149 = (bf16[512,256]{1,0:T(8,128)(2,1)}, bf16[512,256]{1,0:T(8,128)(2,1)}, u32[]{:S(2)}, u32[]{:S(2)}) collective-permute-start(bf16[512,256]{1,0:T(8,128)(2,1)} %collective-permute-done.147.refs_5_), channel_id=1, source_target_pairs={{2,0},{4,2},{6,4},{0,6},{3,1},{5,3},{7,5},{1,7},{10,8},{12,10},{14... | collective-permute-start | bytes 786440 | tf_op jit(solution)/shard_map/ppermute | solution.py:308
  648.5 133.0 %collective-permute-start.196 = (bf16[2048,256]{1,0:T(8,128)(2,1)}, bf16[2048,256]{1,0:T(8,128)(2,1)S(1)}, u32[]{:S(2)}, u32[]{:S(2)}) collective-permute-start(bf16[2048,256]{1,0:T(8,128)(2,1)} %pad_maximum_fusion.2), channel_id=1, source_target_pairs={{0,1},{1,0},{2,3},{3,2},{4,5},{5,4},{6,7},{7,6},{8,9},{9,8},{10,11... | collective-permute-start | bytes 3145736 | tf_op jit(solution)/shard_map/ppermute | solution.py:302
  648.6 36.1 %collective-permute-start.171 = (bf16[512,256]{1,0:T(8,128)(2,1)S(1)}, bf16[512,256]{1,0:T(8,128)(2,1)S(1)}, u32[]{:S(2)}, u32[]{:S(2)}) collective-permute-start(bf16[512,256]{1,0:T(8,128)(2,1)S(1)} %copy-done.198), channel_id=1, source_target_pairs={{0,2},{2,4},{4,6},{6,0},{1,3},{3,5},{5,7},{7,1},{8,10},{10,12},{12... | collective-permute-start | bytes 786440 | tf_op jit(solution)/shard_map/ppermute | solution.py:305
  648.7 36.1 %collective-permute-start.172 = (bf16[512,256]{1,0:T(8,128)(2,1)S(1)}, bf16[512,256]{1,0:T(8,128)(2,1)}, u32[]{:S(2)}, u32[]{:S(2)}) collective-permute-start(bf16[512,256]{1,0:T(8,128)(2,1)S(1)} %copy-done.197), channel_id=1, source_target_pairs={{2,0},{4,2},{6,4},{0,6},{3,1},{5,3},{7,5},{1,7},{10,8},{12,10},{14... | collective-permute-start | bytes 786440 | tf_op jit(solution)/shard_map/ppermute | solution.py:308
  651.9 33.4 %collective-permute-start.174 = (bf16[512,256]{1,0:T(8,128)(2,1)}, bf16[512,256]{1,0:T(8,128)(2,1)}, u32[]{:S(2)}, u32[]{:S(2)}) collective-permute-start(bf16[512,256]{1,0:T(8,128)(2,1)} %collective-permute-done.170.refs_2_), channel_id=1, source_target_pairs={{0,2},{2,4},{4,6},{6,0},{1,3},{3,5},{5,7},{7,1},{8,10},{10,12},{12... | collective-permute-start | bytes 786440 | tf_op jit(solution)/shard_map/ppermute | solution.py:305
  651.9 33.4 %collective-permute-start.175 = (bf16[512,256]{1,0:T(8,128)(2,1)}, bf16[512,256]{1,0:T(8,128)(2,1)}, u32[]{:S(2)}, u32[]{:S(2)}) collective-permute-start(bf16[512,256]{1,0:T(8,128)(2,1)} %collective-permute-done.173.refs_5_), channel_id=1, source_target_pairs={{2,0},{4,2},{6,4},{0,6},{3,1},{5,3},{7,5},{1,7},{10,8},{12,10},{14... | collective-permute-start | bytes 786440 | tf_op jit(solution)/shard_map/ppermute | solution.py:308
  684.7 100.1 %collective-permute-start.198 = (bf16[2048,256]{1,0:T(8,128)(2,1)}, bf16[2048,256]{1,0:T(8,128)(2,1)}, u32[]{:S(2)}, u32[]{:S(2)}) collective-permute-start(bf16[2048,256]{1,0:T(8,128)(2,1)} %pad_maximum_fusion.4), channel_id=1, source_target_pairs={{0,1},{1,0},{2,3},{3,2},{4,5},{5,4},{6,7},{7,6},{8,9},{9,8},{10,11... | collective-permute-start | bytes 3145736 | tf_op jit(solution)/shard_map/ppermute | solution.py:302
  684.8 124.7 %collective-permute-start.197 = (bf16[2048,256]{1,0:T(8,128)(2,1)}, bf16[2048,256]{1,0:T(8,128)(2,1)}, u32[]{:S(2)}, u32[]{:S(2)}) collective-permute-start(bf16[2048,256]{1,0:T(8,128)(2,1)} %pad_maximum_fusion.3), channel_id=1, source_target_pairs={{0,1},{1,0},{2,3},{3,2},{4,5},{5,4},{6,7},{7,6},{8,9},{9,8},{10,11... | collective-permute-start | bytes 3145736 | tf_op jit(solution)/shard_map/ppermute | solution.py:302
  685.3 83.1 %collective-permute-start.100 = (bf16[64,2048]{1,0:T(8,128)(2,1)}, bf16[64,2048]{1,0:T(8,128)(2,1)}, u32[]{:S(2)}, u32[]{:S(2)}) collective-permute-start(bf16[64,2048]{1,0:T(8,128)(2,1)} %get-tuple-element.189), channel_id=1, source_target_pairs={{2,0},{4,2},{6,4},{0,6},{3,1},{5,3},{7,5},{1,7},{10,8},{12,10},{14... | collective-permute-start | bytes 786440 | tf_op jit(solution)/shard_map/ppermute | solution.py:308
  (389 other events, 7051.2 us)

commit v3 on v2

v3 whole, which is shorter than its diff:
```python
import functools

import jax
import jax.numpy as jnp
from jax import lax
from jax.experimental import pallas as pl
from jax.experimental.pallas import tpu as pltpu
from jax.sharding import Mesh
from jax.sharding import PartitionSpec as P


RMS_EPS = 1e-6
ROPE_BASE = 10000.0
CORES = 2
CHIPS = 4
CHUNKS = 4
ROW_TILE = 256
FF_TILE = 256
VMEM = 60 * 1024 * 1024
BF16 = jnp.bfloat16
F32 = jnp.float32
ANY = pl.BlockSpec(memory_space=pl.ANY)
SMEM = pl.BlockSpec(memory_space=pltpu.SMEM)
OFFSETS = (0, 3, 1, 2)
MESH = pl.DeviceIdType.MESH


def cost(flops, nbytes, exps=0):
    return pl.CostEstimate(flops=int(flops), bytes_accessed=int(nbytes), transcendentals=int(exps))


def norm_rows(x_f32, gain):
    mean_sq = jnp.mean(x_f32 * x_f32, axis=-1, keepdims=True)
    return (x_f32 * lax.rsqrt(mean_sq + RMS_EPS) * (1.0 + gain)).astype(BF16)


def struct(shape, dtype=BF16):
    return jax.ShapeDtypeStruct(shape, dtype)


def whole(shape):
    return pl.BlockSpec(shape, lambda *_: (0,) * len(shape))


def piece_rows(place, part):
    return pl.multiple_of(lax.rem(lax.axis_index("x") + OFFSETS[place], CHIPS) * part, part)


def to_right():
    return {"x": lax.rem(lax.axis_index("x") + 1, CHIPS)}


def to_left():
    return {"x": lax.rem(lax.axis_index("x") + CHIPS - 1, CHIPS)}


def to_partner():
    return {"core": 1 - lax.axis_index("core")}


def remote(src, dst, send, recv, device):
    return pltpu.make_async_remote_copy(src_ref=src, dst_ref=dst, send_sem=send, recv_sem=recv, device_id=device, device_id_type=MESH)


class Gather:
    def __init__(self, block):
        self.inputs = [block]
        shape = struct(block.shape, block.dtype)
        self.out_shapes, self.out_specs = [shape] * 3, [ANY] * 3
        self.scratch = [pltpu.SemaphoreType.DMA((4,)), pltpu.SemaphoreType.DMA((4,))]

    def bind(self, inputs, outputs, scratch):
        own, (r, l, f), (send, recv) = inputs[0], outputs, scratch
        half = own.shape[0] // 2
        top, low = pl.ds(0, half), pl.ds(half, half)
        first = lambda: (remote(own, r, send.at[0], recv.at[0], to_right()), remote(own, l, send.at[1], recv.at[1], to_left()))
        second = lambda: (
            remote(r.at[top], f.at[top], send.at[2], recv.at[2], to_right()),
            remote(l.at[low], f.at[low], send.at[3], recv.at[3], to_left()),
        )

        def begin():
            for c in first():
                c.start()

        def onward():
            for a, b in zip(first(), second()):
                a.wait_recv()
                b.start()

        def finish():
            for c in first():
                c.wait_send()
            for c in second():
                c.wait()

        return {0: begin, 2: onward, 3: finish}


class Reduce:
    def __init__(self, base, left, right, far):
        self.inputs = [base, left, right, far]
        rows, width = base.shape
        self.out_shapes, self.out_specs = [struct((rows, width))], [whole((rows, width))]
        half, full = pltpu.VMEM((rows // 2, width), BF16), pltpu.VMEM((rows, width), BF16)
        self.scratch = [half, half, half, half, full, full, pltpu.VMEM((rows, width), F32)]
        self.scratch += [pltpu.SemaphoreType.DMA((6,)), pltpu.SemaphoreType.DMA((6,)), pltpu.SemaphoreType.DMA((3,))]

    def bind(self, inputs, outputs, scratch):
        base, left, right, far = inputs
        t_r, t_l, add_r, add_l, in_r, in_l, base_v, send, recv, load = scratch
        rows = base.shape[0]
        half = rows // 2
        top, low = pl.ds(0, half), pl.ds(half, half)
        first = lambda: (
            remote(far.at[top], t_r, send.at[0], recv.at[0], to_right()),
            remote(far.at[low], t_l, send.at[1], recv.at[1], to_left()),
        )
        direct = lambda: (
            remote(right.at[low], in_r.at[low], send.at[2], recv.at[2], to_right()),
            remote(left.at[top], in_l.at[top], send.at[3], recv.at[3], to_left()),
        )
        second = lambda: (
            remote(add_r, in_r.at[top], send.at[4], recv.at[4], to_right()),
            remote(add_l, in_l.at[low], send.at[5], recv.at[5], to_left()),
        )
        local = lambda: (
            pltpu.make_async_copy(right.at[top], add_r, load.at[0]),
            pltpu.make_async_copy(left.at[low], add_l, load.at[1]),
            pltpu.make_async_copy(base, base_v, load.at[2]),
        )

        def begin():
            for c in (*first(), *direct(), *local()):
                c.start()

        def onward():
            for c in local():
                c.wait()
            for c, add, t in zip(first(), (add_r, add_l), (t_r, t_l)):
                c.wait_recv()
                add[...] = (add[...].astype(F32) + t[...].astype(F32)).astype(BF16)
            for c in second():
                c.start()

        def finish():
            for c in first():
                c.wait_send()
            for c in (*direct(), *second()):
                c.wait()
            outputs[0][...] = (base_v[...] + in_r[...].astype(F32) + in_l[...].astype(F32)).astype(BF16)

        return {0: begin, 1: onward, 3: finish}


class Exchange:
    def __init__(self, blocks):
        self.inputs = list(blocks)
        self.out_shapes, self.out_specs = [struct(b.shape, b.dtype) for b in blocks], [ANY] * len(blocks)
        self.scratch = [pltpu.SemaphoreType.DMA((len(blocks),)), pltpu.SemaphoreType.DMA((len(blocks),))]

    def bind(self, inputs, outputs, scratch):
        send, recv = scratch
        copies = lambda: [remote(a, b, send.at[n], recv.at[n], to_partner()) for n, (a, b) in enumerate(zip(inputs, outputs))]

        def begin():
            for c in copies():
                c.start()

        def finish():
            for c in copies():
                c.wait()

        return {0: begin, 3: finish}


def stage(compute, inputs, in_specs, out_shapes, out_specs, scratch, comms, grid, cost_estimate, ident):
    sizes = [(len(c.inputs), len(c.out_shapes), len(c.scratch)) for c in comms]
    counts = [len(inputs), len(out_shapes), len(scratch)]
    all_in, all_specs = list(inputs), list(in_specs)
    all_shapes, all_outs, all_scratch = list(out_shapes), list(out_specs), list(scratch)
    for c in comms:
        all_in += c.inputs
        all_specs += [ANY] * len(c.inputs)
        all_shapes += c.out_shapes
        all_outs += c.out_specs
        all_scratch += c.scratch
    total_in, total_out = len(all_in), len(all_shapes)
    partner = any(isinstance(c, Exchange) for c in comms)
    ring = any(not isinstance(c, Exchange) for c in comms)

    def kernel(*refs):
        groups = [list(refs[:total_in]), list(refs[total_in : total_in + total_out]), list(refs[total_in + total_out :])]
        mine = [g[:n] for g, n in zip(groups, counts)]
        rest = [g[n:] for g, n in zip(groups, counts)]
        acts = []
        for c, size in zip(comms, sizes):
            acts.append(c.bind(*[g[:n] for g, n in zip(rest, size)]))
            rest = [g[n:] for g, n in zip(rest, size)]

        def at(point):
            if point == 0 and comms:
                barrier = pltpu.get_barrier_semaphore()
                targets = ([to_right(), to_left()] if ring else []) + ([to_partner()] if partner else [])
                for t in targets:
                    pl.semaphore_signal(barrier, inc=1, device_id=t, device_id_type=MESH)
                pl.semaphore_wait(barrier, len(targets))
            for a in acts:
                if point in a:
                    a[point]()

        compute(*mine, at)

    extra = dict(collective_id=ident, has_side_effects=True) if comms else {}
    out = pl.pallas_call(
        kernel,
        grid=grid,
        out_shape=all_shapes,
        in_specs=all_specs,
        out_specs=all_outs,
        scratch_shapes=all_scratch,
        compiler_params=pltpu.CompilerParams(vmem_limit_bytes=VMEM, **extra),
        cost_estimate=cost_estimate,
    )(*all_in)
    made = list(out[: counts[1]])
    rest = list(out[counts[1] :])
    results = []
    for _, n, _ in sizes:
        results.append(rest[:n])
        rest = rest[n:]
    return made, results


def front_body(layer, chunk, pieces, inputs, outputs, scratch, at):
    at(0)
    refs = list(inputs)
    len_ref, gain_ref, cos_ref, sin_ref = (refs.pop(0) for _ in range(4))
    x_refs = [refs.pop(0) for _ in range(CHIPS if pieces else 1)]
    w_refs = [refs.pop(0) for _ in range(6)]
    old = [[refs.pop(0) for _ in range(chunk)] for _ in range(4)]
    new, o_ref = outputs[:4], outputs[4]
    x_buf, normed, w_buf, q_buf, x_sem, w_sem, out_sem = scratch
    rows, _ = x_buf.shape
    head = q_buf.shape[-1]
    half = head // 2
    if pieces:
        part = rows // CHIPS
        copies = [pltpu.make_async_copy(x_refs[n], x_buf.at[pl.ds(piece_rows(n, part), part)], x_sem.at[n]) for n in range(CHIPS)]
    else:
        copies = [pltpu.make_async_copy(x_refs[0].at[lax.axis_index("core"), pl.ds(chunk * rows, rows)], x_buf, x_sem.at[0])]
    for c in copies:
        c.start()
    loads = [pltpu.make_async_copy(w_refs[n].at[layer], w_buf.at[n], w_sem.at[n]) for n in range(6)]
    for c in loads:
        c.start()
    for c in copies:
        c.wait()
    save = None
    if pieces:
        save = pltpu.make_async_copy(x_buf, outputs[5], out_sem)
        save.start()
    tile = min(ROW_TILE, rows)
    for r in range(0, rows, tile):
        normed[pl.ds(r, tile)] = norm_rows(x_buf[pl.ds(r, tile)].astype(F32), gain_ref[...])

    def rope(y, r):
        low, high = y[:, :half], y[:, half:]
        c, s = cos_ref[pl.ds(r, tile)], sin_ref[pl.ds(r, tile)]
        return jnp.concatenate([low * c - high * s, high * c + low * s], axis=-1)

    for n in range(6):
        loads[n].wait()
        for r in range(0, rows, tile):
            y = jnp.dot(normed[pl.ds(r, tile)], w_buf[n], preferred_element_type=F32)
            if n < 2:
                q_buf[n, pl.ds(r, tile)] = (rope(y, r) * head**-0.5).astype(BF16)
            elif n < 4:
                new[n - 2][pl.ds(r, tile)] = rope(y, r).astype(BF16)
            else:
                new[n - 2][pl.ds(r, tile)] = y.astype(BF16)
    at(1)
    dims = (((1,), (1,)), ((), ()))
    length = len_ref[0]
    col = lax.broadcasted_iota(jnp.int32, (1, rows), 1)
    lower = lax.broadcasted_iota(jnp.int32, (tile, rows), 1) - lax.broadcasted_iota(jnp.int32, (tile, rows), 0)
    bias = [jnp.where(col < length - j * rows, 0.0, -1e30).astype(F32) for j in range(chunk + 1)]
    for h in range(2):
        keys = old[h] + [new[h]]
        values = old[2 + h] + [new[2 + h]]
        for r in range(0, rows, tile):
            query = q_buf[h, pl.ds(r, tile)]
            blocks = []
            for j in range(chunk + 1):
                scores = lax.dot_general(query, keys[j][...], dims, preferred_element_type=F32) + bias[j]
                if j == chunk:
                    scores = jnp.where(lower <= r, scores, -1e30)
                blocks.append(scores)
            top = functools.reduce(jnp.maximum, [jnp.max(b, axis=-1, keepdims=True) for b in blocks])
            blocks = [jnp.exp(b - top) for b in blocks]
            inv = 1.0 / functools.reduce(jnp.add, [jnp.sum(b, axis=-1, keepdims=True) for b in blocks])
            total = None
            for j in range(chunk + 1):
                prod = jnp.dot((blocks[j] * inv).astype(BF16), values[j][...], preferred_element_type=F32)
                total = prod if total is None else total + prod
            o_ref[pl.ds(r, tile), pl.ds(h * head, head)] = total.astype(BF16)
        if h == 0:
            at(2)
    if save is not None:
        save.wait()
    at(3)


def front_call(layer, chunk, length, gain, cos_t, sin_t, x_list, weights, old, rows, comms, ident):
    width, head = weights[0].shape[1:]
    pieces = len(x_list) > 1
    small = whole((rows, head))
    table = pl.BlockSpec((rows, head // 2), lambda *_: (chunk, 0))
    flops = 12 * rows * width * head + 8 * rows * rows * (chunk + 1) * head
    shapes, specs = [struct((rows, head))] * 4 + [struct((rows, 2 * head))], [small] * 4 + [whole((rows, 2 * head))]
    if pieces:
        shapes, specs = shapes + [struct((rows, width))], specs + [ANY]
    return stage(
        functools.partial(front_body, layer, chunk, pieces),
        [length, gain, cos_t, sin_t, *x_list, *weights, *[k for group in old for k in group]],
        [SMEM, whole((1, width)), table, table] + [ANY] * (len(x_list) + 6) + [small] * (4 * chunk),
        shapes,
        specs,
        [
            pltpu.VMEM((rows, width), BF16),
            pltpu.VMEM((rows, width), BF16),
            pltpu.VMEM((6, width, head), BF16),
            pltpu.VMEM((2, rows, head), BF16),
            pltpu.SemaphoreType.DMA((CHIPS,)),
            pltpu.SemaphoreType.DMA((6,)),
            pltpu.SemaphoreType.DMA,
        ],
        comms,
        (1,),
        cost(flops, 12 * width * head + 4 * rows * width, 2 * rows * rows * (chunk + 1)),
        ident,
    )


def back_body(chunk, from_hidden, inputs, outputs, scratch, at):
    gain_ref, x_ref = inputs[:2]
    o_refs, w_refs, ff = inputs[2:6], inputs[6:14], inputs[14:]
    x_buf, o_buf, w_buf, normed, acc, x_sem, o_sem, w_sem = scratch
    rows, _ = x_buf.shape
    inner = o_refs[0].shape[-1]
    head = w_refs[0].shape[0]
    part = rows // CHIPS
    step = pl.program_id(0)
    tile = min(ROW_TILE, rows)

    @pl.when(step == 0)
    def _():
        src = x_ref.at[lax.axis_index("core"), pl.ds(chunk * rows, rows)] if from_hidden else x_ref
        x_copy = pltpu.make_async_copy(src, x_buf, x_sem)
        o_copies = [pltpu.make_async_copy(o_refs[n], o_buf.at[:, pl.ds(n * inner, inner)], o_sem.at[n]) for n in range(CHIPS)]
        w_copies = [pltpu.make_async_copy(w_refs[n], w_buf.at[pl.ds(n * head, head)], w_sem.at[n]) for n in range(8)]
        for n in range(CHIPS):
            o_copies[n].start()
            w_copies[2 * n].start()
            w_copies[2 * n + 1].start()
        x_copy.start()
        at(0)
        for group in range(2):
            for n in range(2 * group, 2 * group + 2):
                o_copies[n].wait()
                w_copies[2 * n].wait()
                w_copies[2 * n + 1].wait()
            if group == 1:
                x_copy.wait()
            cut = pl.ds(2 * group * inner, 2 * inner)
            for r in range(0, rows, tile):
                prod = jnp.dot(o_buf[pl.ds(r, tile), cut], w_buf[cut], preferred_element_type=F32)
                if group == 0:
                    acc[pl.ds(r, tile)] = prod
                else:
                    mid = (x_buf[pl.ds(r, tile)].astype(F32) + (acc[pl.ds(r, tile)] + prod)).astype(BF16)
                    x_buf[pl.ds(r, tile)] = mid
                    normed[pl.ds(r, tile)] = norm_rows(mid.astype(F32), gain_ref[...])

    @pl.when(step == 1)
    def _():
        at(1)

    @pl.when(step == pl.num_programs(0) - 1)
    def _():
        at(2)

    a = normed[...]
    total = None
    for n in range(2):
        gate = jnp.dot(a, ff[n][...], preferred_element_type=F32)
        up = jnp.dot(a, ff[2 + n][...], preferred_element_type=F32)
        act = (jax.nn.gelu(gate, approximate=True) * up).astype(BF16)
        prod = jnp.dot(act, ff[4 + n][...], preferred_element_type=F32)
        total = prod if total is None else total + prod

    @pl.when(step == 0)
    def _():
        acc[...] = total

    @pl.when(step > 0)
    def _():
        acc[...] += total

    @pl.when(step == pl.num_programs(0) - 1)
    def _():
        own = pl.ds(piece_rows(0, part), part)
        outputs[0][...] = x_buf[own].astype(F32) + acc[own]
        for place in range(1, CHIPS):
            outputs[place][...] = acc[pl.ds(piece_rows(place, part), part)].astype(BF16)
        at(3)


def back_call(layer, chunk, gain, x, o_list, w_list, ff_w, rows, comms, ident):
    head, width = w_list[0].shape
    ff = ff_w[0].shape[-1]
    tile = min(FF_TILE, ff)
    col = pl.BlockSpec((None, width, tile), lambda i: (layer, 0, i))
    row = pl.BlockSpec((None, tile, width), lambda i: (layer, i, 0))
    part = rows // CHIPS
    return stage(
        functools.partial(back_body, chunk, x.ndim == 3),
        [gain, x, *o_list, *w_list, *ff_w],
        [whole((1, width))] + [ANY] * 13 + [col] * 4 + [row] * 2,
        [struct((part, width), F32)] + [struct((part, width))] * 3,
        [whole((part, width))] * 4,
        [
            pltpu.VMEM((rows, width), BF16),
            pltpu.VMEM((rows, 8 * head), BF16),
            pltpu.VMEM((8 * head, width), BF16),
            pltpu.VMEM((rows, width), BF16),
            pltpu.VMEM((rows, width), F32),
            pltpu.SemaphoreType.DMA,
            pltpu.SemaphoreType.DMA((CHIPS,)),
            pltpu.SemaphoreType.DMA((8,)),
        ],
        comms,
        (ff // tile,),
        cost(12 * rows * width * ff + 16 * rows * head * width, 12 * width * ff + 16 * head * width + 8 * rows * width, 2 * rows * ff),
        ident,
    )


def idle_body(inputs, outputs, scratch, at):
    for point in range(4):
        at(point)


def idle_call(comms, ident):
    return stage(idle_body, [], [], [], [], [], comms, (1,), cost(2e10, 1 << 22), ident)[1]


def place_kernel(*refs):
    h_ref, buf, in_sem, out_sem = refs[-4:]
    pieces = refs[:-4]
    part = pieces[0].shape[0]
    depth = buf.shape[0]
    core = lax.axis_index("core")
    count = len(pieces)
    loads, saves = [], []
    for n in range(count):
        chunk, rest = divmod(n, 2 * CHIPS)
        prompt = core if rest < CHIPS else 1 - core
        at = pl.multiple_of(chunk * part * CHIPS + piece_rows(rest % CHIPS, part), part)
        loads.append(pltpu.make_async_copy(pieces[n], buf.at[n % depth], in_sem.at[n % depth]))
        saves.append(pltpu.make_async_copy(buf.at[n % depth], h_ref.at[prompt, pl.ds(at, part)], out_sem.at[n % depth]))
    for n in range(depth):
        loads[n].start()
    for n in range(count):
        loads[n].wait()
        saves[n].start()
        m = n - depth // 2
        if m >= 0 and m + depth < count:
            saves[m].wait()
            loads[m + depth].start()
    for n in range(max(0, count - depth), count):
        saves[n].wait()


def place_call(pieces, shape):
    depth = min(16, len(pieces))
    return pl.pallas_call(
        place_kernel,
        out_shape=struct(shape),
        in_specs=[ANY] * len(pieces),
        out_specs=ANY,
        scratch_shapes=[pltpu.VMEM((depth, *pieces[0].shape), BF16), pltpu.SemaphoreType.DMA((depth,)), pltpu.SemaphoreType.DMA((depth,))],
        compiler_params=pltpu.CompilerParams(vmem_limit_bytes=VMEM),
        cost_estimate=cost(1e10, 1 << 25),
    )(*pieces)


def rope_tables(seq_len, head_dim):
    half_dim = head_dim // 2
    inv_freq = ROPE_BASE ** (-jnp.arange(half_dim, dtype=F32) * (2.0 / head_dim))
    angles = jnp.arange(seq_len, dtype=F32)[:, None] * inv_freq[None, :]
    return jnp.cos(angles), jnp.sin(angles)


def solution(mesh):
    groups, members = mesh.devices.shape
    chips = members // CORES
    assert chips == CHIPS
    fine = Mesh(mesh.devices.reshape(groups, chips, CORES), ("dp", "x", "core"))
    tp = ("x", "core")

    def swap(value):
        return lax.ppermute(value, "core", [(0, 1), (1, 0)])

    def right(value):
        return lax.ppermute(value, "x", [(i, (i + 1) % chips) for i in range(chips)])

    def left(value):
        return lax.ppermute(value, "x", [((i + 1) % chips, i) for i in range(chips)])

    def layers_body(hidden, lengths, w_query, w_key, w_value, w_out, w_gate, w_up, w_down, norm_attn, norm_mlp):
        core = lax.axis_index("core")
        layers = w_query.shape[0]
        _, seq, width = hidden.shape
        head = w_query.shape[-1]
        rows = seq // CHUNKS
        length = lax.dynamic_slice_in_dim(lengths, core, 1)
        cos_t, sin_t = rope_tables(seq, head)
        qkv_w = []
        for w in (w_query, w_key, w_value):
            own = w.reshape(layers, width, head)
            qkv_w += [own, swap(own)]
        ff_w = []
        for w in (w_gate, w_up, w_down):
            ff_w += [w, swap(w)]
        out_w = []
        for l in range(layers):
            own = w_out[l].reshape(head, width)
            from_left, from_right = right(own), left(own)
            far = right(from_left) if l % 2 == 0 else left(from_right)
            mine = [own, from_left, from_right, far]
            out_w.append([w for m in mine for w in (m, swap(m))])
        x = [[hidden]] * CHUNKS
        k_cache, v_cache = [], []
        waiting = []
        ident = iter(range(1000))
        other = [None] * CHUNKS

        def carry(call):
            now = [make() for make, _ in waiting]
            sinks = [sink for _, sink in waiting]
            waiting.clear()
            made, results = call(now, next(ident))
            for sink, result in zip(sinks, results):
                sink(result)
            return made

        def send_x(i, block, final):
            def landed(blocks):
                x[i] = [block, *blocks]
                if final:
                    waiting.append((lambda: Exchange(x[i]), functools.partial(other.__setitem__, i)))

            waiting.append((lambda: Gather(block), landed))

        def send_sum(i, parts, final):
            waiting.append((lambda: Reduce(*parts), lambda got: send_x(i, got[0], final)))

        for l in range(layers):
            final = l == layers - 1
            old = [[], [], [], []]
            o_all = [None] * CHUNKS
            for i in range(CHUNKS):
                made = carry(
                    lambda comms, n: front_call(l, i, length, norm_attn[l][None, :], cos_t, sin_t, x[i], qkv_w, old, rows, comms, n)
                )
                old = [group + [k] for group, k in zip(old, made[:4])]
                o = made[4]
                if l > 0:
                    x[i] = [made[5]]
                waiting.append((lambda o=o: Gather(o), lambda got, i=i, o=o: o_all.__setitem__(i, [o, *got])))
            for i in range(CHUNKS):
                made = carry(
                    lambda comms, n: back_call(l, i, norm_mlp[l][None, :], x[i][0], o_all[i], out_w[l], ff_w, rows, comms, n)
                )
                send_sum(i, made, final)
            for cache, own, theirs in ((k_cache, old[0], old[1]), (v_cache, old[2], old[3])):
                own = jnp.concatenate(own, axis=0)
                got = swap(jnp.concatenate(theirs, axis=0))
                cache.append(jnp.where(core == 0, jnp.stack([own, got]), jnp.stack([got, own]))[:, None])
        while waiting:
            carry(lambda comms, n: ([], idle_call(comms, n)))
        h_out = place_call([p for i in range(CHUNKS) for p in (*x[i], *other[i])], hidden.shape)
        return h_out, jnp.stack(k_cache), jnp.stack(v_cache)

    head_cols = P(None, None, tp, None)
    step = jax.shard_map(
        layers_body,
        mesh=fine,
        in_specs=(P("dp"), P("dp"), head_cols, head_cols, head_cols, P(None, tp, None, None), P(None, None, tp), P(None, None, tp), P(None, tp, None), P(), P()),
        out_specs=(P("dp"), P(None, "dp", tp), P(None, "dp", tp)),
        check_vma=False,
    )
    return lambda *args: step(*args)
```

time: 941 us -> 739 us (0.79)
  waiting for transfers between devices: 321 us -> 62.6 us
  Pallas kernels: 368 us -> 620 us
  starting transfers between devices: 200 us -> 14.7 us
    pallas_call x20, Pallas kernels: 368 us -> 620 us  [the longest x19 608 us: stage(): pl.pallas_call(kernel, grid=grid, out_shape=all_shapes, in_specs=all_spec...]
    ppermute x75 -> x3, waiting for transfers between devices: 219 us -> 22.7 us  [right(): lax.ppermute(value, 'x', [(i, (i + 1) % chips) for i in range(chips)])]
    ppermute x75 -> x3, starting transfers between devices: 156 us -> 5.93 us  [left(): lax.ppermute(value, 'x', [((i + 1) % chips, i) for i in range(chips)])]
    ppermute x75 -> x3, waiting for transfers between devices: 87.2 us -> 38.1 us  [left(): lax.ppermute(value, 'x', [((i + 1) % chips, i) for i in range(chips)])]
    ppermute x75 -> x3, starting transfers between devices: 33.6 us -> 4.65 us  [right(): lax.ppermute(value, 'x', [(i, (i + 1) % chips) for i in range(chips)])]
    ppermute x50 -> x18, waiting for transfers between devices: 14.8 us -> 1.74 us  [swap(): return lax.ppermute(value, 'core', [(0, 1), (1, 0)])]
  transfers between devices with their start and end apart: 200 -> 24, of which waited for: 74 -> 4; matrix products, arithmetic and copies ran while one was open for 3% -> 3% of each run, Pallas kernels for 39% -> 84%
where the time goes in v3:
time: 739 us; the launch traced here: 736 us
  Pallas kernels  620 us (84%)
  waiting for transfers between devices  62.6 us (8%)
  other arithmetic  27.4 us (4%)
  starting transfers between devices  14.7 us (2%)
  local copies, waits for them, and re-layouts  9.24 us (1%)
    pallas_call x19, Pallas kernels, stage(): pl.pallas_call(kernel, grid=grid, out_shape=all_shapes, in_specs=all_spec...  608 us
    ppermute x3, waiting for transfers between devices, left(): lax.ppermute(value, 'x', [((i + 1) % chips, i) for i in range(chips)])  38.1 us
    ppermute x3, waiting for transfers between devices, right(): lax.ppermute(value, 'x', [(i, (i + 1) % chips) for i in range(chips)])  22.7 us
  transfers between devices with their start and end apart: 24, of which 4 were waited for; matrix products, arithmetic and copies ran while one was open for 3% of the time, Pallas kernels for 84%

profile of v3, /device:TPU:112, one launch (start us, length us, event | category | flops | bytes accessed | tf_op | source)
XLA Modules:
  0.0 735.9 jit_solution(11035931896274921050)
XLA Ops:
  0.7 2.9 slice_bitcast_fusion
  3.5 2.3 collective-permute-start.4
  5.9 1.6 collective-permute-start.6
  8.0 22.7 %collective-permute-done.4.refs_8_ = bf16[256,2048]{1,0:T(8,128)(2,1)} collective-permute-done((bf16[256,2048]{1,0:T(8,128)(2,1)S(1)}, bf16[256,2048]{1,0:T(8,128)(2,1)}, u32[]{:S(2)}, u32[]{:S(2)}) %collective-permute-start.4) | collective-permute-done | bytes 1048608 | tf_op jit(solution)/shard_map/ppermute | solution.py:515
  31.3 2.5 collective-permute-start.16
  33.8 23.3 %collective-permute-done.16.refs_10_ = bf16[256,2048]{1,0:T(8,128)(2,1)S(1)} collective-permute-done((bf16[256,2048]{1,0:T(8,128)(2,1)}, bf16[256,2048]{1,0:T(8,128)(2,1)S(1)}, u32[]{:S(2)}, u32[]{:S(2)}) %collective-permute-start.16) | collective-permute-done | bytes 1048608 | tf_op jit(solution)/shard_map/ppermute | solution.py:518
  57.1 1.3 copy-done.1
  59.5 4.9 fusion
  64.4 1.0 collective-permute-start.14
  65.4 1.3 collective-permute-start.8
  66.8 0.6 fusion.2
  67.4 12.3 %shard_map.130 = (bf16[512,256]{1,0:T(8,128)(2,1)}, bf16[512,256]{1,0:T(8,128)(2,1)}, bf16[512,256]{1,0:T(8,128)(2,1)}, bf16[512,256]{1,0:T(8,128)(2,1)}, bf16[512,512]{1,0:T(8,128)(2,1)}) custom-call(s32[1]{0:T(128)} %dynamic_slice.3.refs_0_, f32[1,2048]{1,0:T(1,128)} %get-tuple-element.301.refs_1_, f32[2048,128]{1,0:T(8,128)} %get-tuple-element.306.refs_2_, ...), custom_call_target="tpu_custom_call" | custom-call | flops 3758096384 | bytes 10485760 | tf_op jit(solution)/shard_map/pallas_call | solution.py:215
  79.6 54.9 %shard_map.131 = (bf16[512,256]{1,0:T(8,128)(2,1)}, bf16[512,256]{1,0:T(8,128)(2,1)}, bf16[512,256]{1,0:T(8,128)(2,1)}, bf16[512,256]{1,0:T(8,128)(2,1)}, bf16[5...) custom-call(s32[1]{0:T(128)} %dynamic_slice.3.refs_0_, ...), custom_call_target="tpu_custom_call" | custom-call | flops 4294967296 | bytes 10485760 | tf_op jit(solution)/shard_map/pallas_call | solution.py:215
  135.1 25.7 %shard_map.132 = (bf16[512,256]{1,0:T(8,128)(2,1)}, bf16[512,256]{1,0:T(8,128)(2,1)}, bf16[512,256]{1,0:T(8,128)(2,1)}, bf16[512,256]{1,0:T(8,128)(2,1)}, bf16[5...) custom-call(s32[1]{0:T(128)} %dynamic_slice.3.refs_0_, ...), custom_call_target="tpu_custom_call" | custom-call | flops 4831838208 | bytes 10485760 | tf_op jit(solution)/shard_map/pallas_call | solution.py:215
  160.9 24.5 %shard_map.133 = (bf16[512,256]{1,0:T(8,128)(2,1)}, bf16[512,256]{1,0:T(8,128)(2,1)}, bf16[512,256]{1,0:T(8,128)(2,1)}, bf16[512,256]{1,0:T(8,128)(2,1)}, bf16[5...) custom-call(s32[1]{0:T(128)} %dynamic_slice.3.refs_0_, ...), custom_call_target="tpu_custom_call" | custom-call | flops 5368709120 | bytes 10485760 | tf_op jit(solution)/shard_map/pallas_call | solution.py:215
  185.5 2.2 pad_maximum_fusion.4
  187.6 1.0 pad_maximum_fusion.2
  189.2 0.8 fusion.3
  190.0 1.7 collective-permute-done.22
  191.7 1.8 collective-permute-start.18
  193.5 1.3 maximum_bitcast_fusion.2
  194.8 1.2 maximum_bitcast_fusion
  196.0 3.2 maximum_select_fusion.2
  199.2 3.2 maximum_select_fusion
  202.4 14.8 %collective-permute-done.18.refs_12_ = bf16[256,2048]{1,0:T(8,128)(2,1)} collective-permute-done((bf16[256,2048]{1,0:T(8,128)(2,1)}, bf16[256,2048]{1,0:T(8,128)(2,1)}, u32[]{:S(2)}, u32[]{:S(2)}) %collective-permute-start.18) | collective-permute-done | bytes 1048608 | tf_op jit(solution)/shard_map/ppermute | solution.py:518
  218.3 35.7 %shard_map.134 = (f32[128,2048]{1,0:T(8,128)}, bf16[128,2048]{1,0:T(8,128)(2,1)}, bf16[128,2048]{1,0:T(8,128)(2,1)}, bf16[128,2048]{1,0:T(8,128)(2,1)}, bf16[512...) custom-call(f32[1,2048]{1,0:T(1,128)} %get-tuple-element.303.refs_0_, ...), custom_call_target="tpu_custom_call" | custom-call | flops 17179869184 | bytes 41943040 | tf_op jit(solution)/shard_map/pallas_call | solution.py:215
  254.0 30.7 %shard_map.135 = (f32[128,2048]{1,0:T(8,128)}, bf16[128,2048]{1,0:T(8,128)(2,1)}, bf16[128,2048]{1,0:T(8,128)(2,1)}, bf16[128,2048]{1,0:T(8,128)(2,1)}, bf16[128,2048]{1,0:T(8,128)(2,1)}) custom-call(f32[1,2048]{1,0:T(1,128)} %get-tuple-element.303.refs_0_, bf16[2,2048,2048]{2,1,0:T(8,128)(2,1)} %refs_1_.7, ...), custom_call_target="tpu_custom_call" | custom-call | flops 17179869184 | bytes 41943040 | tf_op jit(solution)/shard_map/pallas_call | solution.py:215
  284.7 43.8 %shard_map.136 = (f32[128,2048]{1,0:T(8,128)}, bf16[128,2048]{1,0:T(8,128)(2,1)}, bf16[128,2048]{1,0:T(8,128)(2,1)}, bf16[128,2048]{1,0:T(8,128)(2,1)}, bf16[128...) custom-call(f32[1,2048]{1,0:T(1,128)} %get-tuple-element.303.refs_0_, ...), custom_call_target="tpu_custom_call" | custom-call | flops 17179869184 | bytes 41943040 | tf_op jit(solution)/shard_map/pallas_call | solution.py:215
  328.5 43.3 %shard_map.137 = (f32[128,2048]{1,0:T(8,128)}, bf16[128,2048]{1,0:T(8,128)(2,1)}, bf16[128,2048]{1,0:T(8,128)(2,1)}, bf16[128,2048]{1,0:T(8,128)(2,1)}, bf16[128...) custom-call(f32[1,2048]{1,0:T(1,128)} %get-tuple-element.303.refs_0_, ...), custom_call_target="tpu_custom_call" | custom-call | flops 17179869184 | bytes 41943040 | tf_op jit(solution)/shard_map/pallas_call | solution.py:215
  371.8 39.2 %shard_map.138 = (bf16[512,256]{1,0:T(8,128)(2,1)}, bf16[512,256]{1,0:T(8,128)(2,1)}, bf16[512,256]{1,0:T(8,128)(2,1)}, bf16[512,256]{1,0:T(8,128)(2,1)}, bf16[5...) custom-call(s32[1]{0:T(128)} %dynamic_slice.3.refs_0_, ...), custom_call_target="tpu_custom_call" | custom-call | flops 3758096384 | bytes 10485760 | tf_op jit(solution)/shard_map/pallas_call | solution.py:215
  411.0 38.4 %shard_map.139 = (bf16[512,256]{1,0:T(8,128)(2,1)}, bf16[512,256]{1,0:T(8,128)(2,1)}, bf16[512,256]{1,0:T(8,128)(2,1)}, bf16[512,256]{1,0:T(8,128)(2,1)}, bf16[5...) custom-call(s32[1]{0:T(128)} %dynamic_slice.3.refs_0_, ...), custom_call_target="tpu_custom_call" | custom-call | flops 4294967296 | bytes 10485760 | tf_op jit(solution)/shard_map/pallas_call | solution.py:215
  449.4 21.5 %shard_map.140 = (bf16[512,256]{1,0:T(8,128)(2,1)}, bf16[512,256]{1,0:T(8,128)(2,1)}, bf16[512,256]{1,0:T(8,128)(2,1)}, bf16[512,256]{1,0:T(8,128)(2,1)}, bf16[5...) custom-call(s32[1]{0:T(128)} %dynamic_slice.3.refs_0_, ...), custom_call_target="tpu_custom_call" | custom-call | flops 4831838208 | bytes 10485760 | tf_op jit(solution)/shard_map/pallas_call | solution.py:215
  471.0 23.3 %shard_map.141 = (bf16[512,256]{1,0:T(8,128)(2,1)}, bf16[512,256]{1,0:T(8,128)(2,1)}, bf16[512,256]{1,0:T(8,128)(2,1)}, bf16[512,256]{1,0:T(8,128)(2,1)}, bf16[5...) custom-call(s32[1]{0:T(128)} %dynamic_slice.3.refs_0_, ...), custom_call_target="tpu_custom_call" | custom-call | flops 5368709120 | bytes 10485760 | tf_op jit(solution)/shard_map/pallas_call | solution.py:215
  494.3 2.1 pad_maximum_fusion.5
  496.4 1.0 pad_maximum_fusion.3
  498.4 34.6 %shard_map.142 = (f32[128,2048]{1,0:T(8,128)}, bf16[128,2048]{1,0:T(8,128)(2,1)}, bf16[128,2048]{1,0:T(8,128)(2,1)}, bf16[128,2048]{1,0:T(8,128)(2,1)}, bf16[512...) custom-call(f32[1,2048]{1,0:T(1,128)} %get-tuple-element.304.refs_0_, ...), custom_call_target="tpu_custom_call" | custom-call | flops 17179869184 | bytes 41943040 | tf_op jit(solution)/shard_map/pallas_call | solution.py:215
  533.0 30.5 %shard_map.143 = (f32[128,2048]{1,0:T(8,128)}, bf16[128,2048]{1,0:T(8,128)(2,1)}, bf16[128,2048]{1,0:T(8,128)(2,1)}, bf16[128,2048]{1,0:T(8,128)(2,1)}, bf16[128,2048]{1,0:T(8,128)(2,1)}) custom-call(f32[1,2048]{1,0:T(1,128)} %get-tuple-element.304.refs_0_, bf16[512,2048]{1,0:T(8,128)(2,1)} %get-tuple-element.210.refs_1_, ...), custom_call_target="tpu_custom_call" | custom-call | flops 17179869184 | bytes 41943040 | tf_op jit(solution)/shard_map/pallas_call | solution.py:215
  563.6 43.6 %shard_map.144 = (f32[128,2048]{1,0:T(8,128)}, bf16[128,2048]{1,0:T(8,128)(2,1)}, bf16[128,2048]{1,0:T(8,128)(2,1)}, bf16[128,2048]{1,0:T(8,128)(2,1)}, bf16[128...) custom-call(f32[1,2048]{1,0:T(1,128)} %get-tuple-element.304.refs_0_, ...), custom_call_target="tpu_custom_call" | custom-call | flops 17179869184 | bytes 41943040 | tf_op jit(solution)/shard_map/pallas_call | solution.py:215
  607.2 42.8 %shard_map.145 = (f32[128,2048]{1,0:T(8,128)}, bf16[128,2048]{1,0:T(8,128)(2,1)}, bf16[128,2048]{1,0:T(8,128)(2,1)}, bf16[128,2048]{1,0:T(8,128)(2,1)}, bf16[128...) custom-call(f32[1,2048]{1,0:T(1,128)} %get-tuple-element.304.refs_0_, ...), custom_call_target="tpu_custom_call" | custom-call | flops 17179869184 | bytes 41943040 | tf_op jit(solution)/shard_map/pallas_call | solution.py:215
  650.0 38.5 %shard_map.146 = (bf16[128,2048]{1,0:T(8,128)(2,1)}, bf16[128,2048]{1,0:T(8,128)(2,1)}, bf16[128,2048]{1,0:T(8,128)(2,1)}, bf16[128,2048]{1,0:T(8,128)(2,1)}, bf...) custom-call(bf16[128,2048]{1,0:T(8,128)(2,1)} %get-tuple-element.255, ...), custom_call_target="tpu_custom_call" | custom-call | flops 20000000000 | bytes 4194304 | tf_op jit(solution)/shard_map/pallas_call | solution.py:215
  688.6 20.5 %shard_map.147 = (bf16[128,2048]{1,0:T(8,128)(2,1)}, bf16[128,2048]{1,0:T(8,128)(2,1)}, bf16[128,2048]{1,0:T(8,128)(2,1)}, bf16[128,2048]{1,0:T(8,128)(2,1)}, bf...) custom-call(bf16[128,2048]{1,0:T(8,128)(2,1)} %get-tuple-element.267.refs_4_.refs_0_.refs_16_, ...), custom_call_target="tpu_custom_call" | custom-call | flops 20000000000 | bytes 4194304 | tf_op jit(solution)/shard_map/pallas_call | solution.py:215
  709.0 4.6 shard_map.148
  713.7 12.1 %shard_map.149 = bf16[2,2048,2048]{2,1,0:T(8,128)(2,1)} custom-call(bf16[128,2048]{1,0:T(8,128)(2,1)} %get-tuple-element.239.refs_20_.refs_0_, bf16[128,2048]{1,0:T(8,128)(2,1)} %get-tuple-element.248.refs_21_.refs_1_, bf16[128,2048]{1,0:T(8,128)(2,1)} %get-tuple-element.249.refs_22_.refs_2_, bf16[128,2048]{1,0:T(8,128)(2,1)} %get-tuple-element.250.refs_23_.refs_3_, ...), custom_call_target="tpu_custom_call" | custom-call | flops 10000000000 | bytes 33554432 | tf_op jit(solution)/shard_map/pallas_call | solution.py:486
  725.9 0.8 copy-done.18
  727.4 1.2 copy-done.14
  728.7 2.4 pad_maximum_fusion.1
  731.0 2.1 maximum_select_fusion.1
  733.3 2.4 pad_maximum_fusion
  (120 shorter events, 6.3 us)
Async XLA Ops:
  0.6 6.9 copy-start
  0.6 58.3 %copy-start.39 = (s32[2]{0:T(128)S(1)}, s32[2]{0:T(128)}, u32[]{:S(2)}) copy-start(s32[2]{0:T(128)} %param.12) | copy-start | bytes 28
  3.5 76.1 %copy-start.3 = (bf16[256,2048]{1,0:T(8,128)(2,1)}, bf16[256,2048]{1,0:T(8,128)(2,1)S(1)}, u32[]{:S(2)}) copy-start(bf16[256,2048]{1,0:T(8,128)(2,1)S(1)} %get-tuple-element.300.refs_6_) | copy-start | bytes 3145732
  3.5 63.2 %copy-start.37 = (f32[2,2048]{1,0:T(2,128)S(1)}, f32[2,2048]{1,0:T(2,128)}, u32[]{:S(2)}) copy-start(f32[2,2048]{1,0:T(2,128)} %param.20) | copy-start | bytes 49156
  3.5 27.2 %collective-permute-start.4 = (bf16[256,2048]{1,0:T(8,128)(2,1)S(1)}, bf16[256,2048]{1,0:T(8,128)(2,1)}, u32[]{:S(2)}, u32[]{:S(2)}) collective-permute-start(bf16[256,2048]{1,0:T(8,128)(2,1)S(1)} %get-tuple-element.300.refs_6_), channel_id=1, source_target_pairs={{0,2},{2,4},{4,6},{6,0},{1,3},{3,5},{5,7},{7,1},{8,10},{10,12},{12... | collective-permute-start | bytes 3145736 | tf_op jit(solution)/shard_map/ppermute | solution.py:515
  5.9 24.9 %collective-permute-start.6 = (bf16[256,2048]{1,0:T(8,128)(2,1)S(1)}, bf16[256,2048]{1,0:T(8,128)(2,1)S(1)}, u32[]{:S(2)}, u32[]{:S(2)}) collective-permute-start(bf16[256,2048]{1,0:T(8,128)(2,1)S(1)} %get-tuple-element.300.refs_6_), channel_id=1, source_target_pairs={{2,0},{4,2},{6,4},{0,6},{3,1},{5,3},{7,5},{1,7},{10,8},{12,10},{14... | collective-permute-start | bytes 3145736 | tf_op jit(solution)/shard_map/ppermute | solution.py:518
  7.5 23.8 %collective-permute-start.3 = (bf16[256,2048]{1,0:T(8,128)(2,1)S(1)}, bf16[256,2048]{1,0:T(8,128)(2,1)S(1)}, u32[]{:S(2)}, u32[]{:S(2)}) collective-permute-start(bf16[256,2048]{1,0:T(8,128)(2,1)S(1)} %get-tuple-element.300.refs_6_), channel_id=1, source_target_pairs={{0,1},{1,0},{2,3},{3,2},{4,5},{5,4},{6,7},{7,6},{8,9},{9,8},{10,11... | collective-permute-start | bytes 3145736 | tf_op jit(solution)/shard_map/ppermute | solution.py:512
  7.5 49.6 %collective-permute-start = (bf16[2,2048,256]{2,1,0:T(8,128)(2,1)S(1)}, bf16[2,2048,256]{2,1,0:T(8,128)(2,1)S(1)}, u32[]{:S(2)}, u32[]{:S(2)}) collective-permute-start(bf16[2,2048,256]{2,1,0:T(8,128)(2,1)S(1)} %bitcast.27), channel_id=1, source_target_pairs={{0,1},{1,0},{2,3},{3,2},{4,5},{5,4},{6,7},{7,6},{8,9},{9,8},{10,11... | collective-permute-start | bytes 6291464 | tf_op jit(solution)/shard_map/ppermute | solution.py:512
  8.0 209.8 %collective-permute-start.10 = (bf16[2,2048,1024]{2,1,0:T(8,128)(2,1)}, bf16[2,2048,1024]{2,1,0:T(8,128)(2,1)}, u32[]{:S(2)}, u32[]{:S(2)}) collective-permute-start(bf16[2,2048,1024]{2,1,0:T(8,128)(2,1)} %refs_14_.15), channel_id=1, source_target_pairs={{0,1},{1,0},{2,3},{3,2},{4,5},{5,4},{6,7},{7,6},{8,9},{9,8},{10,11... | collective-permute-start | bytes 25165832 | tf_op jit(solution)/shard_map/ppermute | solution.py:512
  30.7 187.2 %collective-permute-start.11 = (bf16[2,2048,1024]{2,1,0:T(8,128)(2,1)}, bf16[2,2048,1024]{2,1,0:T(8,128)(2,1)}, u32[]{:S(2)}, u32[]{:S(2)}) collective-permute-start(bf16[2,2048,1024]{2,1,0:T(8,128)(2,1)} %refs_16_.15), channel_id=1, source_target_pairs={{0,1},{1,0},{2,3},{3,2},{4,5},{5,4},{6,7},{7,6},{8,9},{9,8},{10,11... | collective-permute-start | bytes 25165832 | tf_op jit(solution)/shard_map/ppermute | solution.py:512
  30.8 27.7 %copy-start.4 = (bf16[256,2048]{1,0:T(8,128)(2,1)}, bf16[256,2048]{1,0:T(8,128)(2,1)S(1)}, u32[]{:S(2)}) copy-start(bf16[256,2048]{1,0:T(8,128)(2,1)S(1)} %collective-permute-done.6.refs_10_) | copy-start | bytes 3145732
  30.8 187.6 %collective-permute-start.12 = (bf16[2,1024,2048]{2,1,0:T(8,128)(2,1)}, bf16[2,1024,2048]{2,1,0:T(8,128)(2,1)}, u32[]{:S(2)}, u32[]{:S(2)}) collective-permute-start(bf16[2,1024,2048]{2,1,0:T(8,128)(2,1)} %refs_18_.15), channel_id=1, source_target_pairs={{0,1},{1,0},{2,3},{3,2},{4,5},{5,4},{6,7},{7,6},{8,9},{9,8},{10,11... | collective-permute-start | bytes 25165832 | tf_op jit(solution)/shard_map/ppermute | solution.py:512
  31.3 27.7 %copy-start.6 = (bf16[256,2048]{1,0:T(8,128)(2,1)}, bf16[256,2048]{1,0:T(8,128)(2,1)S(1)}, u32[]{:S(2)}) copy-start(bf16[256,2048]{1,0:T(8,128)(2,1)S(1)} %collective-permute-done.3.refs_7_) | copy-start | bytes 3145732
  31.3 25.8 %collective-permute-start.16 = (bf16[256,2048]{1,0:T(8,128)(2,1)}, bf16[256,2048]{1,0:T(8,128)(2,1)S(1)}, u32[]{:S(2)}, u32[]{:S(2)}) collective-permute-start(bf16[256,2048]{1,0:T(8,128)(2,1)} %get-tuple-element.299.refs_6_), channel_id=1, source_target_pairs={{2,0},{4,2},{6,4},{0,6},{3,1},{5,3},{7,5},{1,7},{10,8},{12,10},{14... | collective-permute-start | bytes 3145736 | tf_op jit(solution)/shard_map/ppermute | solution.py:518
  57.1 7.3 collective-permute-start.1
  58.5 7.0 collective-permute-start.2
  64.4 70.1 %collective-permute-start.14 = (bf16[256,2048]{1,0:T(8,128)(2,1)}, bf16[256,2048]{1,0:T(8,128)(2,1)}, u32[]{:S(2)}, u32[]{:S(2)}) collective-permute-start(bf16[256,2048]{1,0:T(8,128)(2,1)} %get-tuple-element.299.refs_6_), channel_id=1, source_target_pairs={{0,2},{2,4},{4,6},{6,0},{1,3},{3,5},{5,7},{7,1},{8,10},{10,12},{12... | collective-permute-start | bytes 3145736 | tf_op jit(solution)/shard_map/ppermute | solution.py:515
  65.4 69.2 %collective-permute-start.8 = (bf16[256,2048]{1,0:T(8,128)(2,1)}, bf16[256,2048]{1,0:T(8,128)(2,1)}, u32[]{:S(2)}, u32[]{:S(2)}) collective-permute-start(bf16[256,2048]{1,0:T(8,128)(2,1)} %collective-permute-done.4.refs_8_), channel_id=1, source_target_pairs={{0,2},{2,4},{4,6},{6,0},{1,3},{3,5},{5,7},{7,1},{8,10},{10,12},{12... | collective-permute-start | bytes 3145736 | tf_op jit(solution)/shard_map/ppermute | solution.py:515
  79.6 55.0 %copy-start.5 = (bf16[256,2048]{1,0:T(8,128)(2,1)S(1)}, bf16[256,2048]{1,0:T(8,128)(2,1)}, u32[]{:S(2)}) copy-start(bf16[256,2048]{1,0:T(8,128)(2,1)} %copy-done.4) | copy-start | bytes 3145732
  134.6 54.1 %collective-permute-start.5 = (bf16[256,2048]{1,0:T(8,128)(2,1)}, bf16[256,2048]{1,0:T(8,128)(2,1)S(1)}, u32[]{:S(2)}, u32[]{:S(2)}) collective-permute-start(bf16[256,2048]{1,0:T(8,128)(2,1)} %collective-permute-done.4.refs_8_), channel_id=1, source_target_pairs={{0,1},{1,0},{2,3},{3,2},{4,5},{5,4},{6,7},{7,6},{8,9},{9,8},{10,11... | collective-permute-start | bytes 3145736 | tf_op jit(solution)/shard_map/ppermute | solution.py:512
  134.7 54.0 %collective-permute-start.7 = (bf16[256,2048]{1,0:T(8,128)(2,1)S(1)}, bf16[256,2048]{1,0:T(8,128)(2,1)S(1)}, u32[]{:S(2)}, u32[]{:S(2)}) collective-permute-start(bf16[256,2048]{1,0:T(8,128)(2,1)S(1)} %copy-done.5), channel_id=1, source_target_pairs={{0,1},{1,0},{2,3},{3,2},{4,5},{5,4},{6,7},{7,6},{8,9},{9,8},{10,11... | collective-permute-start | bytes 3145736 | tf_op jit(solution)/shard_map/ppermute | solution.py:512
  160.8 24.6 %copy-start.17 = (bf16[512,256]{1,0:T(8,128)(2,1)S(1)}, bf16[512,256]{1,0:T(8,128)(2,1)}, u32[]{:S(2)}) copy-start(bf16[512,256]{1,0:T(8,128)(2,1)} %get-tuple-element.154.refs_14_.refs_17_.refs_20_) | copy-start | bytes 786436
  160.9 24.6 %copy-start.23 = (bf16[512,256]{1,0:T(8,128)(2,1)S(1)}, bf16[512,256]{1,0:T(8,128)(2,1)}, u32[]{:S(2)}) copy-start(bf16[512,256]{1,0:T(8,128)(2,1)} %get-tuple-element.159.refs_18_.refs_21_) | copy-start | bytes 786436
  185.4 2.2 copy-start.16
  185.4 2.2 copy-start.22
  185.4 3.8 copy-start.38
  187.6 7.1 copy-start.15
  188.7 7.3 copy-start.7
  188.7 3.0 collective-permute-start.22
  188.7 7.3 copy-start.8
  188.7 4.8 collective-permute-start.20
  191.7 25.5 %collective-permute-start.18 = (bf16[256,2048]{1,0:T(8,128)(2,1)}, bf16[256,2048]{1,0:T(8,128)(2,1)}, u32[]{:S(2)}, u32[]{:S(2)}) collective-permute-start(bf16[256,2048]{1,0:T(8,128)(2,1)} %copy-done.10), channel_id=1, source_target_pairs={{2,0},{4,2},{6,4},{0,6},{3,1},{5,3},{7,5},{1,7},{10,8},{12,10},{14... | collective-permute-start | bytes 3145736 | tf_op jit(solution)/shard_map/ppermute | solution.py:518
  193.5 23.7 %collective-permute-start.9 = (bf16[256,2048]{1,0:T(8,128)(2,1)}, bf16[256,2048]{1,0:T(8,128)(2,1)S(1)}, u32[]{:S(2)}, u32[]{:S(2)}) collective-permute-start(bf16[256,2048]{1,0:T(8,128)(2,1)} %collective-permute-done.8.refs_12_), channel_id=1, source_target_pairs={{0,1},{1,0},{2,3},{3,2},{4,5},{5,4},{6,7},{7,6},{8,9},{9,8},{10,11... | collective-permute-start | bytes 3145736 | tf_op jit(solution)/shard_map/ppermute | solution.py:512
  199.2 18.0 %copy-start.11 = (bf16[256,2048]{1,0:T(8,128)(2,1)S(1)}, bf16[256,2048]{1,0:T(8,128)(2,1)}, u32[]{:S(2)}) copy-start(bf16[256,2048]{1,0:T(8,128)(2,1)} %copy-done.10) | copy-start | bytes 3145732
  217.2 280.2 %collective-permute-start.13 = (bf16[256,2048]{1,0:T(8,128)(2,1)}, bf16[256,2048]{1,0:T(8,128)(2,1)S(1)}, u32[]{:S(2)}, u32[]{:S(2)}) collective-permute-start(bf16[256,2048]{1,0:T(8,128)(2,1)} %get-tuple-element.299.refs_6_), channel_id=1, source_target_pairs={{0,1},{1,0},{2,3},{3,2},{4,5},{5,4},{6,7},{7,6},{8,9},{9,8},{10,11... | collective-permute-start | bytes 3145736 | tf_op jit(solution)/shard_map/ppermute | solution.py:512
  217.2 280.7 %collective-permute-start.17 = (bf16[256,2048]{1,0:T(8,128)(2,1)S(1)}, bf16[256,2048]{1,0:T(8,128)(2,1)}, u32[]{:S(2)}, u32[]{:S(2)}) collective-permute-start(bf16[256,2048]{1,0:T(8,128)(2,1)S(1)} %copy-done.11), channel_id=1, source_target_pairs={{0,1},{1,0},{2,3},{3,2},{4,5},{5,4},{6,7},{7,6},{8,9},{9,8},{10,11... | collective-permute-start | bytes 3145736 | tf_op jit(solution)/shard_map/ppermute | solution.py:512
  217.8 280.1 %collective-permute-start.15 = (bf16[256,2048]{1,0:T(8,128)(2,1)}, bf16[256,2048]{1,0:T(8,128)(2,1)}, u32[]{:S(2)}, u32[]{:S(2)}) collective-permute-start(bf16[256,2048]{1,0:T(8,128)(2,1)} %collective-permute-done.14.refs_8_), channel_id=1, source_target_pairs={{0,1},{1,0},{2,3},{3,2},{4,5},{5,4},{6,7},{7,6},{8,9},{9,8},{10,11... | collective-permute-start | bytes 3145736 | tf_op jit(solution)/shard_map/ppermute | solution.py:512
  217.9 280.0 %collective-permute-start.19 = (bf16[256,2048]{1,0:T(8,128)(2,1)}, bf16[256,2048]{1,0:T(8,128)(2,1)}, u32[]{:S(2)}, u32[]{:S(2)}) collective-permute-start(bf16[256,2048]{1,0:T(8,128)(2,1)} %collective-permute-done.18.refs_12_), channel_id=1, source_target_pairs={{0,1},{1,0},{2,3},{3,2},{4,5},{5,4},{6,7},{7,6},{8,9},{9,8},{10,11... | collective-permute-start | bytes 3145736 | tf_op jit(solution)/shard_map/ppermute | solution.py:512
  470.9 23.4 %copy-start.21 = (bf16[512,256]{1,0:T(8,128)(2,1)S(1)}, bf16[512,256]{1,0:T(8,128)(2,1)}, u32[]{:S(2)}) copy-start(bf16[512,256]{1,0:T(8,128)(2,1)} %get-tuple-element.207.refs_17_.refs_20_.refs_23_) | copy-start | bytes 786436
  470.9 23.4 %copy-start.27 = (bf16[512,256]{1,0:T(8,128)(2,1)S(1)}, bf16[512,256]{1,0:T(8,128)(2,1)}, u32[]{:S(2)}) copy-start(bf16[512,256]{1,0:T(8,128)(2,1)} %get-tuple-element.218.refs_21_.refs_24_) | copy-start | bytes 786436
  470.9 23.4 %copy-start.31 = (bf16[512,256]{1,0:T(8,128)(2,1)S(1)}, bf16[512,256]{1,0:T(8,128)(2,1)}, u32[]{:S(2)}) copy-start(bf16[512,256]{1,0:T(8,128)(2,1)} %get-tuple-element.232.refs_25_) | copy-start | bytes 786436
  496.4 230.7 %collective-permute-start.23 = (bf16[2048,256]{1,0:T(8,128)(2,1)}, bf16[2048,256]{1,0:T(8,128)(2,1)S(1)}, u32[]{:S(2)}, u32[]{:S(2)}) collective-permute-start(bf16[2048,256]{1,0:T(8,128)(2,1)} %pad_maximum_fusion.5), channel_id=1, source_target_pairs={{0,1},{1,0},{2,3},{3,2},{4,5},{5,4},{6,7},{7,6},{8,9},{9,8},{10,11... | collective-permute-start | bytes 3145736 | tf_op jit(solution)/shard_map/ppermute | solution.py:512
  497.4 233.6 %collective-permute-start.21 = (bf16[2048,256]{1,0:T(8,128)(2,1)}, bf16[2048,256]{1,0:T(8,128)(2,1)}, u32[]{:S(2)}, u32[]{:S(2)}) collective-permute-start(bf16[2048,256]{1,0:T(8,128)(2,1)} %pad_maximum_fusion.3), channel_id=1, source_target_pairs={{0,1},{1,0},{2,3},{3,2},{4,5},{5,4},{6,7},{7,6},{8,9},{9,8},{10,11... | collective-permute-start | bytes 3145736 | tf_op jit(solution)/shard_map/ppermute | solution.py:512
  713.7 12.2 %copy-start.19 = (bf16[512,256]{1,0:T(8,128)(2,1)S(1)}, bf16[512,256]{1,0:T(8,128)(2,1)}, u32[]{:S(2)}) copy-start(bf16[512,256]{1,0:T(8,128)(2,1)} %get-tuple-element.206.refs_16_.refs_18_.refs_20_) | copy-start | bytes 786436
  713.7 12.2 %copy-start.25 = (bf16[512,256]{1,0:T(8,128)(2,1)S(1)}, bf16[512,256]{1,0:T(8,128)(2,1)}, u32[]{:S(2)}) copy-start(bf16[512,256]{1,0:T(8,128)(2,1)} %get-tuple-element.217.refs_19_.refs_21_) | copy-start | bytes 786436
  713.7 12.2 %copy-start.29 = (bf16[512,256]{1,0:T(8,128)(2,1)S(1)}, bf16[512,256]{1,0:T(8,128)(2,1)}, u32[]{:S(2)}) copy-start(bf16[512,256]{1,0:T(8,128)(2,1)} %get-tuple-element.231.refs_22_) | copy-start | bytes 786436
  713.7 12.2 %copy-start.34 = (bf16[512,256]{1,0:T(8,128)(2,1)S(1)}, bf16[512,256]{1,0:T(8,128)(2,1)}, u32[]{:S(2)}) copy-start(bf16[512,256]{1,0:T(8,128)(2,1)} %get-tuple-element.297) | copy-start | bytes 786436
  731.0 2.2 copy-start.13
  (16 other events, 25.9 us)
